TPU v7x, 8 devices: a whole 2x2x1 slice. The times are simulated.
8 devices in a mesh: dp: 1 (over z), cp: 2 (over y), tp: 4 (over x, core).
Axes of the slice: x: 2, y: 2, z: 1, core: 2. Of those that a mesh axis runs over, the one named last changes fastest.
Arguments:
- x: bfloat16 [3072, 3584], P(('dp', 'cp', 'tp'))
- idx: int32 [3072, 2], P(('dp', 'cp', 'tp'))
- gates: float32 [3072, 2], P(('dp', 'cp', 'tp'))
- wq: bfloat16 [3584, 3584], P(None, 'tp')
- wk: bfloat16 [3584, 512], P(None, 'tp')
- wv: bfloat16 [3584, 512], P(None, 'tp')
- wo: bfloat16 [3584, 3584], P('tp')
- w1g: bfloat16 [8, 3584, 2560], P(('cp', 'tp'))
- w1u: bfloat16 [8, 3584, 2560], P(('cp', 'tp'))
- w2: bfloat16 [8, 2560, 3584], P(('cp', 'tp'))
Outputs:
- output: bfloat16 [3072, 3584], P(('dp', 'cp', 'tp'))
All inputs are finite; a program needn't handle non-finite values.
Results may differ from a plain program's by a relative error of at most 0.00918231.
Values are sent between devices in bfloat16 or wider.
A program may use at most 1 GiB of HBM per device.

v0:
```python
import jax
import jax.numpy as jnp
from jax import lax
from jax.sharding import PartitionSpec as P

HEAD_DIM = 128
NEG = -1e30


def expert_ffn(rows, wg, wu, wd):
    gg = jnp.dot(rows, wg, preferred_element_type=jnp.float32)
    uu = jnp.dot(rows, wu, preferred_element_type=jnp.float32)
    act = (jax.nn.silu(gg) * uu).astype(jnp.bfloat16)
    return jnp.dot(act, wd, preferred_element_type=jnp.float32).astype(jnp.bfloat16)


def attention_residual(x, wq, wk, wv, wo, cp):
    rank = lax.axis_index('cp')
    xs = lax.all_gather(x, 'tp', axis=0, tiled=True)
    n = xs.shape[0]
    seg = n // 2
    q = jnp.dot(xs, wq, preferred_element_type=jnp.float32).astype(jnp.bfloat16)
    k = jnp.dot(xs, wk, preferred_element_type=jnp.float32).astype(jnp.bfloat16)
    v = jnp.dot(xs, wv, preferred_element_type=jnp.float32).astype(jnp.bfloat16)
    hq = q.shape[1] // HEAD_DIM
    hkvv = k.shape[1] // HEAD_DIM
    g = hq // hkvv
    kvs = lax.all_gather(jnp.concatenate([k, v], axis=1), 'cp', axis=0)
    rows = jnp.arange(n)

    def positions(src):
        s_id = jnp.where(rows < seg, src, 2 * cp - 1 - src)
        return s_id * seg + rows % seg

    qpos = positions(rank)
    q4 = q.reshape(n, hkvv, g, HEAD_DIM)
    scale = HEAD_DIM ** -0.5
    m = jnp.full((hkvv, g, n), NEG, jnp.float32)
    l = jnp.zeros((hkvv, g, n), jnp.float32)
    acc = jnp.zeros((hkvv, g, n, HEAD_DIM), jnp.float32)
    for j in range(cp):
        kj = kvs[j, :, :hkvv * HEAD_DIM].reshape(n, hkvv, HEAD_DIM)
        vj = kvs[j, :, hkvv * HEAD_DIM:].reshape(n, hkvv, HEAD_DIM)
        mask = positions(j)[None, :] <= qpos[:, None]
        s = jnp.einsum('nkgd,mkd->kgnm', q4, kj, preferred_element_type=jnp.float32) * scale
        s = jnp.where(mask, s, NEG)
        mn = jnp.maximum(m, jnp.max(s, axis=-1))
        w = jnp.where(mask, jnp.exp(s - mn[:, :, :, None]), 0.0)
        c = jnp.exp(m - mn)
        l = l * c + jnp.sum(w, axis=-1)
        acc = acc * c[:, :, :, None] + jnp.einsum('kgnm,mkd->kgnd', w.astype(jnp.bfloat16), vj, preferred_element_type=jnp.float32)
        m = mn
    o = (acc / l[:, :, :, None]).transpose(2, 0, 1, 3).reshape(n, hq * HEAD_DIM).astype(jnp.bfloat16)
    part = jnp.dot(o, wo, preferred_element_type=jnp.float32)
    att = lax.psum_scatter(part, 'tp', scatter_dimension=0, tiled=True)
    return (x.astype(jnp.float32) + att).astype(jnp.bfloat16)


def solution(mesh):
    cp = mesh.shape['cp']
    tp = mesh.shape['tp']
    ne = cp * tp
    rows_spec = P(('dp', 'cp', 'tp'), None)
    exp_spec = P(('cp', 'tp'), None, None)

    def local(x, idx, gates, wq, wk, wv, wo, w1g, w1u, w2):
        h = attention_residual(x, wq, wk, wv, wo, cp)
        t, hd = h.shape
        kk = idx.shape[1]
        cap = 4 * t // ne
        ea = idx.reshape(-1)
        tok = jnp.arange(t * kk) // kk
        onehot = (ea[:, None] == jnp.arange(ne)[None, :]).astype(jnp.int32)
        slot = jnp.take_along_axis(jnp.cumsum(onehot, axis=0), ea[:, None], axis=1)[:, 0] - 1
        send = jnp.zeros((ne, cap, hd), jnp.bfloat16).at[ea, slot].set(h[tok])
        recv = lax.all_to_all(send, ('cp', 'tp'), 0, 0, tiled=True)
        z = expert_ffn(recv.reshape(ne * cap, hd), w1g[0], w1u[0], w2[0])
        back = lax.all_to_all(z.reshape(ne, cap, hd), ('cp', 'tp'), 0, 0, tiled=True)
        zt = back[ea, slot].astype(jnp.float32).reshape(t, kk, hd)
        y = h.astype(jnp.float32) + jnp.sum(gates[:, :, None] * zt, axis=1)
        return y.astype(jnp.bfloat16)

    return jax.shard_map(local, mesh=mesh, in_specs=(rows_spec, rows_spec, rows_spec, P(None, 'tp'), P(None, 'tp'), P(None, 'tp'), P('tp', None), exp_spec, exp_spec, exp_spec), out_specs=rows_spec, check_vma=False)
```

profile of v0, /device:TPU:0, one launch (start us, length us, event | category | flops | bytes accessed | tf_op | source)
XLA Modules:
  0.0 1075.3 jit_solution(3610956173331828886)
XLA Ops:
  6.5 0.0 copy-start
  6.5 0.0 all-gather.4.cloned.1.call-start
  6.5 0.7 all-gather.4.cloned.1.call-update
  7.3 0.0 copy-start.6
  7.3 0.0 all-gather.6.cloned.1.call-start
  7.4 4.2 broadcast_compare_fusion
  11.6 71.0 %all-gather.4.cloned.1.call-done = bf16[1536,3584]{1,0:T(8,128)(2,1)} async-done(((bf16[384,3584]{1,0:T(8,128)(2,1)}), bf16[1536,3584]{1,0:T(8,128)(2,1)}) %all-gather.4.cloned.1.call-update) | async-done | bytes 11010064 | tf_op jit(solution)/shard_map/all_gather | solution.py:19
  82.6 0.0 copy-done
  82.6 8.0 convolution_convert_fusion.1
  90.6 0.0 copy-done.6
  90.6 0.0 copy-done.2
  90.6 3.7 convolution_convert_fusion.2
  94.4 1.0 pad_maximum_fusion
  95.3 0.0 all-gather.6.cloned.1.call-update
  95.4 0.3 reduce-scatter.2.cloned.1.call-start
  95.7 16.0 %convolution_convert_fusion = bf16[1536,896]{0,1:T(8,128)(2,1)} fusion(bf16[1536,3584]{1,0:T(8,128)(2,1)} %all-gather.4.cloned.1.call-done, bf16[3584,896]{1,0:T(8,128)(2,1)} %param.13), kind=kOutput, calls=%fused_computation.32 | convolution fusion | flops 9866379264 | bytes 20185088 | tf_op jit(solution)/shard_map/dot_general | solution.py:22
  111.7 7.9 all-gather.6.cloned.1.call-done
  119.6 4.0 reshape.413
  123.7 3.2 fusion.51
  126.9 0.7 copy.40
  127.6 0.7 copy.42
  128.2 0.0 copy-start.4
  128.3 27.6 %fusion.52 = (f32[7,1536]{1,0:T(8,128)S(1)}, f32[1,7,1536,1536]{2,3,1,0:T(8,128)}) fusion(bf16[1536,7,128]{0,2,1:T(8,128)(2,1)} %bitcast.85, bf16[1,1536,128]{2,1,0:T(8,128)(2,1)S(1)} %copy.40, pred[1536,1536]{0,1:T(8,128)(4,1)} %get-tuple-element.17), kind=kOutput, calls=%fused_computation.90 | convolution fusion | flops 4277392896 | bytes 71608320 | tf_op jit(solution)/shard_map/nkgd,mkd->kgnm/dot_general | solution.py:45
  155.8 0.0 copy-done.4
  155.8 26.4 %fusion.53 = (f32[7,1536]{1,0:T(8,128)S(1)}, f32[1,7,1536,1536]{2,3,1,0:T(8,128)}) fusion(bf16[1536,7,128]{0,2,1:T(8,128)(2,1)} %bitcast.86, bf16[1,1536,128]{2,1,0:T(8,128)(2,1)S(1)} %copy.42, pred[1536,1536]{0,1:T(8,128)(4,1)S(1)} %copy-done.4), kind=kOutput, calls=%fused_computation.91 | convolution fusion | flops 4277392896 | bytes 71608320 | tf_op jit(solution)/shard_map/nkgd,mkd->kgnm/dot_general | solution.py:45
  182.2 0.0 copy-done.8
  182.2 0.0 copy-start.5
  182.2 30.8 %fusion.6 = f32[7,1536,128]{1,2,0:T(8,128)} fusion(f32[1,7,1536,1536]{2,3,1,0:T(8,128)} %get-tuple-element.19, f32[7,1536]{1,0:T(8,128)S(1)} %get-tuple-element.15, pred[1536,1536]{0,1:T(8,128)(4,1)} %get-tuple-element.17, bf16[1,1536,128]{1,0,2:T(2,128)(2,1)S(1)} %copy-done.8), kind=kOutput, calls=%fused_computation.14 | convolution fusion | flops 4277403648 | bytes 74360832 | tf_op jit(solution)/shard_map/kgnm,mkd->kgnd/dot_general | solution.py:51
  213.0 0.0 copy-done.5
  213.0 41.2 %fusion = (f32[7,1536]{1,0:T(8,128)S(1)}, f32[7,1536]{1,0:T(8,128)S(1)}) fusion(f32[1,7,1536,1536]{2,3,1,0:T(8,128)} %get-tuple-element.19, f32[7,1536]{1,0:T(8,128)S(1)} %get-tuple-element.15, pred[1536,1536]{0,1:T(8,128)(4,1)S(1)} %copy-done.5, f32[1,7,1536,1536]{2,3,1,0:T(8,128)} %get-tuple-element.21, f32[7,1536]{1,0:T(8,128)S(1)} %get-tuple-element.14, ...), kind=kLoop, calls=%fused_computation.8 | loop fusion | flops 99068928 | bytes 137011200 | tf_op jit(solution)/shard_map/reduce_sum | solution.py:50
  254.3 26.9 %divide_convert_fusion = bf16[7,1536,128]{1,2,0:T(8,128)(2,1)} fusion(f32[7,1536,128]{1,2,0:T(8,128)} %fusion.6, f32[1,7,1536,1536]{2,3,1,0:T(8,128)} %get-tuple-element.21, f32[7,1536]{1,0:T(8,128)S(1)} %get-tuple-element.14, pred[1536,1536]{0,1:T(8,128)(4,1)S(1)} %copy-done.4, f32[7,1536]{1,0:T(8,128)S(1)} %get-tuple-element.7, ...), kind=kOutput, calls=%fused_computation.29 | convolution fusion | flops 4284284928 | bytes 77242368 | tf_op jit(solution)/shard_map/kgnm,mkd->kgnd/dot_general | solution.py:51
  281.2 18.8 %fusion.54 = f32[1536,3584]{1,0:T(8,128)} fusion(bf16[1536,896]{0,1:T(8,128)(2,1)} %bitcast.87, bf16[896,3584]{1,0:T(8,128)(2,1)} %param.16), kind=kOutput, calls=%fused_computation.92 | convolution fusion | flops 9865003008 | bytes 31195136 | tf_op jit(solution)/shard_map/dot_general | solution.py:54
  299.9 0.0 reduce-scatter.2.cloned.1.call-update
  300.0 0.7 copy-done.9
  300.6 0.1 copy.31
  300.8 0.1 eq.21
  300.9 0.2 broadcast_in_dim_reshape.4
  301.1 0.2 reshape.380
  301.2 1.7 reduce-window.6
  302.9 0.1 slice.36
  303.0 0.1 copy.33
  303.2 0.2 reduce-window.9
  303.3 0.1 copy.34
  303.5 0.1 add_bitcast_fusion
  303.5 4.7 gather_fusion.2
  308.2 0.2 fusion.40
  308.5 0.6 fusion.49
  309.1 141.3 %reduce-scatter.2.cloned.1.call-done = f32[384,3584]{1,0:T(8,128)} async-done(((f32[1536,3584]{1,0:T(8,128)}), f32[384,3584]{1,0:T(8,128)}) %reduce-scatter.2.cloned.1.call-update) | async-done | bytes 5505040 | tf_op jit(solution)/shard_map/reduce_scatter | solution.py:55
  450.4 5.7 add_convert_fusion.1
  456.1 13.1 %gather_fusion = bf16[768,3584]{1,0:T(8,128)(2,1)} fusion(bf16[384,3584]{1,0:T(8,128)(2,1)} %add_convert_fusion.1, s32[1024]{0:T(1024)S(1)} %pad_clamp_fusion), kind=kCustom, calls=%fused_computation | custom fusion | bytes 11013120 | tf_op jit(solution)/shard_map/gather | solution.py:75
  469.2 5.1 broadcast_in_dim.82
  474.3 182.0 %scatter_fusion = bf16[8,192,3584]{2,1,0:T(8,128)(2,1)} fusion(bf16[8,192,3584]{2,1,0:T(8,128)(2,1)} %broadcast_in_dim.82, s32[768]{0:T(1024)S(1)} %get-tuple-element.6, bf16[768,3584]{1,0:T(8,128)(2,1)} %gather_fusion), kind=kCustom, calls=%fused_computation.3 | custom fusion | bytes 16521216 | tf_op jit(solution)/shard_map/scatter | solution.py:75
  656.3 124.9 %all_to_all.10 = bf16[8,192,3584]{2,1,0:T(8,128)(2,1)S(1)} all-to-all(bf16[8,192,3584]{2,1,0:T(8,128)(2,1)} %scatter_fusion), channel_id=1, replica_groups=mesh['dp'=1,'cp'=2,'tp'=4] {'cp','tp'}, dimensions={0} | all-to-all | bytes 22020096 | tf_op jit(solution)/shard_map/all_to_all | solution.py:76
  781.2 34.5 %fusion.16 = f32[1536,2560]{1,0:T(8,128)} fusion(bf16[1536,3584]{1,0:T(8,128)(2,1)S(1)} %bitcast.81, bf16[1,3584,2560]{2,1,0:T(8,128)(2,1)} %param.17), kind=kOutput, calls=%fused_computation.22 | convolution fusion | flops 28185722880 | bytes 45088768 | tf_op jit(solution)/shard_map/dot_general | solution.py:11
  815.7 36.1 %multiply_convert_fusion = bf16[1536,2560]{1,0:T(8,128)(2,1)S(1)} fusion(f32[1536,2560]{1,0:T(8,128)} %fusion.16, bf16[1536,3584]{1,0:T(8,128)(2,1)S(1)} %bitcast.82, bf16[1,3584,2560]{2,1,0:T(8,128)(2,1)} %param.18), kind=kOutput, calls=%fused_computation.24 | convolution fusion | flops 28209315840 | bytes 52953088 | tf_op jit(solution)/shard_map/dot_general | solution.py:12
  851.8 33.9 %fusion.18 = bf16[1536,3584]{1,0:T(8,128)(2,1)} fusion(bf16[1536,2560]{1,0:T(8,128)(2,1)S(1)} %multiply_convert_fusion, bf16[1,2560,3584]{2,1,0:T(8,128)(2,1)} %param.19), kind=kOutput, calls=%fused_computation.25 | convolution fusion | flops 28191227904 | bytes 37224448 | tf_op jit(solution)/shard_map/dot_general | solution.py:14
  885.7 4.2 all-to-all-start.1
  890.0 0.1 copy.30
  890.1 122.0 %all-to-all-done.1 = bf16[8,192,3584]{2,1,0:T(8,128)(2,1)} async-done(((bf16[8,192,3584]{2,1,0:T(8,128)(2,1)}), bf16[8,192,3584]{2,1,0:T(8,128)(2,1)}, u32[]{:S(2)}, u32[]{:S(2)}) %all-to-all-start.1) | async-done | bytes 11010080 | tf_op jit(solution)/shard_map/all_to_all | solution.py:78
  1012.1 0.0 copy-done.3
  1012.1 19.4 %gather_fusion.1 = bf16[768,3584]{1,0:T(8,128)(2,1)} fusion(bf16[8,192,3584]{2,1,0:T(8,128)(2,1)} %all-to-all-done.1, s32[768]{0:T(1024)S(1)} %copy-done.3), kind=kCustom, calls=%fused_computation.1 | custom fusion | bytes 11016192 | tf_op jit(solution)/shard_map/gather | solution.py:79
  1031.4 12.4 %reshape.384 = f32[384,2,3584]{2,1,0:T(2,128)} reshape(bf16[768,3584]{1,0:T(8,128)(2,1)} %gather_fusion.1) | data formatting | bytes 16515072 | tf_op jit(solution)/shard_map/convert_element_type | solution.py:79
  1043.9 19.1 %multiply_reduce_fusion = f32[384,3584]{1,0:T(8,128)} fusion(f32[384,2,3584]{2,1,0:T(2,128)} %reshape.384, f32[384,2]{1,0:T(8,128)S(1)} %copy.30), kind=kLoop, calls=%fused_computation.26 | loop fusion | flops 4128768 | bytes 16518144 | tf_op jit(solution)/shard_map/reduce_sum | solution.py:80
  1062.9 5.7 add_convert_fusion
  (21 shorter events, 0.2 us)
Async XLA Ops:
  6.5 76.1 %copy-start = (bf16[3584,128]{1,0:T(8,128)(2,1)S(1)}, bf16[3584,128]{1,0:T(8,128)(2,1)}, u32[]{:S(2)}) copy-start(bf16[3584,128]{1,0:T(8,128)(2,1)} %param.15) | copy-start | bytes 2752516
  6.5 76.1 %all-gather.4.cloned.1.call-start = ((), (), s32[]{:S(2)}) async-start(), calls=%async_computation.3 | async-start | bytes 13762560 | tf_op jit(solution)/shard_map/all_gather | solution.py:19
  7.3 83.4 %copy-start.6 = (bf16[3584,128]{1,0:T(8,128)(2,1)S(1)}, bf16[3584,128]{1,0:T(8,128)(2,1)}, u32[]{:S(2)}) copy-start(bf16[3584,128]{1,0:T(8,128)(2,1)} %param.14) | copy-start | bytes 2752516
  7.3 112.4 %all-gather.6.cloned.1.call-start = ((), (), s32[]{:S(2)}) async-start(), calls=%async_computation.5 | async-start | bytes 2359296 | tf_op jit(solution)/shard_map/all_gather | solution.py:28
  82.6 8.0 copy-start.2
  95.4 355.0 %reduce-scatter.2.cloned.1.call-start = ((), (), s32[]{:S(2)}) async-start(), calls=%async_computation.4 | async-start | bytes 27525120 | tf_op jit(solution)/shard_map/reduce_scatter | solution.py:55
  128.2 27.6 %copy-start.4 = (pred[1536,1536]{0,1:T(8,128)(4,1)S(1)}, pred[1536,1536]{0,1:T(8,128)(4,1)}, u32[]{:S(2)}) copy-start(pred[1536,1536]{0,1:T(8,128)(4,1)} %get-tuple-element.16) | copy-start | bytes 7077892
  155.8 26.4 %copy-start.8 = (bf16[1,1536,128]{1,0,2:T(2,128)(2,1)S(1)}, bf16[1,1536,128]{1,0,2:T(2,128)(2,1)}, u32[]{:S(2)}) copy-start(bf16[1,1536,128]{1,0,2:T(2,128)(2,1)} %get-tuple-element.10) | copy-start | bytes 1179652
  182.2 30.8 %copy-start.5 = (pred[1536,1536]{0,1:T(8,128)(4,1)S(1)}, pred[1536,1536]{0,1:T(8,128)(4,1)}, u32[]{:S(2)}) copy-start(pred[1536,1536]{0,1:T(8,128)(4,1)} %get-tuple-element.17) | copy-start | bytes 7077892
  213.0 41.2 %copy-start.7 = (bf16[1,1536,128]{1,0,2:T(2,128)(2,1)S(1)}, bf16[1,1536,128]{1,0,2:T(2,128)(2,1)}, u32[]{:S(2)}) copy-start(bf16[1,1536,128]{1,0,2:T(2,128)(2,1)} %get-tuple-element.9) | copy-start | bytes 1179652
  299.9 0.7 copy-start.9
  885.7 4.2 copy-start.10
  885.7 126.3 %copy-start.3 = (s32[768]{0:T(1024)S(1)}, s32[768]{0:T(1024)}, u32[]{:S(2)}) copy-start(s32[768]{0:T(1024)} %get-tuple-element.5) | copy-start | bytes 9220
  885.7 126.3 %all-to-all-start.1 = ((bf16[8,192,3584]{2,1,0:T(8,128)(2,1)}), bf16[8,192,3584]{2,1,0:T(8,128)(2,1)}, u32[]{:S(2)}, u32[]{:S(2)}) async-start(bf16[8,192,3584]{2,1,0:T(8,128)(2,1)} %bitcast.80), calls=%async_computation.2 | async-start | bytes 22020096 | tf_op jit(solution)/shard_map/all_to_all | solution.py:78
  1031.4 37.2 %copy-start.1 = (bf16[3584,128]{1,0:T(8,128)(2,1)S(1)}, bf16[3584,128]{1,0:T(8,128)(2,1)}, u32[]{:S(2)}) copy-start(bf16[3584,128]{1,0:T(8,128)(2,1)} %param.15) | copy-start | bytes 2752516
Sparse Core Ops, SparseCore 0:
  8.9 73.6 all-gather.3
  95.5 24.1 all-gather.5
  300.1 150.2 reduce-scatter.1
where the time goes:
time: 1080 us
  waiting for transfers between devices  343 us (32%)
  matrix products  263 us (24%)
  local copies, waits for them, and re-layouts  247 us (23%)
  blocking collectives  125 us (12%)
  other arithmetic  79.8 us (7%)
  between operations  13.5 us (1%)
    scatter x1, local copies, waits for them, and re-layouts, local(): send = jnp.zeros((ne, cap, hd), jnp.bfloat16).at[ea, slot].set(h[tok])  182 us
    reduce_scatter x1, waiting for transfers between devices, attention_residual(): att = lax.psum_scatter(part, 'tp', scatter_dimension=0, tiled=True)  141 us
    all_to_all x1, blocking collectives, local(): recv = lax.all_to_all(send, ('cp', 'tp'), 0, 0, tiled=True)  125 us
    all_to_all x1, waiting for transfers between devices, local(): lax.all_to_all(z.reshape(ne, cap, hd), ('cp', 'tp'), 0, 0, tiled=True)  122 us
    all_gather x1, waiting for transfers between devices, attention_residual(): xs = lax.all_gather(x, 'tp', axis=0, tiled=True)  71 us
    dot_general x2, matrix products, attention_residual(): jnp.einsum('kgnm,mkd->kgnd', w.astype(jnp.bfloat16), vj, preferred_elemen...  57.7 us
    dot_general x2, matrix products, attention_residual(): jnp.einsum('nkgd,mkd->kgnm', q4, kj, preferred_element_type=jnp.float32)  53.9 us
    reduce_sum x1, other arithmetic, attention_residual(): l = l * c + jnp.sum(w, axis=-1)  41.2 us
  transfers between devices with their start and end apart: 4, of which 4 were waited for; matrix products, arithmetic and copies ran while one was open for 3% of the time, Pallas kernels for 0%

commit v1 on v0

v1 whole, which is shorter than its diff:
```python
import functools
import math
import jax, jax.numpy as jnp
from jax import lax
from jax.experimental import pallas as pl
from jax.experimental.pallas import tpu as pltpu
from jax.sharding import PartitionSpec as P
D=128
def attn_kernel(seg, bq, bk, heads, cp, q_ref, kv_ref, o_ref, m_ref, l_ref, acc_ref):
    rank = lax.axis_index('cp')
    i = pl.program_id(0)
    per = seg // bq
    s_id = jnp.where(i < per, rank, 2*cp-1-rank)
    nfull = s_id*per + lax.rem(i, per)
    c = D**-0.5*math.log2(math.e)
    def scores(h, j):
        k = kv_ref[pl.ds(pl.multiple_of(j*bk, bk), bk), :D]
        q = q_ref[:, h*D:(h+1)*D]
        return lax.dot_general(q, k, (((1,),(1,)),((),())), preferred_element_type=jnp.float32)
    def pv(p, j):
        v = kv_ref[pl.ds(pl.multiple_of(j*bk, bk), bk), D:]
        return jnp.dot(p.astype(jnp.bfloat16), v, preferred_element_type=jnp.float32)
    def lanes(p):
        t = p[:, :128]
        for a in range(128, bk, 128):
            t = t + p[:, a:a+128]
        return t
    mask = lax.broadcasted_iota(jnp.int32,(bq,bk),1) <= lax.broadcasted_iota(jnp.int32,(bq,bk),0)
    for h in range(heads):
        s = jnp.where(mask, scores(h, nfull)*c, -1e30)
        m = jnp.max(s, axis=1, keepdims=True)
        p = jnp.where(mask, jnp.exp2(s-m), 0.0)
        m_ref[h] = jnp.broadcast_to(m,(bq,128))
        l_ref[h] = lanes(p)
        acc_ref[h] = pv(p, nfull)
    def body(j, _):
        for h in range(heads):
            s = scores(h, j)*c
            mo = m_ref[h]
            mn = jnp.maximum(mo, jnp.max(s, axis=1, keepdims=True))
            p = jnp.exp2(s - jnp.concatenate([mn]*(bk//128),axis=1))
            al = jnp.exp2(mo-mn)
            m_ref[h] = mn
            l_ref[h] = l_ref[h]*al + lanes(p)
            acc_ref[h] = acc_ref[h]*al + pv(p, j)
        return 0
    lax.fori_loop(0, nfull, body, 0)
    for h in range(heads):
        l = jnp.sum(l_ref[h], axis=1, keepdims=True)
        o_ref[:, h*D:(h+1)*D] = (acc_ref[h]/l).astype(jnp.bfloat16)

def attention(q, kv, cp, bq=256, bk=256):
    n, hd = q.shape
    heads = hd//D
    seg = n//2
    return pl.pallas_call(
        functools.partial(attn_kernel, seg, bq, bk, heads, cp),
        grid=(n//bq,),
        in_specs=[pl.BlockSpec((bq,hd), lambda i:(i,0)), pl.BlockSpec(kv.shape, lambda i:(0,0))],
        out_specs=pl.BlockSpec((bq,hd), lambda i:(i,0)),
        out_shape=jax.ShapeDtypeStruct((n,hd), jnp.bfloat16),
        scratch_shapes=[pltpu.VMEM((heads,bq,128),jnp.float32)]*3,
        compiler_params=pltpu.CompilerParams(vmem_limit_bytes=60*1024*1024),
        name='attn')(q, kv)


def expert_ffn(rows, wg, wu, wd):
    gg = jnp.dot(rows, wg, preferred_element_type=jnp.float32)
    uu = jnp.dot(rows, wu, preferred_element_type=jnp.float32)
    act = (jax.nn.silu(gg) * uu).astype(jnp.bfloat16)
    return jnp.dot(act, wd, preferred_element_type=jnp.float32).astype(jnp.bfloat16)


def attention_residual(x, wq, wk, wv, wo, cp):
    xs = lax.all_gather(x, 'tp', axis=0, tiled=True)
    seg = xs.shape[0] // 2
    wkv = jnp.concatenate([wk, wv], axis=1)
    kv = jnp.dot(xs, wkv, preferred_element_type=jnp.float32).astype(jnp.bfloat16)
    kvs = lax.all_gather(kv, 'cp', axis=0)
    q = jnp.dot(xs, wq, preferred_element_type=jnp.float32).astype(jnp.bfloat16)
    kvp = jnp.concatenate([kvs[r, :seg] for r in range(cp)] + [kvs[r, seg:] for r in reversed(range(cp))], axis=0)
    o = attention(q, kvp, cp)
    part = jnp.dot(o, wo, preferred_element_type=jnp.float32)
    att = lax.psum_scatter(part, 'tp', scatter_dimension=0, tiled=True)
    return (x.astype(jnp.float32) + att).astype(jnp.bfloat16)


def routing(idx, ne):
    t = idx.shape[0]
    it = idx.T
    hit = (it[0][None, :] == jnp.arange(ne)[:, None]) | (it[1][None, :] == jnp.arange(ne)[:, None])
    before = (jnp.arange(t)[:, None] < jnp.arange(t)[None, :]).astype(jnp.bfloat16)
    rank = jnp.dot(hit.astype(jnp.bfloat16), before, preferred_element_type=jnp.float32).astype(jnp.int32)
    return jnp.where(hit, rank, -1)


def solution(mesh):
    cp = mesh.shape['cp']
    tp = mesh.shape['tp']
    ne = cp * tp
    rows_spec = P(('dp', 'cp', 'tp'), None)
    exp_spec = P(('cp', 'tp'), None, None)

    def local(x, idx, gates, wq, wk, wv, wo, w1g, w1u, w2):
        t, hd = x.shape
        cap = 4 * t // ne
        slot = routing(idx, ne)
        h = attention_residual(x, wq, wk, wv, wo, cp)
        pick = (slot[:, None, :] == jnp.arange(cap)[None, :, None]).astype(jnp.bfloat16).reshape(ne * cap, t)
        send = jnp.dot(pick, h, preferred_element_type=jnp.float32).astype(jnp.bfloat16)
        recv = lax.all_to_all(send.reshape(ne, cap, hd), ('cp', 'tp'), 0, 0, tiled=True)
        z = expert_ffn(recv.reshape(ne * cap, hd), w1g[0], w1u[0], w2[0])
        back = lax.all_to_all(z.reshape(ne, cap, hd), ('cp', 'tp'), 0, 0, tiled=True).reshape(ne * cap, hd)
        flat = jnp.arange(ne * cap)
        y = h.astype(jnp.float32)
        for k in range(2):
            mine = jnp.sum(jnp.where(idx[:, k][None, :] == jnp.arange(ne)[:, None], jnp.arange(ne)[:, None] * cap + slot, 0), axis=0)
            sel = (mine[:, None] == flat[None, :]).astype(jnp.bfloat16)
            y = y + gates[:, k:k + 1] * jnp.dot(sel, back, preferred_element_type=jnp.float32)
        return y.astype(jnp.bfloat16)

    return jax.shard_map(local, mesh=mesh, in_specs=(rows_spec, rows_spec, rows_spec, P(None, 'tp'), P(None, 'tp'), P(None, 'tp'), P('tp', None), exp_spec, exp_spec, exp_spec), out_specs=rows_spec, check_vma=False)
```

time: 1080 us -> 723 us (0.67)
  local copies, waits for them, and re-layouts: 247 us -> 2.53 us
  matrix products: 263 us -> 177 us
  other arithmetic: 79.8 us -> 2.46 us
  Pallas kernels: 0 us -> 46.9 us
    scatter x1 -> x0, local copies, waits for them, and re-layouts: 182 us -> none  [local(): send = jnp.zeros((ne, cap, hd), jnp.bfloat16).at[ea, slot].set(h[tok])]
    dot_general x6 -> x5, matrix products: 123 us -> 36.8 us  [the longest x2 19 us: local(): jnp.dot(sel, back, preferred_element_type=jnp.float32)]
    reduce_sum x2 -> x0, other arithmetic: 60.3 us -> none  [the longest x1 41.2 us: attention_residual(): l = l * c + jnp.sum(w, axis=-1)]
    pallas_call x0 -> x1, Pallas kernels: none -> 46.9 us  [attention(): pl.pallas_call(functools.partial(attn_kernel, seg, bq, bk, heads, cp), gr...]
    gather x3 -> x0, local copies, waits for them, and re-layouts: 37.1 us -> none  [the longest x1 19.4 us: local(): zt = back[ea, slot].astype(jnp.float32).reshape(t, kk, hd)]
    convert_element_type x1 -> x0, local copies, waits for them, and re-layouts: 12.4 us -> none  [local(): zt = back[ea, slot].astype(jnp.float32).reshape(t, kk, hd)]
    convert_element_type x3 -> x0, other arithmetic: 11.4 us -> none  [the longest x1 5.7 us: attention_residual(): return (x.astype(jnp.float32) + att).astype(jnp.bfloat16)]
where the time goes in v1:
time: 723 us
  waiting for transfers between devices  353 us (49%)
  matrix products  177 us (24%)
  blocking collectives  123 us (17%)
  Pallas kernels  46.9 us (6%)
  between operations  13.2 us (2%)
    reduce_scatter x1, waiting for transfers between devices, attention_residual(): att = lax.psum_scatter(part, 'tp', scatter_dimension=0, tiled=True)  148 us
    all_to_all x1, blocking collectives, local(): lax.all_to_all(send.reshape(ne, cap, hd), ('cp', 'tp'), 0, 0, tiled=True)  123 us
    all_to_all x1, waiting for transfers between devices, local(): lax.all_to_all(z.reshape(ne, cap, hd), ('cp', 'tp'), 0, 0, tiled=True)  122 us
    all_gather x1, waiting for transfers between devices, attention_residual(): xs = lax.all_gather(x, 'tp', axis=0, tiled=True)  75.3 us
    pallas_call x1, Pallas kernels, attention(): pl.pallas_call(functools.partial(attn_kernel, seg, bq, bk, heads, cp), gr...  46.9 us
    dot_general x1, matrix products, expert_ffn(): uu = jnp.dot(rows, wu, preferred_element_type=jnp.float32)  36.1 us
    dot_general x1, matrix products, expert_ffn(): gg = jnp.dot(rows, wg, preferred_element_type=jnp.float32)  34.5 us
    dot_general x1, matrix products, expert_ffn(): jnp.dot(act, wd, preferred_element_type=jnp.float32).astype(jnp.bfloat16)  33.9 us
  transfers between devices with their start and end apart: 4, of which 4 were waited for; matrix products, arithmetic and copies ran while one was open for 3% of the time, Pallas kernels for 0%

profile of v1, /device:TPU:0, one launch (start us, length us, event | category | flops | bytes accessed | tf_op | source)
XLA Modules:
  0.0 722.7 jit_solution(6410601796938279792)
XLA Ops:
  6.5 0.0 all-gather.4.cloned.1.call-start
  6.5 0.7 all-gather.4.cloned.1.call-update
  7.3 0.0 all-gather.6.cloned.1.call-start
  7.3 75.3 %all-gather.4.cloned.1.call-done = bf16[1536,3584]{1,0:T(8,128)(2,1)} async-done(((bf16[384,3584]{1,0:T(8,128)(2,1)}), bf16[1536,3584]{1,0:T(8,128)(2,1)}) %all-gather.4.cloned.1.call-update) | async-done | bytes 11010064 | tf_op jit(solution)/shard_map/all_gather | solution.py:75
  82.6 8.7 %fusion.14 = bf16[1536,256]{0,1:T(8,128)(2,1)} fusion(bf16[1536,3584]{1,0:T(8,128)(2,1)} %all-gather.4.cloned.1.call-done, bf16[3584,128]{1,0:T(8,128)(2,1)} %param.15, bf16[3584,128]{1,0:T(8,128)(2,1)} %param.14), kind=kOutput, calls=%fused_computation.17 | convolution fusion | flops 2822635520 | bytes 13631488 | tf_op jit(solution)/shard_map/dot_general | solution.py:78
  91.3 0.0 all-gather.6.cloned.1.call-update
  91.3 0.2 reduce-scatter.2.cloned.1.call-start
  91.5 16.7 %convolution_convert_fusion.1.q_ref = bf16[1536,896]{1,0:T(8,128)(2,1)} fusion(bf16[1536,3584]{1,0:T(8,128)(2,1)} %all-gather.4.cloned.1.call-done, bf16[3584,896]{1,0:T(8,128)(2,1)} %param.13), kind=kOutput, calls=%fused_computation.15 | convolution fusion | flops 9866379264 | bytes 20185088 | tf_op jit(solution)/shard_map/dot_general | solution.py:80
  108.3 7.3 %all-gather.6.cloned.1.call-done = bf16[3072,256]{0,1:T(8,128)(2,1)} async-done(((bf16[1536,256]{0,1:T(8,128)(2,1)}), bf16[3072,256]{0,1:T(8,128)(2,1)}) %all-gather.6.cloned.1.call-update) | async-done | bytes 1572880 | tf_op jit(solution)/shard_map/all_gather | solution.py:79
  115.6 1.7 copy.11
  117.3 0.1 slice_bitcast_fusion.3
  117.4 1.3 pad_maximum_fusion.kv_ref
  118.7 46.9 %attn.1 = bf16[1536,896]{1,0:T(8,128)(2,1)} custom-call(bf16[1536,896]{1,0:T(8,128)(2,1)} %convolution_convert_fusion.1.q_ref, bf16[3072,256]{1,0:T(8,128)(2,1)} %pad_maximum_fusion.kv_ref), custom_call_target="tpu_custom_call" | custom-call | tf_op jit(solution)/shard_map/attn/pallas_call | solution.py:56
  165.5 18.7 %fusion.26 = f32[1536,3584]{1,0:T(8,128)} fusion(bf16[1536,896]{1,0:T(8,128)(2,1)} %attn.1, bf16[896,3584]{1,0:T(8,128)(2,1)} %param.16), kind=kOutput, calls=%fused_computation.51 | convolution fusion | flops 9865003008 | bytes 31195136 | tf_op jit(solution)/shard_map/dot_general | solution.py:83
  184.2 0.0 copy-start.1
  184.2 0.0 reduce-scatter.2.cloned.1.call-update
  184.2 0.1 eq.124
  184.3 0.6 copy-done.1
  184.9 0.8 select_reduce_fusion.1
  185.7 1.2 bitcast_compare_fusion
  186.9 147.7 %reduce-scatter.2.cloned.1.call-done = f32[384,3584]{1,0:T(8,128)} async-done(((f32[1536,3584]{1,0:T(8,128)}), f32[384,3584]{1,0:T(8,128)}) %reduce-scatter.2.cloned.1.call-update) | async-done | bytes 5505040 | tf_op jit(solution)/shard_map/reduce_scatter | solution.py:84
  334.6 8.4 %convolution_convert_fusion = bf16[1536,3584]{1,0:T(8,128)(2,1)S(1)} fusion(pred[1536,384]{1,0:T(32,128)(4,1)} %bitcast_compare_fusion, f32[384,3584]{1,0:T(8,128)} %reduce-scatter.2.cloned.1.call-done, bf16[384,3584]{1,0:T(8,128)(2,1)} %param.10), kind=kOutput, calls=%fused_computation.8 | convolution fusion | flops 4237492224 | bytes 19857408 | tf_op jit(solution)/shard_map/dot_general | solution.py:110
  343.0 123.5 %all_to_all.10 = bf16[8,192,3584]{2,1,0:T(8,128)(2,1)S(1)} all-to-all(bf16[8,192,3584]{2,1,0:T(8,128)(2,1)S(1)} %bitcast.45), channel_id=1, replica_groups=mesh['dp'=1,'cp'=2,'tp'=4] {'cp','tp'}, dimensions={0} | all-to-all | bytes 22020096 | tf_op jit(solution)/shard_map/all_to_all | solution.py:111
  466.5 34.5 %fusion.4 = f32[1536,2560]{1,0:T(8,128)} fusion(bf16[1536,3584]{1,0:T(8,128)(2,1)S(1)} %bitcast.43, bf16[1,3584,2560]{2,1,0:T(8,128)(2,1)} %param.17), kind=kOutput, calls=%fused_computation.4 | convolution fusion | flops 28185722880 | bytes 45088768 | tf_op jit(solution)/shard_map/dot_general | solution.py:68
  501.0 36.1 %multiply_convert_fusion = bf16[1536,2560]{1,0:T(8,128)(2,1)S(1)} fusion(f32[1536,2560]{1,0:T(8,128)} %fusion.4, bf16[1536,3584]{1,0:T(8,128)(2,1)S(1)} %bitcast.44, bf16[1,3584,2560]{2,1,0:T(8,128)(2,1)} %param.18), kind=kOutput, calls=%fused_computation.6 | convolution fusion | flops 28209315840 | bytes 52953088 | tf_op jit(solution)/shard_map/dot_general | solution.py:69
  537.1 33.9 %fusion.6 = bf16[1536,3584]{1,0:T(8,128)(2,1)} fusion(bf16[1536,2560]{1,0:T(8,128)(2,1)S(1)} %multiply_convert_fusion, bf16[1,2560,3584]{2,1,0:T(8,128)(2,1)} %param.19), kind=kOutput, calls=%fused_computation.7 | convolution fusion | flops 28191227904 | bytes 37224448 | tf_op jit(solution)/shard_map/dot_general | solution.py:71
  571.0 0.0 copy-start.2
  571.0 0.0 copy-start.4
  571.0 4.3 all-to-all-start.1
  575.4 0.0 copy-done.2
  575.4 121.8 %all-to-all-done.1 = bf16[8,192,3584]{2,1,0:T(8,128)(2,1)} async-done(((bf16[8,192,3584]{2,1,0:T(8,128)(2,1)}), bf16[8,192,3584]{2,1,0:T(8,128)(2,1)}, u32[]{:S(2)}, u32[]{:S(2)}) %all-to-all-start.1) | async-done | bytes 11010080 | tf_op jit(solution)/shard_map/all_to_all | solution.py:113
  697.2 0.0 copy-done.4
  697.2 0.0 copy-start
  697.2 0.0 copy-start.3
  697.2 7.5 %convolution_multiply_fusion = f32[384,3584]{1,0:T(8,128)S(1)} fusion(bf16[1536,3584]{1,0:T(8,128)(2,1)} %bitcast.14, f32[384]{0:T(512)S(1)} %get-tuple-element.10, s32[384]{0:T(512)S(1)} %copy-done.4), kind=kOutput, calls=%fused_computation.9 | convolution fusion | flops 4229824512 | bytes 16518144 | tf_op jit(solution)/shard_map/dot_general | solution.py:119
  704.7 0.0 copy-done
  704.8 0.0 copy-done.3
  704.8 11.4 %fusion.13 = bf16[384,3584]{1,0:T(8,128)(2,1)} fusion(f32[384,3584]{1,0:T(8,128)S(1)} %convolution_multiply_fusion, bf16[1536,3584]{1,0:T(8,128)(2,1)} %bitcast.14, f32[384]{0:T(512)S(1)} %get-tuple-element.9, s32[384]{0:T(512)S(1)} %copy-done.3, f32[384,3584]{1,0:T(8,128)} %reduce-scatter.2.cloned.1.call-done, bf16[384,3584]{1,0:T(8,128)(2,1)S(1)} %copy-done), kind=kOutput, calls=%fused_computation.13 | convolution fusion | flops 4239458304 | bytes 27528192 | tf_op jit(solution)/shard_map/dot_general | solution.py:119
  (5 shorter events, 0.1 us)
Async XLA Ops:
  6.5 76.1 %all-gather.4.cloned.1.call-start = ((), (), s32[]{:S(2)}) async-start(), calls=%async_computation.3 | async-start | bytes 13762560 | tf_op jit(solution)/shard_map/all_gather | solution.py:75
  7.3 108.3 %all-gather.6.cloned.1.call-start = ((), (), s32[]{:S(2)}) async-start(), calls=%async_computation.5 | async-start | bytes 2359296 | tf_op jit(solution)/shard_map/all_gather | solution.py:79
  91.3 243.3 %reduce-scatter.2.cloned.1.call-start = ((), (), s32[]{:S(2)}) async-start(), calls=%async_computation.4 | async-start | bytes 27525120 | tf_op jit(solution)/shard_map/reduce_scatter | solution.py:84
  184.2 0.7 copy-start.1
  571.0 4.3 copy-start.2
  571.0 126.2 %copy-start.4 = (s32[384]{0:T(512)S(1)}, s32[384]{0:T(512)}, u32[]{:S(2)}) copy-start(s32[384]{0:T(512)} %get-tuple-element.6) | copy-start | bytes 4612
  571.0 126.2 %all-to-all-start.1 = ((bf16[8,192,3584]{2,1,0:T(8,128)(2,1)}), bf16[8,192,3584]{2,1,0:T(8,128)(2,1)}, u32[]{:S(2)}, u32[]{:S(2)}) async-start(bf16[8,192,3584]{2,1,0:T(8,128)(2,1)} %bitcast.42), calls=%async_computation.2 | async-start | bytes 22020096 | tf_op jit(solution)/shard_map/all_to_all | solution.py:113
  697.2 7.6 %copy-start = (bf16[384,3584]{1,0:T(8,128)(2,1)S(1)}, bf16[384,3584]{1,0:T(8,128)(2,1)}, u32[]{:S(2)}) copy-start(bf16[384,3584]{1,0:T(8,128)(2,1)} %param.10) | copy-start | bytes 8257540
  697.2 7.6 %copy-start.3 = (s32[384]{0:T(512)S(1)}, s32[384]{0:T(512)}, u32[]{:S(2)}) copy-start(s32[384]{0:T(512)} %get-tuple-element.5) | copy-start | bytes 4612
Sparse Core Ops, SparseCore 0:
  8.9 73.6 all-gather.3
  91.4 24.1 all-gather.5
  184.4 150.2 reduce-scatter.1

commit v2 on v1

--- a/solution.py
+++ b/solution.py
@@ -1,10 +1,13 @@
 import functools
 import math
-import jax, jax.numpy as jnp
+
+import jax
+import jax.numpy as jnp
 from jax import lax
 from jax.experimental import pallas as pl
 from jax.experimental.pallas import tpu as pltpu
 from jax.sharding import PartitionSpec as P
+
 D=128
 def attn_kernel(seg, bq, bk, heads, cp, q_ref, kv_ref, o_ref, m_ref, l_ref, acc_ref):
     rank = lax.axis_index('cp')
@@ -64,6 +67,174 @@
         name='attn')(q, kv)
 
 
+MESH = pl.DeviceIdType.MESH
+NEAR = 6
+FT = 256
+NT = 512
+
+
+def peer(r):
+    c, t = lax.axis_index('cp'), lax.axis_index('tp')
+    core, xx = lax.rem(t, 2), t // 2
+    core = 1 - core if r & 1 else core
+    xx = 1 - xx if r & 2 else xx
+    c = 1 - c if r & 4 else c
+    return c, xx * 2 + core
+
+
+def device(r):
+    c, t = peer(r)
+    return (lax.axis_index('dp'), c, t)
+
+
+def greet(peers):
+    bar = pltpu.get_barrier_semaphore()
+    for r in peers:
+        pl.semaphore_signal(bar, inc=1, device_id=device(r), device_id_type=MESH)
+    pl.semaphore_wait(bar, len(peers))
+
+
+def moe_kernel(ne, cap, h_ref, slot_ref, flat_ref, gate_ref, w1g_ref, w1u_ref, w2_ref, y_ref,
+               send, recv, act, zsend, zrecv, pick, w1b, w2b, ds, dr, zs, zr, w1s, w2s):
+    t, hd = h_ref.shape
+    ff = w2_ref.shape[0]
+    nf, nz = ff // FT, hd // NT
+
+    def w1_copy(tile, slot, which):
+        src = (w1g_ref, w1u_ref)[which]
+        return pltpu.make_async_copy(src.at[:, pl.ds(pl.multiple_of(tile * FT, FT), FT)], w1b.at[slot, which], w1s.at[slot, which])
+
+    def w2_copy(tile, slot):
+        return pltpu.make_async_copy(w2_ref.at[:, pl.ds(pl.multiple_of(tile * NT, NT), NT)], w2b.at[slot], w2s.at[slot])
+
+    for s in range(2):
+        w1_copy(s, s, 0).start()
+        w1_copy(s, s, 1).start()
+    for s in range(2):
+        w2_copy(s, s).start()
+
+    def out_copy(r):
+        return pltpu.make_async_remote_copy(src_ref=send.at[r], dst_ref=recv.at[r], send_sem=ds.at[r], recv_sem=dr.at[r], device_id=device(r), device_id_type=MESH)
+
+    def dispatch(r, dst):
+        c, tt = peer(r)
+        row = slot_ref[pl.ds(c * (ne // 2) + tt, 1), :]
+        sel = (jnp.broadcast_to(row, (cap, t)) == lax.broadcasted_iota(jnp.int32, (cap, t), 0)).astype(jnp.bfloat16)
+
+        def tile(n, _):
+            cols = pl.ds(pl.multiple_of(n * NT, NT), NT)
+            dst[r, :, cols] = jnp.dot(sel, h_ref[:, cols], preferred_element_type=jnp.float32).astype(jnp.bfloat16)
+            return 0
+        lax.fori_loop(0, nz, tile, 0)
+
+    order = (2, 4, 3, 5, 6, 7, 1)
+    dispatch(order[0], send)
+    greet(range(1, ne))
+    for a, r in enumerate(order):
+        if a + 1 < len(order):
+            dispatch(order[a + 1], send)
+        else:
+            dispatch(0, recv)
+        out_copy(r).start()
+    for k in range(2):
+        pick[k * t:(k + 1) * t, :] = (flat_ref[:, k:k + 1] == lax.broadcasted_iota(jnp.int32, (t, ne * cap), 1)).astype(jnp.bfloat16)
+
+    def back_copy(r, tile):
+        cols = pl.ds(pl.multiple_of(tile * NT, NT), NT)
+        return pltpu.make_async_remote_copy(src_ref=zsend.at[r, :, cols], dst_ref=zrecv.at[r, :, cols], send_sem=zs.at[r], recv_sem=zr.at[r], device_id=device(r), device_id_type=MESH)
+
+    def experts(lo, hi, again):
+        rows = (hi - lo) * cap
+        off = 0 if again else nz
+
+        def up(f, _):
+            slot = lax.rem(f, 2)
+            w1_copy(f, slot, 0).wait()
+            w1_copy(f, slot, 1).wait()
+            xr = recv[lo:hi].reshape(rows, hd)
+            gg = jnp.dot(xr, w1b[slot, 0], preferred_element_type=jnp.float32)
+            uu = jnp.dot(xr, w1b[slot, 1], preferred_element_type=jnp.float32)
+            act[:rows, pl.ds(pl.multiple_of(f * FT, FT), FT)] = (gg * jax.nn.sigmoid(gg) * uu).astype(jnp.bfloat16)
+            nxt = f + 2
+
+            @pl.when(nxt < (nf + 2 if again else nf))
+            def _():
+                w1_copy(lax.rem(nxt, nf), slot, 0).start()
+                w1_copy(lax.rem(nxt, nf), slot, 1).start()
+            return 0
+        lax.fori_loop(0, nf, up, 0)
+
+        def down(n, _):
+            slot = lax.rem(n + off, 2)
+            w2_copy(n, slot).wait()
+
+            @pl.when(n > 0)
+            def _():
+                for r in range(max(lo, 1), hi):
+                    back_copy(r, n - 1).start()
+            zz = jnp.dot(act[:rows], w2b[slot], preferred_element_type=jnp.float32).astype(jnp.bfloat16)
+            cols = pl.ds(pl.multiple_of(n * NT, NT), NT)
+            for r in range(lo, hi):
+                dst = zrecv if r == 0 else zsend
+                dst[r, :, cols] = zz[(r - lo) * cap:(r - lo + 1) * cap]
+            nxt = n + 2
+
+            @pl.when(nxt < (nz + 2 if again else nz))
+            def _():
+                w2_copy(lax.rem(nxt, nz), slot).start()
+            return 0
+        lax.fori_loop(0, nz, down, 0)
+        for r in range(max(lo, 1), hi):
+            back_copy(r, nz - 1).start()
+
+    for r in range(1, NEAR):
+        out_copy(r).wait_recv()
+    experts(0, NEAR, True)
+    for r in range(NEAR, ne):
+        out_copy(r).wait_recv()
+    experts(NEAR, ne, False)
+    whole = lambda r: pltpu.make_async_remote_copy(src_ref=zsend.at[r], dst_ref=zrecv.at[r], send_sem=zs.at[r], recv_sem=zr.at[r], device_id=device(r), device_id_type=MESH)
+    for r in range(1, ne):
+        whole(r).wait_recv()
+
+    def combine(n, _):
+        cols = pl.ds(pl.multiple_of(n * NT, NT), NT)
+        zt = jnp.dot(pick[...], zrecv[:, :, cols].reshape(ne * cap, NT), preferred_element_type=jnp.float32)
+        y = h_ref[:, cols].astype(jnp.float32) + (gate_ref[:, 0:1] * zt[:t] + gate_ref[:, 1:2] * zt[t:])
+        y_ref[:, cols] = y.astype(jnp.bfloat16)
+        return 0
+    lax.fori_loop(0, nz, combine, 0)
+    for r in range(1, ne):
+        out_copy(r).wait_send()
+        whole(r).wait_send()
+
+
+def moe_fast(h, slot, idx, gates, w1g, w1u, w2, cap, cid):
+    t, hd = h.shape
+    ne = slot.shape[0]
+    me = lax.axis_index('cp') * (ne // 2) + lax.axis_index('tp')
+    e = jnp.arange(ne)
+    flat = []
+    for k in range(2):
+        hit = idx[:, k][None, :] == e[:, None]
+        flat.append(jnp.sum(jnp.where(hit, (e ^ me)[:, None] * cap + slot, 0), axis=0))
+    flat = jnp.stack(flat, axis=1)
+    vm = pl.BlockSpec(memory_space=pltpu.VMEM)
+    hb = pl.BlockSpec(memory_space=pl.ANY)
+    bf = jnp.bfloat16
+    ff = w2.shape[0]
+    return pl.pallas_call(
+        functools.partial(moe_kernel, ne, cap),
+        in_specs=[vm, vm, vm, vm, hb, hb, hb], out_specs=vm,
+        out_shape=jax.ShapeDtypeStruct((t, hd), bf),
+        scratch_shapes=[pltpu.VMEM((ne, cap, hd), bf), pltpu.VMEM((ne, cap, hd), bf), pltpu.VMEM((NEAR * cap, ff), bf),
+                        pltpu.VMEM((ne, cap, hd), bf), pltpu.VMEM((ne, cap, hd), bf), pltpu.VMEM((2 * t, ne * cap), bf),
+                        pltpu.VMEM((2, 2, hd, FT), bf), pltpu.VMEM((2, ff, NT), bf)]
+                       + [pltpu.SemaphoreType.DMA((ne,))] * 4 + [pltpu.SemaphoreType.DMA((2, 2)), pltpu.SemaphoreType.DMA((2,))],
+        compiler_params=pltpu.CompilerParams(collective_id=cid, has_side_effects=True, vmem_limit_bytes=63 * 1024 * 1024),
+        name='moe')(h, slot, flat, gates, w1g, w1u, w2)
+
+
 def expert_ffn(rows, wg, wu, wd):
     gg = jnp.dot(rows, wg, preferred_element_type=jnp.float32)
     uu = jnp.dot(rows, wu, preferred_element_type=jnp.float32)
@@ -94,6 +265,24 @@
     return jnp.where(hit, rank, -1)
 
 
+def moe_any(h, slot, idx, gates, wg, wu, wd):
+    t, hd = h.shape
+    ne = slot.shape[0]
+    cap = 4 * t // ne
+    pick = (slot[:, None, :] == jnp.arange(cap)[None, :, None]).astype(jnp.bfloat16).reshape(ne * cap, t)
+    send = jnp.dot(pick, h, preferred_element_type=jnp.float32).astype(jnp.bfloat16)
+    recv = lax.all_to_all(send.reshape(ne, cap, hd), ('cp', 'tp'), 0, 0, tiled=True)
+    z = expert_ffn(recv.reshape(ne * cap, hd), wg, wu, wd)
+    back = lax.all_to_all(z.reshape(ne, cap, hd), ('cp', 'tp'), 0, 0, tiled=True).reshape(ne * cap, hd)
+    flat = jnp.arange(ne * cap)
+    y = h.astype(jnp.float32)
+    for k in range(2):
+        mine = jnp.sum(jnp.where(idx[:, k][None, :] == jnp.arange(ne)[:, None], jnp.arange(ne)[:, None] * cap + slot, 0), axis=0)
+        sel = (mine[:, None] == flat[None, :]).astype(jnp.bfloat16)
+        y = y + gates[:, k:k + 1] * jnp.dot(sel, back, preferred_element_type=jnp.float32)
+    return y.astype(jnp.bfloat16)
+
+
 def solution(mesh):
     cp = mesh.shape['cp']
     tp = mesh.shape['tp']
@@ -103,20 +292,17 @@
 
     def local(x, idx, gates, wq, wk, wv, wo, w1g, w1u, w2):
         t, hd = x.shape
-        cap = 4 * t // ne
         slot = routing(idx, ne)
         h = attention_residual(x, wq, wk, wv, wo, cp)
-        pick = (slot[:, None, :] == jnp.arange(cap)[None, :, None]).astype(jnp.bfloat16).reshape(ne * cap, t)
-        send = jnp.dot(pick, h, preferred_element_type=jnp.float32).astype(jnp.bfloat16)
-        recv = lax.all_to_all(send.reshape(ne, cap, hd), ('cp', 'tp'), 0, 0, tiled=True)
-        z = expert_ffn(recv.reshape(ne * cap, hd), w1g[0], w1u[0], w2[0])
-        back = lax.all_to_all(z.reshape(ne, cap, hd), ('cp', 'tp'), 0, 0, tiled=True).reshape(ne * cap, hd)
-        flat = jnp.arange(ne * cap)
-        y = h.astype(jnp.float32)
-        for k in range(2):
-            mine = jnp.sum(jnp.where(idx[:, k][None, :] == jnp.arange(ne)[:, None], jnp.arange(ne)[:, None] * cap + slot, 0), axis=0)
-            sel = (mine[:, None] == flat[None, :]).astype(jnp.bfloat16)
-            y = y + gates[:, k:k + 1] * jnp.dot(sel, back, preferred_element_type=jnp.float32)
-        return y.astype(jnp.bfloat16)
+        count = jnp.max(jnp.sum((slot >= 0).astype(jnp.int32), axis=1))
+        worst = lax.pmax(count, ('cp', 'tp'))
+
+        def tight(h):
+            return moe_fast(h, slot, idx, gates, w1g[0], w1u[0], w2[0], t // 4, 3)
+
+        def roomy(h):
+            return moe_any(h, slot, idx, gates, w1g[0], w1u[0], w2[0])
+
+        return lax.cond(worst <= t // 4, tight, roomy, h)
 
     return jax.shard_map(local, mesh=mesh, in_specs=(rows_spec, rows_spec, rows_spec, P(None, 'tp'), P(None, 'tp'), P(None, 'tp'), P('tp', None), exp_spec, exp_spec, exp_spec), out_specs=rows_spec, check_vma=False)

time: 723 us -> 747 us (1.033)
  blocking collectives: 123 us -> 150 us
  waiting for transfers between devices: 353 us -> 331 us
  loops' own time: 0 us -> 11 us
    pmax x0 -> x1, blocking collectives: none -> 22.4 us  [local(): worst = lax.pmax(count, ('cp', 'tp'))]
    reduce_scatter x1, waiting for transfers between devices: 148 us -> 126 us  [attention_residual(): att = lax.psum_scatter(part, 'tp', scatter_dimension=0, tiled=True)]
    another operation x0 -> x1, loops' own time: none -> 11 us  [local(): return lax.cond(worst <= t // 4, tight, roomy, h)]
  transfers between devices with their start and end apart: 4 -> 4, of which waited for: 4 -> 4; matrix products, arithmetic and copies ran while one was open for 3% -> 2% of each run, Pallas kernels for 0% -> 0%
where the time goes in v2:
time: 747 us; the launch traced here: 748 us
  waiting for transfers between devices  331 us (44%)
  matrix products  178 us (24%)
  blocking collectives  150 us (20%)
  Pallas kernels  46.9 us (6%)
  between operations  14.1 us (2%)
  loops' own time  11 us (1%)
    all_to_all x1, blocking collectives, moe_any(): lax.all_to_all(send.reshape(ne, cap, hd), ('cp', 'tp'), 0, 0, tiled=True)  127 us
    reduce_scatter x1, waiting for transfers between devices, attention_residual(): att = lax.psum_scatter(part, 'tp', scatter_dimension=0, tiled=True)  126 us
    all_to_all x1, waiting for transfers between devices, moe_any(): lax.all_to_all(z.reshape(ne, cap, hd), ('cp', 'tp'), 0, 0, tiled=True)  122 us
    all_gather x1, waiting for transfers between devices, attention_residual(): xs = lax.all_gather(x, 'tp', axis=0, tiled=True)  75.3 us
    pallas_call x1, Pallas kernels, attention(): pl.pallas_call(functools.partial(attn_kernel, seg, bq, bk, heads, cp), gr...  46.9 us
    dot_general x1, matrix products, expert_ffn(): uu = jnp.dot(rows, wu, preferred_element_type=jnp.float32)  39.4 us
    dot_general x1, matrix products, expert_ffn(): gg = jnp.dot(rows, wg, preferred_element_type=jnp.float32)  33.1 us
    dot_general x1, matrix products, expert_ffn(): jnp.dot(act, wd, preferred_element_type=jnp.float32).astype(jnp.bfloat16)  32.3 us
  transfers between devices with their start and end apart: 4, of which 4 were waited for; matrix products, arithmetic and copies ran while one was open for 2% of the time, Pallas kernels for 0%

profile of v2, /device:TPU:0, one launch (start us, length us, event | category | flops | bytes accessed | tf_op | source)
XLA Modules:
  0.0 748.3 jit_solution(10994203996787810210)
XLA Ops:
  6.5 0.0 all-gather.4.cloned.1.call-start
  6.5 0.7 all-gather.4.cloned.1.call-update
  7.3 0.0 all-gather.6.cloned.1.call-start
  7.3 75.3 %all-gather.4.cloned.1.call-done = bf16[1536,3584]{1,0:T(8,128)(2,1)} async-done(((bf16[384,3584]{1,0:T(8,128)(2,1)}), bf16[1536,3584]{1,0:T(8,128)(2,1)}) %all-gather.4.cloned.1.call-update) | async-done | bytes 11010064 | tf_op jit(solution)/shard_map/all_gather | solution.py:246
  82.6 8.7 %fusion.16 = bf16[1536,256]{0,1:T(8,128)(2,1)} fusion(bf16[1536,3584]{1,0:T(8,128)(2,1)} %all-gather.4.cloned.1.call-done, bf16[3584,128]{1,0:T(8,128)(2,1)} %param.17, bf16[3584,128]{1,0:T(8,128)(2,1)} %param.16), kind=kOutput, calls=%fused_computation.39 | convolution fusion | flops 2822635520 | bytes 13631488 | tf_op jit(solution)/shard_map/dot_general | solution.py:249
  91.3 0.0 all-gather.6.cloned.1.call-update
  91.3 0.5 reduce-scatter.2.cloned.1.call-start
  91.8 16.7 %convolution_convert_fusion.1.q_ref = bf16[1536,896]{1,0:T(8,128)(2,1)} fusion(bf16[1536,3584]{1,0:T(8,128)(2,1)} %all-gather.4.cloned.1.call-done, bf16[3584,896]{1,0:T(8,128)(2,1)} %param.15), kind=kOutput, calls=%fused_computation.37 | convolution fusion | flops 9866379264 | bytes 20185088 | tf_op jit(solution)/shard_map/dot_general | solution.py:251
  108.5 7.1 all-gather.6.cloned.1.call-done
  115.6 1.7 copy.20
  117.3 0.1 slice_bitcast_fusion.3
  117.4 1.3 pad_maximum_fusion.kv_ref
  118.7 46.9 %attn.1 = bf16[1536,896]{1,0:T(8,128)(2,1)} custom-call(bf16[1536,896]{1,0:T(8,128)(2,1)} %convolution_convert_fusion.1.q_ref, bf16[3072,256]{1,0:T(8,128)(2,1)} %pad_maximum_fusion.kv_ref), custom_call_target="tpu_custom_call" | custom-call | tf_op jit(solution)/shard_map/attn/pallas_call | solution.py:59
  165.6 18.7 %fusion.26 = f32[1536,3584]{1,0:T(8,128)} fusion(bf16[1536,896]{1,0:T(8,128)(2,1)} %attn.1, bf16[896,3584]{1,0:T(8,128)(2,1)} %param.18), kind=kOutput, calls=%fused_computation.60 | convolution fusion | flops 9865003008 | bytes 31195136 | tf_op jit(solution)/shard_map/dot_general | solution.py:254
  184.3 0.0 reduce-scatter.2.cloned.1.call-update
  184.3 0.0 copy-start.4
  184.3 0.0 copy-start.7
  184.3 0.6 copy-done.3
  185.0 0.3 convert_reduce_fusion
  185.2 0.6 reduce_max.9
  185.9 22.4 %pmax.7 = s32[]{:T(128)} all-reduce(s32[]{:T(128)} %reduce_max.9), channel_id=1, replica_groups=mesh['dp'=1,'cp'=2,'tp'=4] {'cp','tp'}, use_global_device_ids=true, to_apply=%region_2.3 | all-reduce | flops 1 | bytes 8 | tf_op jit(solution)/shard_map/pmax | solution.py:298
  209.0 125.7 %reduce-scatter.2.cloned.1.call-done = f32[384,3584]{1,0:T(8,128)} async-done(((f32[1536,3584]{1,0:T(8,128)}), f32[384,3584]{1,0:T(8,128)}) %reduce-scatter.2.cloned.1.call-update) | async-done | bytes 5505040 | tf_op jit(solution)/shard_map/reduce_scatter | solution.py:255
  334.7 0.0 copy-done
  334.7 4.8 add_convert_fusion
  339.6 0.0 copy-done.4
  339.6 0.0 copy-done.7
  339.6 398.4 %conditional.1 = (bf16[384,3584]{1,0:T(8,128)(2,1)}) conditional(s32[]{:T(128)} %convert_element_type.46, (bf16[384,3584]{1,0:T(8,128)(2,1)}, f32[384,2]{0,1:T(2,128)S(1)}, s32[384,2]{0,1:T(2,128)S(1)}, s32[8,384]{1,0:T(8,128)S(1)}, bf16[1,3584,2560]{2,1,0:T(8,128)(2,1)}, /*index=5*/bf16[1,3584,2560]{2,1,0:T(8,128)(2,1)}, ...), branch_computations={%region_4.7_spmd, %region_7.10_spmd} | conditional | flops 97285398528 | bytes 354116160 | solution.py:306
  350.1 0.0 copy-start.1
  350.1 0.0 copy-start.5
  350.1 0.0 copy-start.8
  350.2 0.1 eq.27
  350.2 0.4 bitcast_compare_fusion
  350.6 0.0 slice-start
  350.6 0.0 slice-start.1
  350.7 0.0 slice-start.2
  350.7 10.5 %convolution_convert_fusion = bf16[1536,3584]{1,0:T(8,128)(2,1)} fusion(pred[1536,384]{1,0:T(32,128)(4,1)S(1)} %bitcast_compare_fusion, bf16[384,3584]{1,0:T(8,128)(2,1)} %get-tuple-element.36), kind=kOutput, calls=%fused_computation.8 | convolution fusion | flops 4233363456 | bytes 14352384 | tf_op jit(solution)/shard_map/cond/branch_0_fun/dot_general | solution.py:273
  361.1 0.0 copy-done.1
  361.1 0.0 copy-done.5
  361.1 0.0 copy-done.8
  361.1 0.0 slice-start.3
  361.1 0.0 slice-start.4
  361.2 127.2 %all_to_all.8 = bf16[8,192,3584]{2,1,0:T(8,128)(2,1)} all-to-all(bf16[8,192,3584]{2,1,0:T(8,128)(2,1)} %bitcast.56), channel_id=1, replica_groups=mesh['dp'=1,'cp'=2,'tp'=4] {'cp','tp'}, dimensions={0} | all-to-all | bytes 22020096 | tf_op jit(solution)/shard_map/cond/branch_0_fun/all_to_all | solution.py:274
  488.4 0.0 slice-done
  488.4 0.0 slice-done.1
  488.4 0.0 slice-done.2
  488.4 0.0 slice-done.3
  488.4 0.0 slice-done.4
  488.4 0.0 slice-start.5
  488.4 0.0 slice-start.6
  488.4 0.0 slice-start.7
  488.4 33.1 %fusion.4 = f32[1536,2560]{1,0:T(8,128)} fusion(bf16[1536,3584]{1,0:T(8,128)(2,1)} %bitcast.54, bf16[1,3584,2560]{2,1,0:T(8,128)(2,1)S(1)} %bitcast.47), kind=kOutput, calls=%fused_computation.4 | convolution fusion | flops 28185722880 | bytes 45088768 | tf_op jit(solution)/shard_map/cond/branch_0_fun/dot_general | solution.py:239
  521.5 39.4 %multiply_convert_fusion = bf16[1536,2560]{1,0:T(8,128)(2,1)} fusion(f32[1536,2560]{1,0:T(8,128)} %fusion.4, bf16[1536,3584]{1,0:T(8,128)(2,1)} %bitcast.55, bf16[1,3584,2560]{2,1,0:T(8,128)(2,1)} %get-tuple-element.41), kind=kOutput, calls=%fused_computation.6 | convolution fusion | flops 28209315840 | bytes 52953088 | tf_op jit(solution)/shard_map/cond/branch_0_fun/dot_general | solution.py:240
  560.9 0.0 slice-done.5
  560.9 0.0 slice-done.6
  560.9 0.0 slice-done.7
  561.0 32.3 %fusion.6 = bf16[1536,3584]{1,0:T(8,128)(2,1)} fusion(bf16[1536,2560]{1,0:T(8,128)(2,1)} %multiply_convert_fusion, bf16[1,2560,3584]{2,1,0:T(8,128)(2,1)S(1)} %bitcast.51), kind=kOutput, calls=%fused_computation.7 | convolution fusion | flops 28191227904 | bytes 37224448 | tf_op jit(solution)/shard_map/cond/branch_0_fun/dot_general | solution.py:242
  593.3 4.3 all-to-all-start.1
  597.6 0.0 copy-done.9
  597.7 0.0 copy-done.2
  597.7 0.1 select_reduce_fusion.1
  597.7 121.9 %all-to-all-done.1 = bf16[8,192,3584]{2,1,0:T(8,128)(2,1)} async-done(((bf16[8,192,3584]{2,1,0:T(8,128)(2,1)}), bf16[8,192,3584]{2,1,0:T(8,128)(2,1)}, u32[]{:S(2)}, u32[]{:S(2)}) %all-to-all-start.1) | async-done | bytes 11010080 | tf_op jit(solution)/shard_map/cond/branch_0_fun/all_to_all | solution.py:276
  719.7 7.4 convolution_multiply_fusion
  727.1 10.7 %fusion.13 = bf16[384,3584]{1,0:T(8,128)(2,1)} fusion(f32[384,3584]{1,0:T(8,128)S(1)} %convolution_multiply_fusion, bf16[1536,3584]{1,0:T(8,128)(2,1)} %bitcast.7, bf16[384,3584]{1,0:T(8,128)(2,1)} %get-tuple-element.36, f32[384]{0:T(512)S(1)} %get-tuple-element.76, s32[384]{0:T(512)S(1)} %get-tuple-element.72), kind=kOutput, calls=%fused_computation.13 | convolution fusion | flops 4235329536 | bytes 22023168 | tf_op jit(solution)/shard_map/cond/branch_0_fun/dot_general | solution.py:282
  738.0 3.5 copy.27
  (17 shorter events, 0.1 us)
Async XLA Ops:
  6.5 76.1 %all-gather.4.cloned.1.call-start = ((), (), s32[]{:S(2)}) async-start(), calls=%async_computation.3 | async-start | bytes 13762560 | tf_op jit(solution)/shard_map/all_gather | solution.py:246
  7.3 108.3 %all-gather.6.cloned.1.call-start = ((), (), s32[]{:S(2)}) async-start(), calls=%async_computation.5 | async-start | bytes 2359296 | tf_op jit(solution)/shard_map/all_gather | solution.py:250
  91.3 243.4 %reduce-scatter.2.cloned.1.call-start = ((), (), s32[]{:S(2)}) async-start(), calls=%async_computation.4 | async-start | bytes 27525120 | tf_op jit(solution)/shard_map/reduce_scatter | solution.py:255
  184.3 0.7 copy-start.3
  184.3 150.4 %copy-start = (bf16[384,3584]{1,0:T(8,128)(2,1)S(1)}, bf16[384,3584]{1,0:T(8,128)(2,1)}, u32[]{:S(2)}) copy-start(bf16[384,3584]{1,0:T(8,128)(2,1)} %param.12) | copy-start | bytes 8257540
  184.3 155.3 %copy-start.4 = (s32[384,2]{0,1:T(2,128)S(1)}, s32[384,2]{0,1:T(2,128)}, u32[]{:S(2)}) copy-start(s32[384,2]{0,1:T(2,128)} %param.13) | copy-start | bytes 9220
  184.3 155.2 %copy-start.7 = (f32[384,2]{0,1:T(2,128)S(1)}, f32[384,2]{0,1:T(2,128)}, u32[]{:S(2)}) copy-start(f32[384,2]{0,1:T(2,128)} %param.14) | copy-start | bytes 9220
  350.1 11.0 %copy-start.1 = (s32[8,384]{1,0:T(8,128)}, s32[8,384]{1,0:T(8,128)S(1)}, u32[]{:S(2)}) copy-start(s32[8,384]{1,0:T(8,128)S(1)} %get-tuple-element.39) | copy-start | bytes 36868 | tf_op jit(solution)/shard_map/cond
  350.1 11.0 %copy-start.5 = (s32[384,2]{0,1:T(2,128)}, s32[384,2]{0,1:T(2,128)S(1)}, u32[]{:S(2)}) copy-start(s32[384,2]{0,1:T(2,128)S(1)} %get-tuple-element.38) | copy-start | bytes 9220 | tf_op jit(solution)/shard_map/cond
  350.1 11.0 %copy-start.8 = (f32[384,2]{0,1:T(2,128)}, f32[384,2]{0,1:T(2,128)S(1)}, u32[]{:S(2)}) copy-start(f32[384,2]{0,1:T(2,128)S(1)} %get-tuple-element.37) | copy-start | bytes 9220 | tf_op jit(solution)/shard_map/cond
  350.6 137.7 %slice-start = ((s8[18350080]{0:T(1024)(128)(4,1)}), s8[4194304]{0:T(1024)(128)(4,1)S(1)}, s32[]{:S(2)}) async-start(s8[18350080]{0:T(1024)(128)(4,1)} %bitcast.46), calls=%async_computation.6 | async-start | bytes 8388608 | tf_op jit(solution)/shard_map/cond
  350.6 137.7 %slice-start.1 = ((s8[18350080]{0:T(1024)(128)(4,1)}), s8[4194304]{0:T(1024)(128)(4,1)S(1)}, s32[]{:S(2)}) async-start(s8[18350080]{0:T(1024)(128)(4,1)} %bitcast.46), calls=%async_computation.7 | async-start | bytes 8388608 | tf_op jit(solution)/shard_map/cond
  350.7 137.7 %slice-start.2 = ((s8[18350080]{0:T(1024)(128)(4,1)}), s8[4194304]{0:T(1024)(128)(4,1)S(1)}, s32[]{:S(2)}) async-start(s8[18350080]{0:T(1024)(128)(4,1)} %bitcast.46), calls=%async_computation.8 | async-start | bytes 8388608 | tf_op jit(solution)/shard_map/cond
  361.1 127.2 %slice-start.3 = ((s8[18350080]{0:T(1024)(128)(4,1)}), s8[4194304]{0:T(1024)(128)(4,1)S(1)}, s32[]{:S(2)}) async-start(s8[18350080]{0:T(1024)(128)(4,1)} %bitcast.46), calls=%async_computation.9 | async-start | bytes 8388608 | tf_op jit(solution)/shard_map/cond
  361.1 127.2 %slice-start.4 = ((s8[18350080]{0:T(1024)(128)(4,1)}), s8[1572864]{0:T(1024)(128)(4,1)S(1)}, s32[]{:S(2)}) async-start(s8[18350080]{0:T(1024)(128)(4,1)} %bitcast.46), calls=%async_computation.10 | async-start | bytes 3145728 | tf_op jit(solution)/shard_map/cond
  488.4 72.5 %slice-start.5 = ((s8[18350080]{0:T(1024)(128)(4,1)}), s8[4194304]{0:T(1024)(128)(4,1)S(1)}, s32[]{:S(2)}) async-start(s8[18350080]{0:T(1024)(128)(4,1)} %bitcast.50), calls=%async_computation.11 | async-start | bytes 8388608 | tf_op jit(solution)/shard_map/cond
  488.4 72.5 %slice-start.6 = ((s8[18350080]{0:T(1024)(128)(4,1)}), s8[4194304]{0:T(1024)(128)(4,1)S(1)}, s32[]{:S(2)}) async-start(s8[18350080]{0:T(1024)(128)(4,1)} %bitcast.50), calls=%async_computation.12 | async-start | bytes 8388608 | tf_op jit(solution)/shard_map/cond
  488.4 72.5 %slice-start.7 = ((s8[18350080]{0:T(1024)(128)(4,1)}), s8[1572864]{0:T(1024)(128)(4,1)S(1)}, s32[]{:S(2)}) async-start(s8[18350080]{0:T(1024)(128)(4,1)} %bitcast.50), calls=%async_computation.13 | async-start | bytes 3145728 | tf_op jit(solution)/shard_map/cond
  521.5 39.4 %slice-start.8 = ((s8[18350080]{0:T(1024)(128)(4,1)}), s8[4194304]{0:T(1024)(128)(4,1)S(1)}, s32[]{:S(2)}) async-start(s8[18350080]{0:T(1024)(128)(4,1)} %bitcast.50), calls=%async_computation.14 | async-start | bytes 8388608 | tf_op jit(solution)/shard_map/cond
  521.5 39.4 %slice-start.9 = ((s8[18350080]{0:T(1024)(128)(4,1)}), s8[4194304]{0:T(1024)(128)(4,1)S(1)}, s32[]{:S(2)}) async-start(s8[18350080]{0:T(1024)(128)(4,1)} %bitcast.50), calls=%async_computation.15 | async-start | bytes 8388608 | tf_op jit(solution)/shard_map/cond
  593.3 4.3 copy-start.6
  593.3 4.3 copy-start.9
  593.3 4.3 copy-start.2
  593.3 126.4 %all-to-all-start.1 = ((bf16[8,192,3584]{2,1,0:T(8,128)(2,1)}), bf16[8,192,3584]{2,1,0:T(8,128)(2,1)}, u32[]{:S(2)}, u32[]{:S(2)}) async-start(bf16[8,192,3584]{2,1,0:T(8,128)(2,1)} %bitcast.53), calls=%async_computation.1 | async-start | bytes 22020096 | tf_op jit(solution)/shard_map/cond/branch_0_fun/all_to_all | solution.py:276
Sparse Core Ops, SparseCore 0:
  8.9 73.6 all-gather.3
  91.4 24.1 all-gather.5
  184.4 150.2 reduce-scatter.1

commit v3 on v2

--- a/solution.py
+++ b/solution.py
@@ -7,64 +7,6 @@
 from jax.experimental import pallas as pl
 from jax.experimental.pallas import tpu as pltpu
 from jax.sharding import PartitionSpec as P
-
-D=128
-def attn_kernel(seg, bq, bk, heads, cp, q_ref, kv_ref, o_ref, m_ref, l_ref, acc_ref):
-    rank = lax.axis_index('cp')
-    i = pl.program_id(0)
-    per = seg // bq
-    s_id = jnp.where(i < per, rank, 2*cp-1-rank)
-    nfull = s_id*per + lax.rem(i, per)
-    c = D**-0.5*math.log2(math.e)
-    def scores(h, j):
-        k = kv_ref[pl.ds(pl.multiple_of(j*bk, bk), bk), :D]
-        q = q_ref[:, h*D:(h+1)*D]
-        return lax.dot_general(q, k, (((1,),(1,)),((),())), preferred_element_type=jnp.float32)
-    def pv(p, j):
-        v = kv_ref[pl.ds(pl.multiple_of(j*bk, bk), bk), D:]
-        return jnp.dot(p.astype(jnp.bfloat16), v, preferred_element_type=jnp.float32)
-    def lanes(p):
-        t = p[:, :128]
-        for a in range(128, bk, 128):
-            t = t + p[:, a:a+128]
-        return t
-    mask = lax.broadcasted_iota(jnp.int32,(bq,bk),1) <= lax.broadcasted_iota(jnp.int32,(bq,bk),0)
-    for h in range(heads):
-        s = jnp.where(mask, scores(h, nfull)*c, -1e30)
-        m = jnp.max(s, axis=1, keepdims=True)
-        p = jnp.where(mask, jnp.exp2(s-m), 0.0)
-        m_ref[h] = jnp.broadcast_to(m,(bq,128))
-        l_ref[h] = lanes(p)
-        acc_ref[h] = pv(p, nfull)
-    def body(j, _):
-        for h in range(heads):
-            s = scores(h, j)*c
-            mo = m_ref[h]
-            mn = jnp.maximum(mo, jnp.max(s, axis=1, keepdims=True))
-            p = jnp.exp2(s - jnp.concatenate([mn]*(bk//128),axis=1))
-            al = jnp.exp2(mo-mn)
-            m_ref[h] = mn
-            l_ref[h] = l_ref[h]*al + lanes(p)
-            acc_ref[h] = acc_ref[h]*al + pv(p, j)
-        return 0
-    lax.fori_loop(0, nfull, body, 0)
-    for h in range(heads):
-        l = jnp.sum(l_ref[h], axis=1, keepdims=True)
-        o_ref[:, h*D:(h+1)*D] = (acc_ref[h]/l).astype(jnp.bfloat16)
-
-def attention(q, kv, cp, bq=256, bk=256):
-    n, hd = q.shape
-    heads = hd//D
-    seg = n//2
-    return pl.pallas_call(
-        functools.partial(attn_kernel, seg, bq, bk, heads, cp),
-        grid=(n//bq,),
-        in_specs=[pl.BlockSpec((bq,hd), lambda i:(i,0)), pl.BlockSpec(kv.shape, lambda i:(0,0))],
-        out_specs=pl.BlockSpec((bq,hd), lambda i:(i,0)),
-        out_shape=jax.ShapeDtypeStruct((n,hd), jnp.bfloat16),
-        scratch_shapes=[pltpu.VMEM((heads,bq,128),jnp.float32)]*3,
-        compiler_params=pltpu.CompilerParams(vmem_limit_bytes=60*1024*1024),
-        name='attn')(q, kv)
 
 
 MESH = pl.DeviceIdType.MESH
@@ -235,25 +177,251 @@
         name='moe')(h, slot, flat, gates, w1g, w1u, w2)
 
 
+D = 128
+PIECES = 4
+CHUNKS = 4
+HOOKS = (6, 12)
+
+
+def mate(r):
+    t = lax.axis_index('tp')
+    core = lax.rem(lax.rem(t, 2) + lax.rem(r, 2), 2)
+    xx = lax.rem(t // 2 + r // 2, 2)
+    return xx * 2 + core
+
+
+def segment(t, cp):
+    c = lax.axis_index('cp')
+    return jnp.where(t < 2, c, 2 * cp - 1 - c)
+
+
+def remote(src, dst, send, recv, dev):
+    return pltpu.make_async_remote_copy(src_ref=src, dst_ref=dst, send_sem=send, recv_sem=recv, device_id=dev, device_id_type=MESH)
+
+
+def qkv_kernel(cp, ne, x_ref, cnt_ref, wq_ref, wk_ref, wv_ref, q_ref, kv_ref, all_ref,
+               xs, wqb, wkvb, cs, cr, xsnd, xrcv, fs, fr, bs, br, ks, kr, ws):
+    t = x_ref.shape[0]
+    step = t // PIECES
+    loads = [pltpu.make_async_copy(wk_ref, wkvb.at[:, :D], ws.at[0]), pltpu.make_async_copy(wv_ref, wkvb.at[:, D:], ws.at[1]),
+             pltpu.make_async_copy(wq_ref, wqb, ws.at[2])]
+    for ld in loads:
+        ld.start()
+    greet(range(1, ne))
+    counts = [remote(cnt_ref, all_ref.at[r], cs.at[r], cr.at[r], device(r)) for r in range(1, ne)]
+    for cc in counts:
+        cc.start()
+    rows = lambda p: pl.ds(p * step, step)
+    across = [remote(x_ref.at[rows(p)], xs.at[1, rows(p)], xsnd.at[p], xrcv.at[p], device(2)) for p in range(PIECES)]
+    for a in across:
+        a.start()
+    beside = remote(x_ref, xs.at[0], bs.at[0], br.at[0], device(1))
+    beside.start()
+    onward = [remote(xs.at[1, rows(p)], xs.at[2, rows(p)], fs.at[p], fr.at[p], device(1)) for p in range(PIECES)]
+    all_ref[0] = cnt_ref[...]
+    for ld in loads:
+        ld.wait()
+    sent = []
+
+    def project(block, r, off, n):
+        tt = mate(r)
+        base = pl.multiple_of(segment(tt, cp) * (2 * t) + lax.rem(tt, 2) * t + off, 16)
+        kv_ref[pl.ds(base, n), :] = jnp.dot(block, wkvb[...], preferred_element_type=jnp.float32).astype(jnp.bfloat16)
+        qb = pl.multiple_of(tt * t + off, 16)
+        q_ref[pl.ds(qb, n), :] = jnp.dot(block, wqb[...], preferred_element_type=jnp.float32).astype(jnp.bfloat16)
+        i = len(sent)
+        out = remote(kv_ref.at[pl.ds(base, n)], kv_ref.at[pl.ds(base, n)], ks.at[i], kr.at[i], device(4))
+        out.start()
+        sent.append(out)
+
+    project(x_ref[...], 0, 0, t)
+    beside.wait_recv()
+    project(xs[0], 1, 0, t)
+    for p in range(PIECES):
+        across[p].wait_recv()
+        onward[p].start()
+        project(xs[1, p * step:(p + 1) * step], 2, p * step, step)
+        onward[p].wait_recv()
+        project(xs[2, p * step:(p + 1) * step], 3, p * step, step)
+    for o in sent:
+        o.wait_recv()
+    for cc in counts:
+        cc.wait_recv()
+    for o in counts + across + [beside] + onward + sent:
+        o.wait_send()
+
+
+def qkv(x, cnt, wq, wk, wv, cp, ne, cid):
+    t, hd = x.shape
+    tp = ne // cp
+    vm = pl.BlockSpec(memory_space=pltpu.VMEM)
+    hb = pl.BlockSpec(memory_space=pl.ANY)
+    bf = jnp.bfloat16
+    dma = pltpu.SemaphoreType.DMA
+    nk = 2 + 2 * PIECES
+    return pl.pallas_call(
+        functools.partial(qkv_kernel, cp, ne),
+        in_specs=[vm, vm, hb, hb, hb], out_specs=[vm, vm, vm],
+        out_shape=[jax.ShapeDtypeStruct((tp * t, wq.shape[1]), bf), jax.ShapeDtypeStruct((ne * t, 2 * D), bf), jax.ShapeDtypeStruct((ne,) + cnt.shape, jnp.int32)],
+        scratch_shapes=[pltpu.VMEM((3, t, hd), bf), pltpu.VMEM(wq.shape, bf), pltpu.VMEM((hd, 2 * D), bf),
+                        dma((ne,)), dma((ne,)), dma((PIECES,)), dma((PIECES,)), dma((PIECES,)), dma((PIECES,)), dma((1,)), dma((1,)), dma((nk,)), dma((nk,)), dma((3,))],
+        compiler_params=pltpu.CompilerParams(collective_id=cid, has_side_effects=True, vmem_limit_bytes=60 * 1024 * 1024),
+        name='qkv')(x, cnt, wq, wk, wv)
+
+
+def attn_kernel(cp, q_ref, kv_ref, x_ref, wo_ref, h_ref, wof, ocat, obuf, m_ref, l_ref, acc_ref, part,
+                xs_, xr_, ys_, yr_, ds_, dr_, os_, or_, ls_):
+    t, hd = x_ref.shape
+    w = wo_ref.shape[0]
+    heads = w // D
+    half = w // 2
+    step = half // CHUNKS
+    c = lax.axis_index('cp')
+    mine = pltpu.make_async_copy(wo_ref, wof.at[:w], ls_.at[0])
+    mine.start()
+    greet((1, 2, 3, 4))
+    at = lambda base, j: pl.ds(pl.multiple_of(base + j * step, 16), step)
+    first, second = c * half, (1 - c) * half
+    xc = [remote(wo_ref.at[at(first, j)], wof.at[at(2 * w + first, j)], xs_.at[j], xr_.at[j], device(2)) for j in range(CHUNKS)]
+    yc = [remote(wof.at[at(2 * w + first, j)], wof.at[at(2 * w + first, j)], ys_.at[j], yr_.at[j], device(4)) for j in range(CHUNKS)]
+    dx = [remote(wof.at[at(2 * w + first, j)], wof.at[at(3 * w + first, j)], ds_.at[j], dr_.at[j], device(1)) for j in range(CHUNKS)]
+    dy = [remote(wof.at[at(2 * w + second, j)], wof.at[at(3 * w + second, j)], ds_.at[CHUNKS + j], dr_.at[CHUNKS + j], device(1)) for j in range(CHUNKS)]
+    whole = remote(wo_ref, wof.at[pl.ds(w, w)], ds_.at[2 * CHUNKS], dr_.at[2 * CHUNKS], device(1))
+    for cpy in xc:
+        cpy.start()
+    whole.start()
+
+    def relay_x(j):
+        xc[j].wait_recv()
+        yc[j].start()
+        dx[j].start()
+
+    def relay_y(j):
+        yc[j].wait_recv()
+        dy[j].start()
+
+    scale = D ** -0.5 * math.log2(math.e)
+    mask = lax.broadcasted_iota(jnp.int32, (t, t), 1) <= lax.broadcasted_iota(jnp.int32, (t, t), 0)
+
+    def lanes(p):
+        s = p[:, :128]
+        for a in range(128, t, 128):
+            s = s + p[:, a:a + 128]
+        return s
+
+    def which(b):
+        return jnp.where(b < 2, b + 2, 3 - b)
+
+    def give(b):
+        r = which(b)
+        return remote(obuf.at[r], ocat.at[:, pl.ds(pl.multiple_of(r * w, 128), w)], os_.at[r], or_.at[r], (lax.axis_index('dp'), c, mate(r)))
+
+    def block(b, u):
+        r = which(b)
+        tt = mate(r)
+        qb = pl.multiple_of(tt * t, t)
+        nfull = segment(tt, cp) * 2 + lax.rem(tt, 2)
+
+        def scores(h, j):
+            k = kv_ref[pl.ds(pl.multiple_of(j * t, t), t), :D]
+            q = q_ref[pl.ds(qb, t), h * D:(h + 1) * D]
+            return lax.dot_general(q, k, (((1,), (1,)), ((), ())), preferred_element_type=jnp.float32) * scale
+
+        def pv(p, j):
+            v = kv_ref[pl.ds(pl.multiple_of(j * t, t), t), D:]
+            return jnp.dot(p.astype(jnp.bfloat16), v, preferred_element_type=jnp.float32)
+
+        for h in range(heads):
+            s = jnp.where(mask, scores(h, nfull), -1e30)
+            m = jnp.max(s, axis=1, keepdims=True)
+            p = jnp.where(mask, jnp.exp2(s - m), 0.0)
+            m_ref[h] = jnp.broadcast_to(m, (t, 128))
+            l_ref[h] = lanes(p)
+            acc_ref[h] = pv(p, nfull)
+
+        @pl.when(b > 0)
+        def _():
+            give(b - 1).start()
+
+        def body(j, _):
+            for n, at_unit in enumerate(HOOKS):
+                @pl.when(u + j == at_unit)
+                def _():
+                    relay_x(n)
+            for h in range(heads):
+                s = scores(h, j)
+                mo = m_ref[h]
+                mn = jnp.maximum(mo, jnp.max(s, axis=1, keepdims=True))
+                p = jnp.exp2(s - jnp.concatenate([mn] * (t // 128), axis=1))
+                al = jnp.exp2(mo - mn)
+                m_ref[h] = mn
+                l_ref[h] = l_ref[h] * al + lanes(p)
+                acc_ref[h] = acc_ref[h] * al + pv(p, j)
+            return 0
+
+        lax.fori_loop(0, nfull, body, 0)
+        for h in range(heads):
+            l = jnp.sum(l_ref[h], axis=1, keepdims=True)
+            obuf[r, :, h * D:(h + 1) * D] = (acc_ref[h] / l).astype(jnp.bfloat16)
+        return u + nfull
+
+    units = lax.fori_loop(0, 4, block, 0)
+    ocat[:, :w] = obuf[0]
+    mine.wait()
+    whole.wait_recv()
+    give(2).wait_recv()
+
+    def near(n, _):
+        cols = pl.ds(pl.multiple_of(n * NT, NT), NT)
+        part[:, cols] = jnp.dot(ocat[:, :2 * w], wof[:2 * w, cols], preferred_element_type=jnp.float32)
+        return 0
+    lax.fori_loop(0, hd // NT, near, 0)
+    relay_x(2)
+    relay_y(0)
+    relay_x(3)
+    relay_y(1)
+    relay_y(2)
+    relay_y(3)
+    for j in range(CHUNKS):
+        dx[j].wait_recv()
+        dy[j].wait_recv()
+    give(0).wait_recv()
+    give(1).wait_recv()
+
+    def far(n, _):
+        cols = pl.ds(pl.multiple_of(n * NT, NT), NT)
+        s = part[:, cols] + jnp.dot(ocat[:, 2 * w:], wof[2 * w:, cols], preferred_element_type=jnp.float32)
+        h_ref[:, cols] = (x_ref[:, cols].astype(jnp.float32) + s).astype(jnp.bfloat16)
+        return 0
+    lax.fori_loop(0, hd // NT, far, 0)
+    for cpy in xc + yc + dx + dy + [whole, give(0), give(1), give(2)]:
+        cpy.wait_send()
+
+
+def attention(q, kv, x, wo, cp, cid):
+    t, hd = x.shape
+    w = wo.shape[0]
+    heads = w // D
+    vm = pl.BlockSpec(memory_space=pltpu.VMEM)
+    hb = pl.BlockSpec(memory_space=pl.ANY)
+    bf = jnp.bfloat16
+    dma = pltpu.SemaphoreType.DMA
+    state = pltpu.VMEM((heads, t, 128), jnp.float32)
+    return pl.pallas_call(
+        functools.partial(attn_kernel, cp),
+        in_specs=[vm, vm, vm, hb], out_specs=vm,
+        out_shape=jax.ShapeDtypeStruct((t, hd), bf),
+        scratch_shapes=[pltpu.VMEM((4 * w, hd), bf), pltpu.VMEM((t, 4 * w), bf), pltpu.VMEM((4, t, w), bf), state, state, state, pltpu.VMEM((t, hd), jnp.float32),
+                        dma((CHUNKS,)), dma((CHUNKS,)), dma((CHUNKS,)), dma((CHUNKS,)), dma((2 * CHUNKS + 1,)), dma((2 * CHUNKS + 1,)), dma((4,)), dma((4,)), dma((1,))],
+        compiler_params=pltpu.CompilerParams(collective_id=cid, has_side_effects=True, vmem_limit_bytes=63 * 1024 * 1024),
+        name='attn')(q, kv, x, wo)
+
+
 def expert_ffn(rows, wg, wu, wd):
     gg = jnp.dot(rows, wg, preferred_element_type=jnp.float32)
     uu = jnp.dot(rows, wu, preferred_element_type=jnp.float32)
     act = (jax.nn.silu(gg) * uu).astype(jnp.bfloat16)
     return jnp.dot(act, wd, preferred_element_type=jnp.float32).astype(jnp.bfloat16)
-
-
-def attention_residual(x, wq, wk, wv, wo, cp):
-    xs = lax.all_gather(x, 'tp', axis=0, tiled=True)
-    seg = xs.shape[0] // 2
-    wkv = jnp.concatenate([wk, wv], axis=1)
-    kv = jnp.dot(xs, wkv, preferred_element_type=jnp.float32).astype(jnp.bfloat16)
-    kvs = lax.all_gather(kv, 'cp', axis=0)
-    q = jnp.dot(xs, wq, preferred_element_type=jnp.float32).astype(jnp.bfloat16)
-    kvp = jnp.concatenate([kvs[r, :seg] for r in range(cp)] + [kvs[r, seg:] for r in reversed(range(cp))], axis=0)
-    o = attention(q, kvp, cp)
-    part = jnp.dot(o, wo, preferred_element_type=jnp.float32)
-    att = lax.psum_scatter(part, 'tp', scatter_dimension=0, tiled=True)
-    return (x.astype(jnp.float32) + att).astype(jnp.bfloat16)
 
 
 def routing(idx, ne):
@@ -293,9 +461,10 @@
     def local(x, idx, gates, wq, wk, wv, wo, w1g, w1u, w2):
         t, hd = x.shape
         slot = routing(idx, ne)
-        h = attention_residual(x, wq, wk, wv, wo, cp)
-        count = jnp.max(jnp.sum((slot >= 0).astype(jnp.int32), axis=1))
-        worst = lax.pmax(count, ('cp', 'tp'))
+        counts = jnp.broadcast_to(jnp.sum((slot >= 0).astype(jnp.int32), axis=1)[:, None], (ne, D))
+        q, kv, counts = qkv(x, counts, wq, wk, wv, cp, ne, 1)
+        h = attention(q, kv, x, wo, cp, 2)
+        worst = jnp.max(counts)
 
         def tight(h):
             return moe_fast(h, slot, idx, gates, w1g[0], w1u[0], w2[0], t // 4, 3)

time: 747 us -> 602 us (0.81); the launches traced: 748 us -> 593 us
  waiting for transfers between devices: 331 us -> 122 us
  Pallas kernels: 46.9 us -> 188 us
  matrix products: 178 us -> 133 us
  blocking collectives: 150 us -> 127 us
  between operations: 14.1 us -> 1.16 us
    pallas_call x1 -> x2, Pallas kernels: 46.9 us -> 188 us  [the longest x1 112 us: attention(): pl.pallas_call(functools.partial(attn_kernel, cp), in_specs=[vm, vm, vm,...]
    reduce_scatter x1 -> x0, waiting for transfers between devices: 126 us -> none  [attention_residual(): att = lax.psum_scatter(part, 'tp', scatter_dimension=0, tiled=True)]
    all_gather x2 -> x0, waiting for transfers between devices: 82.3 us -> none  [the longest x1 75.3 us: attention_residual(): xs = lax.all_gather(x, 'tp', axis=0, tiled=True)]
    dot_general x3 -> x0, matrix products: 44.1 us -> none  [the longest x1 18.7 us: attention_residual(): part = jnp.dot(o, wo, preferred_element_type=jnp.float32)]
    pmax x1 -> x0, blocking collectives: 22.4 us -> none  [local(): worst = lax.pmax(count, ('cp', 'tp'))]
  transfers between devices with their start and end apart: 4 -> 1, of which waited for: 4 -> 1; matrix products, arithmetic and copies ran while one was open for 2% -> 0% of each run, Pallas kernels for 0% -> 0%
where the time goes in v3:
time: 602 us; the launch traced here: 593 us
  Pallas kernels  188 us (31%)
  matrix products  133 us (22%)
  blocking collectives  127 us (21%)
  waiting for transfers between devices  122 us (20%)
  loops' own time  11.3 us (2%)
    all_to_all x1, blocking collectives, moe_any(): lax.all_to_all(send.reshape(ne, cap, hd), ('cp', 'tp'), 0, 0, tiled=True)  127 us
    all_to_all x1, waiting for transfers between devices, moe_any(): lax.all_to_all(z.reshape(ne, cap, hd), ('cp', 'tp'), 0, 0, tiled=True)  122 us
    pallas_call x1, Pallas kernels, attention(): pl.pallas_call(functools.partial(attn_kernel, cp), in_specs=[vm, vm, vm,...  112 us
    pallas_call x1, Pallas kernels, qkv(): pl.pallas_call(functools.partial(qkv_kernel, cp, ne), in_specs=[vm, vm, h...  75.6 us
    dot_general x1, matrix products, expert_ffn(): uu = jnp.dot(rows, wu, preferred_element_type=jnp.float32)  39.4 us
    dot_general x1, matrix products, expert_ffn(): gg = jnp.dot(rows, wg, preferred_element_type=jnp.float32)  33.1 us
    dot_general x1, matrix products, expert_ffn(): jnp.dot(act, wd, preferred_element_type=jnp.float32).astype(jnp.bfloat16)  32.4 us
    dot_general x2, matrix products, moe_any(): jnp.dot(sel, back, preferred_element_type=jnp.float32)  17.8 us
  transfers between devices with their start and end apart: 1, of which 1 were waited for; matrix products, arithmetic and copies ran while one was open for 0% of the time, Pallas kernels for 0%

profile of v3, /device:TPU:0, one launch (start us, length us, event | category | flops | bytes accessed | tf_op | source)
XLA Modules:
  0.0 593.4 jit_solution(13128287914588852275)
XLA Ops:
  0.0 0.8 slice_reduce_fusion.7
  0.8 0.3 convert_reduce_fusion
  1.0 0.7 broadcast_in_dim.15.cnt_ref
  1.7 0.0 copy-start.4
  1.7 0.0 copy-start.7
  1.7 75.6 %qkv.1 = (bf16[1536,896]{1,0:T(8,128)(2,1)}, bf16[3072,256]{1,0:T(8,128)(2,1)}, s32[8,8,128]{2,1,0:T(8,128)}) custom-call(bf16[384,3584]{1,0:T(8,128)(2,1)} %x_ref.3, s32[8,128]{1,0:T(8,128)} %broadcast_in_dim.15.cnt_ref, bf16[3584,896]{1,0:T(8,128)(2,1)} %wq_ref.1, bf16[3584,128]{1,0:T(8,128)(2,1)} %wk_ref.1, bf16[3584,128]{1,0:T(8,128)(2,1)} %wv_ref.1), custom_call_target="tpu_custom_call" | custom-call | tf_op jit(solution)/shard_map/qkv/pallas_call | solution.py:262
  77.3 0.0 copy-start.3
  77.3 112.3 %attn.1 = bf16[384,3584]{1,0:T(8,128)(2,1)} custom-call(bf16[1536,896]{1,0:T(8,128)(2,1)} %get-tuple-element.54.q_ref, bf16[3072,256]{1,0:T(8,128)(2,1)} %get-tuple-element.55.kv_ref, bf16[384,3584]{1,0:T(8,128)(2,1)} %x_ref.3, bf16[896,3584]{1,0:T(8,128)(2,1)} %wo_ref.1), custom_call_target="tpu_custom_call" | custom-call | tf_op jit(solution)/shard_map/attn/pallas_call | solution.py:410
  189.6 0.0 copy-done.3
  189.6 0.6 reduce_max.9
  190.9 0.0 copy-done.4
  190.9 0.0 copy-done.7
  190.9 398.5 %conditional.1 = (bf16[384,3584]{1,0:T(8,128)(2,1)}) conditional(s32[]{:T(128)} %convert_element_type.31, (bf16[384,3584]{1,0:T(8,128)(2,1)}, f32[384,2]{0,1:T(2,128)S(1)}, s32[384,2]{0,1:T(2,128)S(1)}, s32[8,384]{1,0:T(8,128)S(1)}, bf16[1,3584,2560]{2,1,0:T(8,128)(2,1)}, /*index=5*/bf16[1,3584,2560]{2,1,0:T(8,128)(2,1)}, ...), branch_computations={%region_2.5_spmd, %region_5.8_spmd} | conditional | flops 97285398528 | bytes 365126240 | solution.py:475
  201.8 0.0 copy-start.1
  201.8 0.0 copy-start.5
  201.8 0.0 copy-start.8
  201.9 0.1 eq.27
  201.9 0.4 bitcast_compare_fusion
  202.3 0.0 slice-start
  202.3 0.0 slice-start.1
  202.3 0.0 slice-start.2
  202.4 10.4 %convolution_convert_fusion = bf16[1536,3584]{1,0:T(8,128)(2,1)} fusion(pred[1536,384]{1,0:T(32,128)(4,1)S(1)} %bitcast_compare_fusion, bf16[384,3584]{1,0:T(8,128)(2,1)} %get-tuple-element.36), kind=kOutput, calls=%fused_computation.8 | convolution fusion | flops 4233363456 | bytes 14352384 | tf_op jit(solution)/shard_map/cond/branch_0_fun/dot_general | solution.py:441
  212.8 0.0 slice-start.3
  212.8 0.0 slice-start.4
  212.8 127.2 %all_to_all.8 = bf16[8,192,3584]{2,1,0:T(8,128)(2,1)} all-to-all(bf16[8,192,3584]{2,1,0:T(8,128)(2,1)} %bitcast.40), channel_id=1, replica_groups=mesh['dp'=1,'cp'=2,'tp'=4] {'cp','tp'}, dimensions={0} | all-to-all | bytes 22020096 | tf_op jit(solution)/shard_map/cond/branch_0_fun/all_to_all | solution.py:442
  340.0 0.0 copy-done.1
  340.0 0.0 copy-done.5
  340.0 0.0 copy-done.8
  340.0 0.0 slice-done
  340.0 0.0 slice-done.1
  340.0 0.0 slice-done.2
  340.0 0.0 slice-done.3
  340.0 0.0 slice-done.4
  340.0 0.0 slice-start.5
  340.1 0.0 slice-start.6
  340.1 0.0 slice-start.7
  340.1 33.1 %fusion.4 = f32[1536,2560]{1,0:T(8,128)} fusion(bf16[1536,3584]{1,0:T(8,128)(2,1)} %bitcast.38, bf16[1,3584,2560]{2,1,0:T(8,128)(2,1)S(1)} %bitcast.31), kind=kOutput, calls=%fused_computation.4 | convolution fusion | flops 28185722880 | bytes 45088768 | tf_op jit(solution)/shard_map/cond/branch_0_fun/dot_general | solution.py:421
  373.2 0.0 slice-start.8
  373.2 0.0 slice-start.9
  373.2 39.4 %multiply_convert_fusion = bf16[1536,2560]{1,0:T(8,128)(2,1)} fusion(f32[1536,2560]{1,0:T(8,128)} %fusion.4, bf16[1536,3584]{1,0:T(8,128)(2,1)} %bitcast.39, bf16[1,3584,2560]{2,1,0:T(8,128)(2,1)} %get-tuple-element.41), kind=kOutput, calls=%fused_computation.6 | convolution fusion | flops 28209315840 | bytes 52953088 | tf_op jit(solution)/shard_map/cond/branch_0_fun/dot_general | solution.py:422
  412.6 0.0 slice-done.5
  412.6 0.0 slice-done.6
  412.6 0.0 slice-done.7
  412.6 0.0 slice-done.8
  412.6 0.0 slice-done.9
  412.6 32.4 %fusion.6 = bf16[1536,3584]{1,0:T(8,128)(2,1)} fusion(bf16[1536,2560]{1,0:T(8,128)(2,1)} %multiply_convert_fusion, bf16[1,2560,3584]{2,1,0:T(8,128)(2,1)S(1)} %bitcast.35), kind=kOutput, calls=%fused_computation.7 | convolution fusion | flops 28191227904 | bytes 37224448 | tf_op jit(solution)/shard_map/cond/branch_0_fun/dot_general | solution.py:424
  445.0 0.0 copy-start.6
  445.0 0.0 copy-start.9
  445.0 0.0 copy-start.2
  445.0 4.3 all-to-all-start.1
  449.3 0.0 copy-done.6
  449.3 0.0 copy-done.9
  449.4 0.0 copy-done.2
  449.4 0.1 select_reduce_fusion.1
  449.5 121.9 %all-to-all-done.1 = bf16[8,192,3584]{2,1,0:T(8,128)(2,1)} async-done(((bf16[8,192,3584]{2,1,0:T(8,128)(2,1)}), bf16[8,192,3584]{2,1,0:T(8,128)(2,1)}, u32[]{:S(2)}, u32[]{:S(2)}) %all-to-all-start.1) | async-done | bytes 11010080 | tf_op jit(solution)/shard_map/cond/branch_0_fun/all_to_all | solution.py:444
  571.4 0.0 copy-start
  571.4 7.5 %convolution_multiply_fusion = f32[384,3584]{1,0:T(8,128)S(1)} fusion(bf16[1536,3584]{1,0:T(8,128)(2,1)} %bitcast.7, f32[384]{0:T(512)S(1)} %get-tuple-element.83, s32[384]{0:T(512)S(1)} %get-tuple-element.79), kind=kOutput, calls=%fused_computation.9 | convolution fusion | flops 4229824512 | bytes 16518144 | tf_op jit(solution)/shard_map/cond/branch_0_fun/dot_general | solution.py:450
  578.9 0.0 copy-done
  578.9 10.3 %fusion.13 = bf16[384,3584]{1,0:T(8,128)(2,1)} fusion(f32[384,3584]{1,0:T(8,128)S(1)} %convolution_multiply_fusion, bf16[1536,3584]{1,0:T(8,128)(2,1)} %bitcast.7, bf16[384,3584]{1,0:T(8,128)(2,1)S(1)} %copy-done, f32[384]{0:T(512)S(1)} %get-tuple-element.82, s32[384]{0:T(512)S(1)} %get-tuple-element.78), kind=kOutput, calls=%fused_computation.13 | convolution fusion | flops 4235329536 | bytes 22023168 | tf_op jit(solution)/shard_map/cond/branch_0_fun/dot_general | solution.py:450
  589.4 3.5 copy.24
  (6 shorter events, 0.1 us)
Async XLA Ops:
  1.7 189.2 %copy-start.4 = (s32[384,2]{0,1:T(2,128)S(1)}, s32[384,2]{0,1:T(2,128)}, u32[]{:S(2)}) copy-start(s32[384,2]{0,1:T(2,128)} %param.13) | copy-start | bytes 9220
  1.7 189.2 %copy-start.7 = (f32[384,2]{0,1:T(2,128)S(1)}, f32[384,2]{0,1:T(2,128)}, u32[]{:S(2)}) copy-start(f32[384,2]{0,1:T(2,128)} %param.14) | copy-start | bytes 9220
  77.3 112.3 %copy-start.3 = (s32[8,8,128]{2,1,0:T(8,128)S(1)}, s32[8,8,128]{2,1,0:T(8,128)}, u32[]{:S(2)}) copy-start(s32[8,8,128]{2,1,0:T(8,128)} %get-tuple-element.53) | copy-start | bytes 98308
  201.8 138.2 %copy-start.1 = (s32[8,384]{1,0:T(8,128)}, s32[8,384]{1,0:T(8,128)S(1)}, u32[]{:S(2)}) copy-start(s32[8,384]{1,0:T(8,128)S(1)} %get-tuple-element.39) | copy-start | bytes 36868 | tf_op jit(solution)/shard_map/cond
  201.8 138.1 %copy-start.5 = (s32[384,2]{0,1:T(2,128)}, s32[384,2]{0,1:T(2,128)S(1)}, u32[]{:S(2)}) copy-start(s32[384,2]{0,1:T(2,128)S(1)} %get-tuple-element.38) | copy-start | bytes 9220 | tf_op jit(solution)/shard_map/cond
  201.8 138.1 %copy-start.8 = (f32[384,2]{0,1:T(2,128)}, f32[384,2]{0,1:T(2,128)S(1)}, u32[]{:S(2)}) copy-start(f32[384,2]{0,1:T(2,128)S(1)} %get-tuple-element.37) | copy-start | bytes 9220 | tf_op jit(solution)/shard_map/cond
  202.3 137.7 %slice-start = ((s8[18350080]{0:T(1024)(128)(4,1)}), s8[4194304]{0:T(1024)(128)(4,1)S(1)}, s32[]{:S(2)}) async-start(s8[18350080]{0:T(1024)(128)(4,1)} %bitcast.30), calls=%async_computation.2 | async-start | bytes 8388608 | tf_op jit(solution)/shard_map/cond
  202.3 137.7 %slice-start.1 = ((s8[18350080]{0:T(1024)(128)(4,1)}), s8[4194304]{0:T(1024)(128)(4,1)S(1)}, s32[]{:S(2)}) async-start(s8[18350080]{0:T(1024)(128)(4,1)} %bitcast.30), calls=%async_computation.3 | async-start | bytes 8388608 | tf_op jit(solution)/shard_map/cond
  202.3 137.7 %slice-start.2 = ((s8[18350080]{0:T(1024)(128)(4,1)}), s8[4194304]{0:T(1024)(128)(4,1)S(1)}, s32[]{:S(2)}) async-start(s8[18350080]{0:T(1024)(128)(4,1)} %bitcast.30), calls=%async_computation.4 | async-start | bytes 8388608 | tf_op jit(solution)/shard_map/cond
  212.8 127.2 %slice-start.3 = ((s8[18350080]{0:T(1024)(128)(4,1)}), s8[4194304]{0:T(1024)(128)(4,1)S(1)}, s32[]{:S(2)}) async-start(s8[18350080]{0:T(1024)(128)(4,1)} %bitcast.30), calls=%async_computation.5 | async-start | bytes 8388608 | tf_op jit(solution)/shard_map/cond
  212.8 127.2 %slice-start.4 = ((s8[18350080]{0:T(1024)(128)(4,1)}), s8[1572864]{0:T(1024)(128)(4,1)S(1)}, s32[]{:S(2)}) async-start(s8[18350080]{0:T(1024)(128)(4,1)} %bitcast.30), calls=%async_computation.6 | async-start | bytes 3145728 | tf_op jit(solution)/shard_map/cond
  340.0 72.5 %slice-start.5 = ((s8[18350080]{0:T(1024)(128)(4,1)}), s8[4194304]{0:T(1024)(128)(4,1)S(1)}, s32[]{:S(2)}) async-start(s8[18350080]{0:T(1024)(128)(4,1)} %bitcast.34), calls=%async_computation.7 | async-start | bytes 8388608 | tf_op jit(solution)/shard_map/cond
  340.1 72.5 %slice-start.6 = ((s8[18350080]{0:T(1024)(128)(4,1)}), s8[4194304]{0:T(1024)(128)(4,1)S(1)}, s32[]{:S(2)}) async-start(s8[18350080]{0:T(1024)(128)(4,1)} %bitcast.34), calls=%async_computation.8 | async-start | bytes 8388608 | tf_op jit(solution)/shard_map/cond
  340.1 72.5 %slice-start.7 = ((s8[18350080]{0:T(1024)(128)(4,1)}), s8[1572864]{0:T(1024)(128)(4,1)S(1)}, s32[]{:S(2)}) async-start(s8[18350080]{0:T(1024)(128)(4,1)} %bitcast.34), calls=%async_computation.9 | async-start | bytes 3145728 | tf_op jit(solution)/shard_map/cond
  373.2 39.4 %slice-start.8 = ((s8[18350080]{0:T(1024)(128)(4,1)}), s8[4194304]{0:T(1024)(128)(4,1)S(1)}, s32[]{:S(2)}) async-start(s8[18350080]{0:T(1024)(128)(4,1)} %bitcast.34), calls=%async_computation.10 | async-start | bytes 8388608 | tf_op jit(solution)/shard_map/cond
  373.2 39.4 %slice-start.9 = ((s8[18350080]{0:T(1024)(128)(4,1)}), s8[4194304]{0:T(1024)(128)(4,1)S(1)}, s32[]{:S(2)}) async-start(s8[18350080]{0:T(1024)(128)(4,1)} %bitcast.34), calls=%async_computation.11 | async-start | bytes 8388608 | tf_op jit(solution)/shard_map/cond
  445.0 4.3 copy-start.6
  445.0 4.3 copy-start.9
  445.0 4.4 copy-start.2
  445.0 126.4 %all-to-all-start.1 = ((bf16[8,192,3584]{2,1,0:T(8,128)(2,1)}), bf16[8,192,3584]{2,1,0:T(8,128)(2,1)}, u32[]{:S(2)}, u32[]{:S(2)}) async-start(bf16[8,192,3584]{2,1,0:T(8,128)(2,1)} %bitcast.37), calls=%async_computation.1 | async-start | bytes 22020096 | tf_op jit(solution)/shard_map/cond/branch_0_fun/all_to_all | solution.py:444
  571.4 7.5 %copy-start = (bf16[384,3584]{1,0:T(8,128)(2,1)S(1)}, bf16[384,3584]{1,0:T(8,128)(2,1)}, u32[]{:S(2)}) copy-start(bf16[384,3584]{1,0:T(8,128)(2,1)} %get-tuple-element.36) | copy-start | bytes 8257540 | tf_op jit(solution)/shard_map/cond

commit v4 on v3

--- a/solution.py
+++ b/solution.py
@@ -11,7 +11,7 @@
 
 MESH = pl.DeviceIdType.MESH
 NEAR = 6
-FT = 256
+FT = 512
 NT = 512
 
 
@@ -29,15 +29,19 @@
     return (lax.axis_index('dp'), c, t)
 
 
-def greet(peers):
+def hail(peers):
     bar = pltpu.get_barrier_semaphore()
     for r in peers:
         pl.semaphore_signal(bar, inc=1, device_id=device(r), device_id_type=MESH)
-    pl.semaphore_wait(bar, len(peers))
-
-
-def moe_kernel(ne, cap, h_ref, slot_ref, flat_ref, gate_ref, w1g_ref, w1u_ref, w2_ref, y_ref,
-               send, recv, act, zsend, zrecv, pick, w1b, w2b, ds, dr, zs, zr, w1s, w2s):
+
+
+def greet(peers):
+    hail(peers)
+    pl.semaphore_wait(pltpu.get_barrier_semaphore(), len(peers))
+
+
+def moe_kernel(ne, cap, h_ref, slot_ref, meta_ref, w1g_ref, w1u_ref, w2_ref, y_ref,
+               send, recv, act, zsend, zrecv, sel, pick, w1b, w2b, ds, dr, zs, zr, zf, w1s, w2s):
     t, hd = h_ref.shape
     ff = w2_ref.shape[0]
     nf, nz = ff // FT, hd // NT
@@ -55,42 +59,49 @@
     for s in range(2):
         w2_copy(s, s).start()
 
-    def out_copy(r):
-        return pltpu.make_async_remote_copy(src_ref=send.at[r], dst_ref=recv.at[r], send_sem=ds.at[r], recv_sem=dr.at[r], device_id=device(r), device_id_type=MESH)
-
-    def dispatch(r, dst):
+    hail(range(1, ne))
+    tile = lambda n: pl.ds(pl.multiple_of(n * NT, NT), NT)
+
+    def out_copy(r, cols=slice(None)):
+        return pltpu.make_async_remote_copy(src_ref=send.at[r, :, cols], dst_ref=recv.at[r, :, cols], send_sem=ds.at[r], recv_sem=dr.at[r], device_id=device(r), device_id_type=MESH)
+
+    for r in range(ne):
         c, tt = peer(r)
         row = slot_ref[pl.ds(c * (ne // 2) + tt, 1), :]
-        sel = (jnp.broadcast_to(row, (cap, t)) == lax.broadcasted_iota(jnp.int32, (cap, t), 0)).astype(jnp.bfloat16)
-
-        def tile(n, _):
-            cols = pl.ds(pl.multiple_of(n * NT, NT), NT)
-            dst[r, :, cols] = jnp.dot(sel, h_ref[:, cols], preferred_element_type=jnp.float32).astype(jnp.bfloat16)
+        sel[r * cap:(r + 1) * cap, :] = (jnp.broadcast_to(row, (cap, t)) == lax.broadcasted_iota(jnp.int32, (cap, t), 0)).astype(jnp.bfloat16)
+    pl.semaphore_wait(pltpu.get_barrier_semaphore(), ne - 1)
+
+    def dispatch(lo, hi, order):
+        def one(n, _):
+            rows = jnp.dot(sel[lo * cap:hi * cap, :], h_ref[:, tile(n)], preferred_element_type=jnp.float32).astype(jnp.bfloat16)
+            for r in range(lo, hi):
+                dst = recv if r == 0 else send
+                dst[r, :, tile(n)] = rows[(r - lo) * cap:(r - lo + 1) * cap]
+
+            @pl.when(n > 0)
+            def _():
+                for r in order:
+                    out_copy(r, tile(n - 1)).start()
             return 0
-        lax.fori_loop(0, nz, tile, 0)
-
-    order = (2, 4, 3, 5, 6, 7, 1)
-    dispatch(order[0], send)
-    greet(range(1, ne))
-    for a, r in enumerate(order):
-        if a + 1 < len(order):
-            dispatch(order[a + 1], send)
-        else:
-            dispatch(0, recv)
-        out_copy(r).start()
+        lax.fori_loop(0, nz, one, 0)
+        for r in order:
+            out_copy(r, tile(nz - 1)).start()
+
+    dispatch(0, NEAR, (2, 4, 3, 5, 1))
+    dispatch(NEAR, ne, (6, 7))
     for k in range(2):
-        pick[k * t:(k + 1) * t, :] = (flat_ref[:, k:k + 1] == lax.broadcasted_iota(jnp.int32, (t, ne * cap), 1)).astype(jnp.bfloat16)
-
-    def back_copy(r, tile):
-        cols = pl.ds(pl.multiple_of(tile * NT, NT), NT)
-        return pltpu.make_async_remote_copy(src_ref=zsend.at[r, :, cols], dst_ref=zrecv.at[r, :, cols], send_sem=zs.at[r], recv_sem=zr.at[r], device_id=device(r), device_id_type=MESH)
+        pick[k * t:(k + 1) * t, :] = (meta_ref[:, k:k + 1] == lax.broadcasted_iota(jnp.int32, (t, ne * cap), 1).astype(jnp.float32)).astype(jnp.bfloat16)
+
+    def back_copy(r, n):
+        got = zr.at[r] if r < NEAR else zf.at[r - NEAR, n]
+        return pltpu.make_async_remote_copy(src_ref=zsend.at[r, :, tile(n)], dst_ref=zrecv.at[r, :, tile(n)], send_sem=zs.at[r], recv_sem=got, device_id=device(r), device_id_type=MESH)
 
     def experts(lo, hi, again):
         rows = (hi - lo) * cap
-        off = 0 if again else nz
+        off, off1 = (0, 0) if again else (nz, nf)
 
         def up(f, _):
-            slot = lax.rem(f, 2)
+            slot = lax.rem(f + off1, 2)
             w1_copy(f, slot, 0).wait()
             w1_copy(f, slot, 1).wait()
             xr = recv[lo:hi].reshape(rows, hd)
@@ -136,13 +147,15 @@
         out_copy(r).wait_recv()
     experts(NEAR, ne, False)
     whole = lambda r: pltpu.make_async_remote_copy(src_ref=zsend.at[r], dst_ref=zrecv.at[r], send_sem=zs.at[r], recv_sem=zr.at[r], device_id=device(r), device_id_type=MESH)
-    for r in range(1, ne):
+    for r in range(1, NEAR):
         whole(r).wait_recv()
 
     def combine(n, _):
-        cols = pl.ds(pl.multiple_of(n * NT, NT), NT)
+        cols = tile(n)
+        for r in range(NEAR, ne):
+            back_copy(r, n).wait_recv()
         zt = jnp.dot(pick[...], zrecv[:, :, cols].reshape(ne * cap, NT), preferred_element_type=jnp.float32)
-        y = h_ref[:, cols].astype(jnp.float32) + (gate_ref[:, 0:1] * zt[:t] + gate_ref[:, 1:2] * zt[t:])
+        y = h_ref[:, cols].astype(jnp.float32) + (meta_ref[:, 2:3] * zt[:t] + meta_ref[:, 3:4] * zt[t:])
         y_ref[:, cols] = y.astype(jnp.bfloat16)
         return 0
     lax.fori_loop(0, nz, combine, 0)
@@ -151,30 +164,23 @@
         whole(r).wait_send()
 
 
-def moe_fast(h, slot, idx, gates, w1g, w1u, w2, cap, cid):
+def moe_fast(h, slot, meta, w1g, w1u, w2, cap, cid):
     t, hd = h.shape
     ne = slot.shape[0]
-    me = lax.axis_index('cp') * (ne // 2) + lax.axis_index('tp')
-    e = jnp.arange(ne)
-    flat = []
-    for k in range(2):
-        hit = idx[:, k][None, :] == e[:, None]
-        flat.append(jnp.sum(jnp.where(hit, (e ^ me)[:, None] * cap + slot, 0), axis=0))
-    flat = jnp.stack(flat, axis=1)
     vm = pl.BlockSpec(memory_space=pltpu.VMEM)
     hb = pl.BlockSpec(memory_space=pl.ANY)
     bf = jnp.bfloat16
     ff = w2.shape[0]
     return pl.pallas_call(
         functools.partial(moe_kernel, ne, cap),
-        in_specs=[vm, vm, vm, vm, hb, hb, hb], out_specs=vm,
+        in_specs=[vm, vm, vm, hb, hb, hb], out_specs=vm,
         out_shape=jax.ShapeDtypeStruct((t, hd), bf),
         scratch_shapes=[pltpu.VMEM((ne, cap, hd), bf), pltpu.VMEM((ne, cap, hd), bf), pltpu.VMEM((NEAR * cap, ff), bf),
-                        pltpu.VMEM((ne, cap, hd), bf), pltpu.VMEM((ne, cap, hd), bf), pltpu.VMEM((2 * t, ne * cap), bf),
+                        pltpu.VMEM((ne, cap, hd), bf), pltpu.VMEM((ne, cap, hd), bf), pltpu.VMEM((ne * cap, t), bf), pltpu.VMEM((2 * t, ne * cap), bf),
                         pltpu.VMEM((2, 2, hd, FT), bf), pltpu.VMEM((2, ff, NT), bf)]
-                       + [pltpu.SemaphoreType.DMA((ne,))] * 4 + [pltpu.SemaphoreType.DMA((2, 2)), pltpu.SemaphoreType.DMA((2,))],
+                       + [pltpu.SemaphoreType.DMA((ne,))] * 4 + [pltpu.SemaphoreType.DMA((ne - NEAR, hd // NT))] + [pltpu.SemaphoreType.DMA((2, 2)), pltpu.SemaphoreType.DMA((2,))],
         compiler_params=pltpu.CompilerParams(collective_id=cid, has_side_effects=True, vmem_limit_bytes=63 * 1024 * 1024),
-        name='moe')(h, slot, flat, gates, w1g, w1u, w2)
+        name='moe')(h, slot, meta, w1g, w1u, w2)
 
 
 D = 128
@@ -199,8 +205,8 @@
     return pltpu.make_async_remote_copy(src_ref=src, dst_ref=dst, send_sem=send, recv_sem=recv, device_id=dev, device_id_type=MESH)
 
 
-def qkv_kernel(cp, ne, x_ref, cnt_ref, wq_ref, wk_ref, wv_ref, q_ref, kv_ref, all_ref,
-               xs, wqb, wkvb, cs, cr, xsnd, xrcv, fs, fr, bs, br, ks, kr, ws):
+def qkv_kernel(cp, ne, x_ref, idx_ref, gate_ref, wq_ref, wk_ref, wv_ref, q_ref, kv_ref, all_ref, slot_ref, meta_ref,
+               cnt, xs, wqb, wkvb, cs, cr, xsnd, xrcv, fs, fr, bs, br, ks, kr, ws):
     t = x_ref.shape[0]
     step = t // PIECES
     loads = [pltpu.make_async_copy(wk_ref, wkvb.at[:, :D], ws.at[0]), pltpu.make_async_copy(wv_ref, wkvb.at[:, D:], ws.at[1]),
@@ -208,9 +214,6 @@
     for ld in loads:
         ld.start()
     greet(range(1, ne))
-    counts = [remote(cnt_ref, all_ref.at[r], cs.at[r], cr.at[r], device(r)) for r in range(1, ne)]
-    for cc in counts:
-        cc.start()
     rows = lambda p: pl.ds(p * step, step)
     across = [remote(x_ref.at[rows(p)], xs.at[1, rows(p)], xsnd.at[p], xrcv.at[p], device(2)) for p in range(PIECES)]
     for a in across:
@@ -218,7 +221,22 @@
     beside = remote(x_ref, xs.at[0], bs.at[0], br.at[0], device(1))
     beside.start()
     onward = [remote(xs.at[1, rows(p)], xs.at[2, rows(p)], fs.at[p], fr.at[p], device(1)) for p in range(PIECES)]
-    all_ref[0] = cnt_ref[...]
+    lane = lax.broadcasted_iota(jnp.int32, (t, 128), 1)
+    named = [idx_ref[:, i:i + 1] == lane for i in range(2)]
+    hit = (named[0] | named[1]).astype(jnp.float32)
+    before = (lax.broadcasted_iota(jnp.int32, (t, t), 1) < lax.broadcasted_iota(jnp.int32, (t, t), 0)).astype(jnp.bfloat16)
+    rank = jnp.dot(before, hit.astype(jnp.bfloat16), preferred_element_type=jnp.float32)
+    slot_ref[...] = jnp.transpose(jnp.where(hit > 0, rank, -1.0))[:ne].astype(jnp.int32)
+    cnt[...] = jnp.broadcast_to(jnp.sum(hit, axis=0, keepdims=True), (8, 128)).astype(jnp.int32)
+    me = lax.axis_index('cp') * (ne // cp) + lax.axis_index('tp')
+    place = jnp.bitwise_xor(lane, me).astype(jnp.float32) * (2 * t // ne) + rank
+    meta = jnp.zeros((t, 128), jnp.float32)
+    for i in range(2):
+        at = jnp.sum(jnp.where(named[i], place, 0.0), axis=1, keepdims=True)
+        meta = jnp.where(lane == i, at, jnp.where(lane == 2 + i, gate_ref[:, i:i + 1], meta))
+    meta_ref[...] = meta
+    all_ref[0] = cnt[...]
+    counts = [remote(cnt, all_ref.at[r], cs.at[r], cr.at[r], device(r)) for r in range(1, ne)]
     for ld in loads:
         ld.wait()
     sent = []
@@ -235,6 +253,8 @@
         sent.append(out)
 
     project(x_ref[...], 0, 0, t)
+    for cc in counts:
+        cc.start()
     beside.wait_recv()
     project(xs[0], 1, 0, t)
     for p in range(PIECES):
@@ -251,7 +271,7 @@
         o.wait_send()
 
 
-def qkv(x, cnt, wq, wk, wv, cp, ne, cid):
+def qkv(x, idx, gates, wq, wk, wv, cp, ne, cid):
     t, hd = x.shape
     tp = ne // cp
     vm = pl.BlockSpec(memory_space=pltpu.VMEM)
@@ -261,12 +281,12 @@
     nk = 2 + 2 * PIECES
     return pl.pallas_call(
         functools.partial(qkv_kernel, cp, ne),
-        in_specs=[vm, vm, hb, hb, hb], out_specs=[vm, vm, vm],
-        out_shape=[jax.ShapeDtypeStruct((tp * t, wq.shape[1]), bf), jax.ShapeDtypeStruct((ne * t, 2 * D), bf), jax.ShapeDtypeStruct((ne,) + cnt.shape, jnp.int32)],
-        scratch_shapes=[pltpu.VMEM((3, t, hd), bf), pltpu.VMEM(wq.shape, bf), pltpu.VMEM((hd, 2 * D), bf),
+        in_specs=[vm, vm, vm, hb, hb, hb], out_specs=[vm] * 5,
+        out_shape=[jax.ShapeDtypeStruct((tp * t, wq.shape[1]), bf), jax.ShapeDtypeStruct((ne * t, 2 * D), bf), jax.ShapeDtypeStruct((ne, 8, 128), jnp.int32), jax.ShapeDtypeStruct((ne, t), jnp.int32), jax.ShapeDtypeStruct((t, 128), jnp.float32)],
+        scratch_shapes=[pltpu.VMEM((8, 128), jnp.int32), pltpu.VMEM((3, t, hd), bf), pltpu.VMEM(wq.shape, bf), pltpu.VMEM((hd, 2 * D), bf),
                         dma((ne,)), dma((ne,)), dma((PIECES,)), dma((PIECES,)), dma((PIECES,)), dma((PIECES,)), dma((1,)), dma((1,)), dma((nk,)), dma((nk,)), dma((3,))],
         compiler_params=pltpu.CompilerParams(collective_id=cid, has_side_effects=True, vmem_limit_bytes=60 * 1024 * 1024),
-        name='qkv')(x, cnt, wq, wk, wv)
+        name='qkv')(x, idx, gates, wq, wk, wv)
 
 
 def attn_kernel(cp, q_ref, kv_ref, x_ref, wo_ref, h_ref, wof, ocat, obuf, m_ref, l_ref, acc_ref, part,
@@ -424,15 +444,6 @@
     return jnp.dot(act, wd, preferred_element_type=jnp.float32).astype(jnp.bfloat16)
 
 
-def routing(idx, ne):
-    t = idx.shape[0]
-    it = idx.T
-    hit = (it[0][None, :] == jnp.arange(ne)[:, None]) | (it[1][None, :] == jnp.arange(ne)[:, None])
-    before = (jnp.arange(t)[:, None] < jnp.arange(t)[None, :]).astype(jnp.bfloat16)
-    rank = jnp.dot(hit.astype(jnp.bfloat16), before, preferred_element_type=jnp.float32).astype(jnp.int32)
-    return jnp.where(hit, rank, -1)
-
-
 def moe_any(h, slot, idx, gates, wg, wu, wd):
     t, hd = h.shape
     ne = slot.shape[0]
@@ -460,14 +471,12 @@
 
     def local(x, idx, gates, wq, wk, wv, wo, w1g, w1u, w2):
         t, hd = x.shape
-        slot = routing(idx, ne)
-        counts = jnp.broadcast_to(jnp.sum((slot >= 0).astype(jnp.int32), axis=1)[:, None], (ne, D))
-        q, kv, counts = qkv(x, counts, wq, wk, wv, cp, ne, 1)
+        q, kv, counts, slot, meta = qkv(x, idx, gates, wq, wk, wv, cp, ne, 1)
         h = attention(q, kv, x, wo, cp, 2)
         worst = jnp.max(counts)
 
         def tight(h):
-            return moe_fast(h, slot, idx, gates, w1g[0], w1u[0], w2[0], t // 4, 3)
+            return moe_fast(h, slot, meta, w1g[0], w1u[0], w2[0], t // 4, 3)
 
         def roomy(h):
             return moe_any(h, slot, idx, gates, w1g[0], w1u[0], w2[0])

time: 602 us -> 603 us (level)
  no operation moved by 1% of the time
where the time goes in v4:
time: 603 us; the launch traced here: 595 us
  Pallas kernels  188 us (31%)
  matrix products  133 us (22%)
  blocking collectives  127 us (21%)
  waiting for transfers between devices  122 us (20%)
  loops' own time  11.3 us (2%)
  local copies, waits for them, and re-layouts  6.7 us (1%)
    all_to_all x1, blocking collectives, moe_any(): lax.all_to_all(send.reshape(ne, cap, hd), ('cp', 'tp'), 0, 0, tiled=True)  127 us
    all_to_all x1, waiting for transfers between devices, moe_any(): lax.all_to_all(z.reshape(ne, cap, hd), ('cp', 'tp'), 0, 0, tiled=True)  122 us
    pallas_call x1, Pallas kernels, attention(): pl.pallas_call(functools.partial(attn_kernel, cp), in_specs=[vm, vm, vm,...  112 us
    pallas_call x1, Pallas kernels, qkv(): pl.pallas_call(functools.partial(qkv_kernel, cp, ne), in_specs=[vm, vm, v...  75.5 us
    dot_general x1, matrix products, expert_ffn(): uu = jnp.dot(rows, wu, preferred_element_type=jnp.float32)  39.4 us
    dot_general x1, matrix products, expert_ffn(): gg = jnp.dot(rows, wg, preferred_element_type=jnp.float32)  33.1 us
    dot_general x1, matrix products, expert_ffn(): jnp.dot(act, wd, preferred_element_type=jnp.float32).astype(jnp.bfloat16)  32.4 us
    dot_general x2, matrix products, moe_any(): jnp.dot(sel, back, preferred_element_type=jnp.float32)  17.8 us
  transfers between devices with their start and end apart: 1, of which 1 were waited for; matrix products, arithmetic and copies ran while one was open for 0% of the time, Pallas kernels for 0%

profile of v4, /device:TPU:0, one launch (start us, length us, event | category | flops | bytes accessed | tf_op | source)
XLA Modules:
  0.0 594.5 jit_solution(6108146039224213101)
XLA Ops:
  0.0 1.5 copy.13.idx_ref
  1.5 1.5 copy.14.gate_ref
  3.0 75.5 %qkv.1 = (bf16[1536,896]{1,0:T(8,128)(2,1)}, bf16[3072,256]{1,0:T(8,128)(2,1)}, s32[8,8,128]{2,1,0:T(8,128)}, s32[8,384]{1,0:T(8,128)S(1)}, f32[384,128]{1,0:T(8,128)S(1)}) custom-call(bf16[384,3584]{1,0:T(8,128)(2,1)} %x_ref.3, s32[384,2]{1,0:T(8,128)} %copy.13.idx_ref, f32[384,2]{1,0:T(8,128)} %copy.14.gate_ref, bf16[3584,896]{1,0:T(8,128)(2,1)} %wq_ref.1, ...), custom_call_target="tpu_custom_call" | custom-call | tf_op jit(solution)/shard_map/qkv/pallas_call | solution.py:282
  78.5 0.0 copy-start.3
  78.5 112.3 %attn.1 = bf16[384,3584]{1,0:T(8,128)(2,1)} custom-call(bf16[1536,896]{1,0:T(8,128)(2,1)} %get-tuple-element.53.q_ref, bf16[3072,256]{1,0:T(8,128)(2,1)} %get-tuple-element.54.kv_ref, bf16[384,3584]{1,0:T(8,128)(2,1)} %x_ref.3, bf16[896,3584]{1,0:T(8,128)(2,1)} %wo_ref.1), custom_call_target="tpu_custom_call" | custom-call | tf_op jit(solution)/shard_map/attn/pallas_call | solution.py:430
  190.8 0.0 copy-done.3
  190.9 0.6 reduce_max.9
  192.1 398.5 %conditional.1 = (bf16[384,3584]{1,0:T(8,128)(2,1)}) conditional(s32[]{:T(128)} %convert_element_type.21, (bf16[384,3584]{1,0:T(8,128)(2,1)}, f32[384,2]{0,1:T(2,128)}, s32[384,2]{0,1:T(2,128)}, s32[8,384]{1,0:T(8,128)S(1)}, bf16[1,3584,2560]{2,1,0:T(8,128)(2,1)}, /*index=5*/bf16[1,3584,2560]{2,1,0:T(8,128)(2,1)}, ...), branch_computations={%region_1.4_spmd, %region_4.5_spmd} | conditional | flops 97285398528 | bytes 365101600 | solution.py:484
  203.0 0.0 copy-start.1
  203.0 0.1 eq.16
  203.1 0.4 bitcast_compare_fusion
  203.5 0.0 slice-start
  203.5 0.0 slice-start.1
  203.5 0.0 slice-start.2
  203.5 10.4 %convolution_convert_fusion = bf16[1536,3584]{1,0:T(8,128)(2,1)} fusion(pred[1536,384]{1,0:T(32,128)(4,1)S(1)} %bitcast_compare_fusion, bf16[384,3584]{1,0:T(8,128)(2,1)} %get-tuple-element.34), kind=kOutput, calls=%fused_computation.8 | convolution fusion | flops 4233363456 | bytes 14352384 | tf_op jit(solution)/shard_map/cond/branch_0_fun/dot_general | solution.py:452
  214.0 0.0 slice-start.3
  214.0 0.0 slice-start.4
  214.0 127.2 %all_to_all.8 = bf16[8,192,3584]{2,1,0:T(8,128)(2,1)} all-to-all(bf16[8,192,3584]{2,1,0:T(8,128)(2,1)} %bitcast.39), channel_id=1, replica_groups=mesh['dp'=1,'cp'=2,'tp'=4] {'cp','tp'}, dimensions={0} | all-to-all | bytes 22020096 | tf_op jit(solution)/shard_map/cond/branch_0_fun/all_to_all | solution.py:453
  341.2 0.0 copy-done.1
  341.2 0.0 slice-done
  341.2 0.0 slice-done.1
  341.2 0.0 slice-done.2
  341.2 0.0 slice-done.3
  341.2 0.0 slice-done.4
  341.2 0.0 slice-start.5
  341.2 0.0 slice-start.6
  341.2 0.0 slice-start.7
  341.2 33.1 %fusion.4 = f32[1536,2560]{1,0:T(8,128)} fusion(bf16[1536,3584]{1,0:T(8,128)(2,1)} %bitcast.37, bf16[1,3584,2560]{2,1,0:T(8,128)(2,1)S(1)} %bitcast.30), kind=kOutput, calls=%fused_computation.4 | convolution fusion | flops 28185722880 | bytes 45088768 | tf_op jit(solution)/shard_map/cond/branch_0_fun/dot_general | solution.py:441
  374.3 0.0 slice-start.8
  374.3 0.0 slice-start.9
  374.3 39.4 %multiply_convert_fusion = bf16[1536,2560]{1,0:T(8,128)(2,1)} fusion(f32[1536,2560]{1,0:T(8,128)} %fusion.4, bf16[1536,3584]{1,0:T(8,128)(2,1)} %bitcast.38, bf16[1,3584,2560]{2,1,0:T(8,128)(2,1)} %get-tuple-element.39), kind=kOutput, calls=%fused_computation.6 | convolution fusion | flops 28209315840 | bytes 52953088 | tf_op jit(solution)/shard_map/cond/branch_0_fun/dot_general | solution.py:442
  413.7 0.0 slice-done.5
  413.7 0.0 slice-done.6
  413.7 0.0 slice-done.7
  413.7 0.0 slice-done.8
  413.7 0.0 slice-done.9
  413.8 32.4 %fusion.6 = bf16[1536,3584]{1,0:T(8,128)(2,1)} fusion(bf16[1536,2560]{1,0:T(8,128)(2,1)} %multiply_convert_fusion, bf16[1,2560,3584]{2,1,0:T(8,128)(2,1)S(1)} %bitcast.34), kind=kOutput, calls=%fused_computation.7 | convolution fusion | flops 28191227904 | bytes 37224448 | tf_op jit(solution)/shard_map/cond/branch_0_fun/dot_general | solution.py:444
  446.1 0.0 copy-start.4
  446.1 0.0 copy-start.5
  446.1 0.0 copy-start.2
  446.1 4.3 all-to-all-start.1
  450.5 0.0 copy-done.4
  450.5 0.0 copy-done.5
  450.5 0.0 copy-done.2
  450.5 0.1 select_reduce_fusion.1
  450.6 121.9 %all-to-all-done.1 = bf16[8,192,3584]{2,1,0:T(8,128)(2,1)} async-done(((bf16[8,192,3584]{2,1,0:T(8,128)(2,1)}), bf16[8,192,3584]{2,1,0:T(8,128)(2,1)}, u32[]{:S(2)}, u32[]{:S(2)}) %all-to-all-start.1) | async-done | bytes 11010080 | tf_op jit(solution)/shard_map/cond/branch_0_fun/all_to_all | solution.py:455
  572.6 0.0 copy-start
  572.6 7.5 %convolution_multiply_fusion = f32[384,3584]{1,0:T(8,128)S(1)} fusion(bf16[1536,3584]{1,0:T(8,128)(2,1)} %bitcast.7, f32[384]{0:T(512)S(1)} %get-tuple-element.63, s32[384]{0:T(512)S(1)} %get-tuple-element.59), kind=kOutput, calls=%fused_computation.9 | convolution fusion | flops 4229824512 | bytes 16518144 | tf_op jit(solution)/shard_map/cond/branch_0_fun/dot_general | solution.py:461
  580.1 0.0 copy-done
  580.1 10.3 %fusion.13 = bf16[384,3584]{1,0:T(8,128)(2,1)} fusion(f32[384,3584]{1,0:T(8,128)S(1)} %convolution_multiply_fusion, bf16[1536,3584]{1,0:T(8,128)(2,1)} %bitcast.7, bf16[384,3584]{1,0:T(8,128)(2,1)S(1)} %copy-done, f32[384]{0:T(512)S(1)} %get-tuple-element.62, s32[384]{0:T(512)S(1)} %get-tuple-element.58), kind=kOutput, calls=%fused_computation.13 | convolution fusion | flops 4235329536 | bytes 22023168 | tf_op jit(solution)/shard_map/cond/branch_0_fun/dot_general | solution.py:461
  590.6 3.5 copy.20
  (6 shorter events, 0.1 us)
Async XLA Ops:
  78.5 112.3 %copy-start.3 = (s32[8,8,128]{2,1,0:T(8,128)S(1)}, s32[8,8,128]{2,1,0:T(8,128)}, u32[]{:S(2)}) copy-start(s32[8,8,128]{2,1,0:T(8,128)} %get-tuple-element.52) | copy-start | bytes 98308
  203.0 138.2 %copy-start.1 = (s32[8,384]{1,0:T(8,128)}, s32[8,384]{1,0:T(8,128)S(1)}, u32[]{:S(2)}) copy-start(s32[8,384]{1,0:T(8,128)S(1)} %get-tuple-element.37) | copy-start | bytes 36868 | tf_op jit(solution)/shard_map/cond
  203.5 137.7 %slice-start = ((s8[18350080]{0:T(1024)(128)(4,1)}), s8[4194304]{0:T(1024)(128)(4,1)S(1)}, s32[]{:S(2)}) async-start(s8[18350080]{0:T(1024)(128)(4,1)} %bitcast.29), calls=%async_computation.2 | async-start | bytes 8388608 | tf_op jit(solution)/shard_map/cond
  203.5 137.7 %slice-start.1 = ((s8[18350080]{0:T(1024)(128)(4,1)}), s8[4194304]{0:T(1024)(128)(4,1)S(1)}, s32[]{:S(2)}) async-start(s8[18350080]{0:T(1024)(128)(4,1)} %bitcast.29), calls=%async_computation.3 | async-start | bytes 8388608 | tf_op jit(solution)/shard_map/cond
  203.5 137.7 %slice-start.2 = ((s8[18350080]{0:T(1024)(128)(4,1)}), s8[4194304]{0:T(1024)(128)(4,1)S(1)}, s32[]{:S(2)}) async-start(s8[18350080]{0:T(1024)(128)(4,1)} %bitcast.29), calls=%async_computation.4 | async-start | bytes 8388608 | tf_op jit(solution)/shard_map/cond
  214.0 127.2 %slice-start.3 = ((s8[18350080]{0:T(1024)(128)(4,1)}), s8[4194304]{0:T(1024)(128)(4,1)S(1)}, s32[]{:S(2)}) async-start(s8[18350080]{0:T(1024)(128)(4,1)} %bitcast.29), calls=%async_computation.5 | async-start | bytes 8388608 | tf_op jit(solution)/shard_map/cond
  214.0 127.2 %slice-start.4 = ((s8[18350080]{0:T(1024)(128)(4,1)}), s8[1572864]{0:T(1024)(128)(4,1)S(1)}, s32[]{:S(2)}) async-start(s8[18350080]{0:T(1024)(128)(4,1)} %bitcast.29), calls=%async_computation.6 | async-start | bytes 3145728 | tf_op jit(solution)/shard_map/cond
  341.2 72.5 %slice-start.5 = ((s8[18350080]{0:T(1024)(128)(4,1)}), s8[4194304]{0:T(1024)(128)(4,1)S(1)}, s32[]{:S(2)}) async-start(s8[18350080]{0:T(1024)(128)(4,1)} %bitcast.33), calls=%async_computation.7 | async-start | bytes 8388608 | tf_op jit(solution)/shard_map/cond
  341.2 72.5 %slice-start.6 = ((s8[18350080]{0:T(1024)(128)(4,1)}), s8[4194304]{0:T(1024)(128)(4,1)S(1)}, s32[]{:S(2)}) async-start(s8[18350080]{0:T(1024)(128)(4,1)} %bitcast.33), calls=%async_computation.8 | async-start | bytes 8388608 | tf_op jit(solution)/shard_map/cond
  341.2 72.5 %slice-start.7 = ((s8[18350080]{0:T(1024)(128)(4,1)}), s8[1572864]{0:T(1024)(128)(4,1)S(1)}, s32[]{:S(2)}) async-start(s8[18350080]{0:T(1024)(128)(4,1)} %bitcast.33), calls=%async_computation.9 | async-start | bytes 3145728 | tf_op jit(solution)/shard_map/cond
  374.3 39.4 %slice-start.8 = ((s8[18350080]{0:T(1024)(128)(4,1)}), s8[4194304]{0:T(1024)(128)(4,1)S(1)}, s32[]{:S(2)}) async-start(s8[18350080]{0:T(1024)(128)(4,1)} %bitcast.33), calls=%async_computation.10 | async-start | bytes 8388608 | tf_op jit(solution)/shard_map/cond
  374.3 39.4 %slice-start.9 = ((s8[18350080]{0:T(1024)(128)(4,1)}), s8[4194304]{0:T(1024)(128)(4,1)S(1)}, s32[]{:S(2)}) async-start(s8[18350080]{0:T(1024)(128)(4,1)} %bitcast.33), calls=%async_computation.11 | async-start | bytes 8388608 | tf_op jit(solution)/shard_map/cond
  446.1 4.3 copy-start.4
  446.1 4.4 copy-start.5
  446.1 4.4 copy-start.2
  446.1 126.4 %all-to-all-start.1 = ((bf16[8,192,3584]{2,1,0:T(8,128)(2,1)}), bf16[8,192,3584]{2,1,0:T(8,128)(2,1)}, u32[]{:S(2)}, u32[]{:S(2)}) async-start(bf16[8,192,3584]{2,1,0:T(8,128)(2,1)} %bitcast.36), calls=%async_computation.1 | async-start | bytes 22020096 | tf_op jit(solution)/shard_map/cond/branch_0_fun/all_to_all | solution.py:455
  572.6 7.5 %copy-start = (bf16[384,3584]{1,0:T(8,128)(2,1)S(1)}, bf16[384,3584]{1,0:T(8,128)(2,1)}, u32[]{:S(2)}) copy-start(bf16[384,3584]{1,0:T(8,128)(2,1)} %get-tuple-element.34) | copy-start | bytes 8257540 | tf_op jit(solution)/shard_map/cond

commit v5 on v4

--- a/solution.py
+++ b/solution.py
@@ -186,7 +186,7 @@
 D = 128
 PIECES = 4
 CHUNKS = 4
-HOOKS = (6, 12)
+HOOKS = (2, 8, 13)
 
 
 def mate(r):
@@ -205,123 +205,115 @@
     return pltpu.make_async_remote_copy(src_ref=src, dst_ref=dst, send_sem=send, recv_sem=recv, device_id=dev, device_id_type=MESH)
 
 
-def qkv_kernel(cp, ne, x_ref, idx_ref, gate_ref, wq_ref, wk_ref, wv_ref, q_ref, kv_ref, all_ref, slot_ref, meta_ref,
-               cnt, xs, wqb, wkvb, cs, cr, xsnd, xrcv, fs, fr, bs, br, ks, kr, ws):
-    t = x_ref.shape[0]
-    step = t // PIECES
+def route(ne, cp, idx_ref, gate_ref, slot_ref, meta_ref, cnt):
+    t = idx_ref.shape[1]
+    lab = lax.broadcasted_iota(jnp.int32, (128, t), 0)
+    named = [idx_ref[i:i + 1, :] == lab for i in range(2)]
+    hit = (named[0] | named[1]).astype(jnp.float32)
+    before = (lax.broadcasted_iota(jnp.int32, (t, t), 0) < lax.broadcasted_iota(jnp.int32, (t, t), 1)).astype(jnp.bfloat16)
+    rank = jnp.dot(hit.astype(jnp.bfloat16), before, preferred_element_type=jnp.float32)
+    slot_ref[...] = jnp.where(hit > 0, rank, -1.0)[:ne].astype(jnp.int32)
+    cnt[...] = jnp.broadcast_to(jnp.sum(hit[:8], axis=1, keepdims=True), (8, 128)).astype(jnp.int32)
+    me = lax.axis_index('cp') * (ne // cp) + lax.axis_index('tp')
+    place = jnp.bitwise_xor(lab, me).astype(jnp.float32) * (2 * t // ne) + rank
+    meta = jnp.zeros((128, t), jnp.float32)
+    for i in range(2):
+        at = jnp.sum(jnp.where(named[i], place, 0.0), axis=0, keepdims=True)
+        meta = jnp.where(lab == i, at, jnp.where(lab == 2 + i, gate_ref[i:i + 1, :], meta))
+    meta_ref[...] = jnp.transpose(meta)
+
+
+def front_kernel(cp, ne, x_ref, idx_ref, gate_ref, wq_ref, wk_ref, wv_ref, wo_ref, h_ref, all_ref, slot_ref, meta_ref,
+                 cnt, xs, wqb, wkvb, q_ref, kv_ref, wof, ocat, st,
+                 cs, cr, as_, ar_, fs, fr, bs, br, ks, kr, ws, xs_, xr_, ys_, yr_, ds_, dr_, os_, or_, ls_, hs_):
+    t, hd = x_ref.shape
+    c = lax.axis_index('cp')
     loads = [pltpu.make_async_copy(wk_ref, wkvb.at[:, :D], ws.at[0]), pltpu.make_async_copy(wv_ref, wkvb.at[:, D:], ws.at[1]),
              pltpu.make_async_copy(wq_ref, wqb, ws.at[2])]
     for ld in loads:
         ld.start()
     greet(range(1, ne))
-    rows = lambda p: pl.ds(p * step, step)
-    across = [remote(x_ref.at[rows(p)], xs.at[1, rows(p)], xsnd.at[p], xrcv.at[p], device(2)) for p in range(PIECES)]
-    for a in across:
-        a.start()
+
+    step = t // PIECES
+    rows = lambda p: pl.ds(pl.multiple_of(p * step, 16), step)
+    across = lambda p: remote(x_ref.at[rows(p)], xs.at[1, rows(p)], as_.at[p], ar_.at[p], device(2))
+    onward = lambda p: remote(xs.at[1, rows(p)], xs.at[2, rows(p)], fs.at[p], fr.at[p], device(1))
     beside = remote(x_ref, xs.at[0], bs.at[0], br.at[0], device(1))
+    for p in range(2):
+        across(p).start()
     beside.start()
-    onward = [remote(xs.at[1, rows(p)], xs.at[2, rows(p)], fs.at[p], fr.at[p], device(1)) for p in range(PIECES)]
-    lane = lax.broadcasted_iota(jnp.int32, (t, 128), 1)
-    named = [idx_ref[:, i:i + 1] == lane for i in range(2)]
-    hit = (named[0] | named[1]).astype(jnp.float32)
-    before = (lax.broadcasted_iota(jnp.int32, (t, t), 1) < lax.broadcasted_iota(jnp.int32, (t, t), 0)).astype(jnp.bfloat16)
-    rank = jnp.dot(before, hit.astype(jnp.bfloat16), preferred_element_type=jnp.float32)
-    slot_ref[...] = jnp.transpose(jnp.where(hit > 0, rank, -1.0))[:ne].astype(jnp.int32)
-    cnt[...] = jnp.broadcast_to(jnp.sum(hit, axis=0, keepdims=True), (8, 128)).astype(jnp.int32)
-    me = lax.axis_index('cp') * (ne // cp) + lax.axis_index('tp')
-    place = jnp.bitwise_xor(lane, me).astype(jnp.float32) * (2 * t // ne) + rank
-    meta = jnp.zeros((t, 128), jnp.float32)
-    for i in range(2):
-        at = jnp.sum(jnp.where(named[i], place, 0.0), axis=1, keepdims=True)
-        meta = jnp.where(lane == i, at, jnp.where(lane == 2 + i, gate_ref[:, i:i + 1], meta))
-    meta_ref[...] = meta
+    route(ne, cp, idx_ref, gate_ref, slot_ref, meta_ref, cnt)
     all_ref[0] = cnt[...]
     counts = [remote(cnt, all_ref.at[r], cs.at[r], cr.at[r], device(r)) for r in range(1, ne)]
-    for ld in loads:
-        ld.wait()
-    sent = []
-
-    def project(block, r, off, n):
+
+    w = wo_ref.shape[0]
+    heads = w // D
+    half = w // 2
+    cut = half // CHUNKS
+    at = lambda base, j: pl.ds(pl.multiple_of(base + j * cut, 16), cut)
+    first, second = c * half, (1 - c) * half
+    mine = pltpu.make_async_copy(wo_ref, wof.at[:w], ls_.at[0])
+    xc = [remote(wo_ref.at[at(first, j)], wof.at[at(2 * w + first, j)], xs_.at[j], xr_.at[j], device(2)) for j in range(CHUNKS)]
+    yc = [remote(wof.at[at(2 * w + first, j)], wof.at[at(2 * w + first, j)], ys_.at[j], yr_.at[j], device(4)) for j in range(CHUNKS)]
+    dx = [remote(wof.at[at(2 * w + first, j)], wof.at[at(3 * w + first, j)], ds_.at[j], dr_.at[j], device(1)) for j in range(CHUNKS)]
+    dy = [remote(wof.at[at(2 * w + second, j)], wof.at[at(3 * w + second, j)], ds_.at[CHUNKS + j], dr_.at[CHUNKS + j], device(1)) for j in range(CHUNKS)]
+    whole = remote(wo_ref, wof.at[pl.ds(w, w)], ds_.at[2 * CHUNKS], dr_.at[2 * CHUNKS], device(1))
+
+    def relay_x(j):
+        xc[j].wait_recv()
+        yc[j].start()
+        dx[j].start()
+
+    def relay_y(j):
+        yc[j].wait_recv()
+        dy[j].start()
+
+    def pair(i, base, n):
+        return remote(kv_ref.at[pl.ds(base, n)], kv_ref.at[pl.ds(base, n)], ks.at[i], kr.at[i], device(4))
+
+    def project(block, r, off, n, i):
         tt = mate(r)
         base = pl.multiple_of(segment(tt, cp) * (2 * t) + lax.rem(tt, 2) * t + off, 16)
         kv_ref[pl.ds(base, n), :] = jnp.dot(block, wkvb[...], preferred_element_type=jnp.float32).astype(jnp.bfloat16)
         qb = pl.multiple_of(tt * t + off, 16)
         q_ref[pl.ds(qb, n), :] = jnp.dot(block, wqb[...], preferred_element_type=jnp.float32).astype(jnp.bfloat16)
-        i = len(sent)
-        out = remote(kv_ref.at[pl.ds(base, n)], kv_ref.at[pl.ds(base, n)], ks.at[i], kr.at[i], device(4))
-        out.start()
-        sent.append(out)
-
-    project(x_ref[...], 0, 0, t)
+        pair(i, base, n).start()
+
     for cc in counts:
         cc.start()
+    for p in range(2, PIECES):
+        across(p).start()
+    for ld in loads:
+        ld.wait()
+    project(x_ref[...], 0, 0, t, 0)
     beside.wait_recv()
-    project(xs[0], 1, 0, t)
+    project(xs[0], 1, 0, t, 1)
+
+    def land(p, _):
+        across(p).wait_recv()
+        onward(p).start()
+
+        @pl.when(p == 2)
+        def _():
+            for cpy in xc:
+                cpy.start()
+        project(xs[1, rows(p)], 2, p * step, step, 2 + 2 * p)
+        onward(p).wait_recv()
+        project(xs[2, rows(p)], 3, p * step, step, 3 + 2 * p)
+        return 0
+    lax.fori_loop(0, PIECES, land, 0)
+    mine.start()
+    whole.start()
+    for i in range(2):
+        pair(i, 0, t).wait_recv()
+    for i in range(2, 2 + 2 * PIECES):
+        pair(i, 0, step).wait_recv()
     for p in range(PIECES):
-        across[p].wait_recv()
-        onward[p].start()
-        project(xs[1, p * step:(p + 1) * step], 2, p * step, step)
-        onward[p].wait_recv()
-        project(xs[2, p * step:(p + 1) * step], 3, p * step, step)
-    for o in sent:
-        o.wait_recv()
-    for cc in counts:
-        cc.wait_recv()
-    for o in counts + across + [beside] + onward + sent:
-        o.wait_send()
-
-
-def qkv(x, idx, gates, wq, wk, wv, cp, ne, cid):
-    t, hd = x.shape
-    tp = ne // cp
-    vm = pl.BlockSpec(memory_space=pltpu.VMEM)
-    hb = pl.BlockSpec(memory_space=pl.ANY)
-    bf = jnp.bfloat16
-    dma = pltpu.SemaphoreType.DMA
-    nk = 2 + 2 * PIECES
-    return pl.pallas_call(
-        functools.partial(qkv_kernel, cp, ne),
-        in_specs=[vm, vm, vm, hb, hb, hb], out_specs=[vm] * 5,
-        out_shape=[jax.ShapeDtypeStruct((tp * t, wq.shape[1]), bf), jax.ShapeDtypeStruct((ne * t, 2 * D), bf), jax.ShapeDtypeStruct((ne, 8, 128), jnp.int32), jax.ShapeDtypeStruct((ne, t), jnp.int32), jax.ShapeDtypeStruct((t, 128), jnp.float32)],
-        scratch_shapes=[pltpu.VMEM((8, 128), jnp.int32), pltpu.VMEM((3, t, hd), bf), pltpu.VMEM(wq.shape, bf), pltpu.VMEM((hd, 2 * D), bf),
-                        dma((ne,)), dma((ne,)), dma((PIECES,)), dma((PIECES,)), dma((PIECES,)), dma((PIECES,)), dma((1,)), dma((1,)), dma((nk,)), dma((nk,)), dma((3,))],
-        compiler_params=pltpu.CompilerParams(collective_id=cid, has_side_effects=True, vmem_limit_bytes=60 * 1024 * 1024),
-        name='qkv')(x, idx, gates, wq, wk, wv)
-
-
-def attn_kernel(cp, q_ref, kv_ref, x_ref, wo_ref, h_ref, wof, ocat, obuf, m_ref, l_ref, acc_ref, part,
-                xs_, xr_, ys_, yr_, ds_, dr_, os_, or_, ls_):
-    t, hd = x_ref.shape
-    w = wo_ref.shape[0]
-    heads = w // D
-    half = w // 2
-    step = half // CHUNKS
-    c = lax.axis_index('cp')
-    mine = pltpu.make_async_copy(wo_ref, wof.at[:w], ls_.at[0])
-    mine.start()
-    greet((1, 2, 3, 4))
-    at = lambda base, j: pl.ds(pl.multiple_of(base + j * step, 16), step)
-    first, second = c * half, (1 - c) * half
-    xc = [remote(wo_ref.at[at(first, j)], wof.at[at(2 * w + first, j)], xs_.at[j], xr_.at[j], device(2)) for j in range(CHUNKS)]
-    yc = [remote(wof.at[at(2 * w + first, j)], wof.at[at(2 * w + first, j)], ys_.at[j], yr_.at[j], device(4)) for j in range(CHUNKS)]
-    dx = [remote(wof.at[at(2 * w + first, j)], wof.at[at(3 * w + first, j)], ds_.at[j], dr_.at[j], device(1)) for j in range(CHUNKS)]
-    dy = [remote(wof.at[at(2 * w + second, j)], wof.at[at(3 * w + second, j)], ds_.at[CHUNKS + j], dr_.at[CHUNKS + j], device(1)) for j in range(CHUNKS)]
-    whole = remote(wo_ref, wof.at[pl.ds(w, w)], ds_.at[2 * CHUNKS], dr_.at[2 * CHUNKS], device(1))
-    for cpy in xc:
-        cpy.start()
-    whole.start()
-
-    def relay_x(j):
-        xc[j].wait_recv()
-        yc[j].start()
-        dx[j].start()
-
-    def relay_y(j):
-        yc[j].wait_recv()
-        dy[j].start()
+        onward(p).wait_send()
 
     scale = D ** -0.5 * math.log2(math.e)
     mask = lax.broadcasted_iota(jnp.int32, (t, t), 1) <= lax.broadcasted_iota(jnp.int32, (t, t), 0)
+    M, L, A = 0, heads, 2 * heads
 
     def lanes(p):
         s = p[:, :128]
@@ -334,7 +326,8 @@
 
     def give(b):
         r = which(b)
-        return remote(obuf.at[r], ocat.at[:, pl.ds(pl.multiple_of(r * w, 128), w)], os_.at[r], or_.at[r], (lax.axis_index('dp'), c, mate(r)))
+        cols = pl.ds(pl.multiple_of(r * w, 128), w)
+        return remote(xs.at[2, :, cols], ocat.at[:, cols], os_.at[r], or_.at[r], (lax.axis_index('dp'), c, mate(r)))
 
     def block(b, u):
         r = which(b)
@@ -355,9 +348,9 @@
             s = jnp.where(mask, scores(h, nfull), -1e30)
             m = jnp.max(s, axis=1, keepdims=True)
             p = jnp.where(mask, jnp.exp2(s - m), 0.0)
-            m_ref[h] = jnp.broadcast_to(m, (t, 128))
-            l_ref[h] = lanes(p)
-            acc_ref[h] = pv(p, nfull)
+            st[M + h] = jnp.broadcast_to(m, (t, 128))
+            st[L + h] = lanes(p)
+            st[A + h] = pv(p, nfull)
 
         @pl.when(b > 0)
         def _():
@@ -370,71 +363,100 @@
                     relay_x(n)
             for h in range(heads):
                 s = scores(h, j)
-                mo = m_ref[h]
+                mo = st[M + h]
                 mn = jnp.maximum(mo, jnp.max(s, axis=1, keepdims=True))
                 p = jnp.exp2(s - jnp.concatenate([mn] * (t // 128), axis=1))
                 al = jnp.exp2(mo - mn)
-                m_ref[h] = mn
-                l_ref[h] = l_ref[h] * al + lanes(p)
-                acc_ref[h] = acc_ref[h] * al + pv(p, j)
+                st[M + h] = mn
+                st[L + h] = st[L + h] * al + lanes(p)
+                st[A + h] = st[A + h] * al + pv(p, j)
             return 0
 
         lax.fori_loop(0, nfull, body, 0)
         for h in range(heads):
-            l = jnp.sum(l_ref[h], axis=1, keepdims=True)
-            obuf[r, :, h * D:(h + 1) * D] = (acc_ref[h] / l).astype(jnp.bfloat16)
+            l = jnp.sum(st[L + h], axis=1, keepdims=True)
+            xs[2, :, pl.ds(pl.multiple_of(r * w + h * D, 128), D)] = (st[A + h] / l).astype(jnp.bfloat16)
         return u + nfull
 
-    units = lax.fori_loop(0, 4, block, 0)
-    ocat[:, :w] = obuf[0]
+    lax.fori_loop(0, 4, block, 0)
+    ocat[:, :w] = xs[2, :, :w]
+
+    tile = lambda n: pl.ds(pl.multiple_of(n * NT, NT), NT)
+    per = NT // 128
+
+    def held(n):
+        return jnp.concatenate([st[n * per + i] for i in range(per)], axis=1)
+
+    def add(lo, hi, fresh):
+        def one(n, _):
+            s = jnp.dot(ocat[:, lo * w:hi * w], wof[lo * w:hi * w, tile(n)], preferred_element_type=jnp.float32)
+            if not fresh:
+                s = s + held(n)
+            for i in range(per):
+                st[n * per + i] = s[:, i * 128:(i + 1) * 128]
+            return 0
+        lax.fori_loop(0, hd // NT, one, 0)
+
     mine.wait()
     whole.wait_recv()
     give(2).wait_recv()
-
-    def near(n, _):
-        cols = pl.ds(pl.multiple_of(n * NT, NT), NT)
-        part[:, cols] = jnp.dot(ocat[:, :2 * w], wof[:2 * w, cols], preferred_element_type=jnp.float32)
-        return 0
-    lax.fori_loop(0, hd // NT, near, 0)
-    relay_x(2)
+    add(0, 2, True)
     relay_y(0)
-    relay_x(3)
-    relay_y(1)
-    relay_y(2)
-    relay_y(3)
+    for j in range(len(HOOKS), CHUNKS):
+        relay_x(j)
+    for j in range(1, CHUNKS):
+        relay_y(j)
     for j in range(CHUNKS):
         dx[j].wait_recv()
         dy[j].wait_recv()
     give(0).wait_recv()
+    add(2, 3, False)
     give(1).wait_recv()
-
-    def far(n, _):
-        cols = pl.ds(pl.multiple_of(n * NT, NT), NT)
-        s = part[:, cols] + jnp.dot(ocat[:, 2 * w:], wof[2 * w:, cols], preferred_element_type=jnp.float32)
-        h_ref[:, cols] = (x_ref[:, cols].astype(jnp.float32) + s).astype(jnp.bfloat16)
+    out = lambda n: pltpu.make_async_copy(xs.at[0, :, tile(n)], h_ref.at[:, tile(n)], hs_.at[0])
+
+    def last(n, _):
+        s = held(n) + jnp.dot(ocat[:, 3 * w:], wof[3 * w:, tile(n)], preferred_element_type=jnp.float32)
+        xs[0, :, tile(n)] = (x_ref[:, tile(n)].astype(jnp.float32) + s).astype(jnp.bfloat16)
+
+        @pl.when(n > 0)
+        def _():
+            out(n - 1).start()
         return 0
-    lax.fori_loop(0, hd // NT, far, 0)
-    for cpy in xc + yc + dx + dy + [whole, give(0), give(1), give(2)]:
+    lax.fori_loop(0, hd // NT, last, 0)
+    out(hd // NT - 1).start()
+    for cc in counts:
+        cc.wait_recv()
+    for p in range(PIECES):
+        across(p).wait_send()
+    for i in range(2):
+        pair(i, 0, t).wait_send()
+    for i in range(2, 2 + 2 * PIECES):
+        pair(i, 0, step).wait_send()
+    for cpy in counts + [beside] + xc + yc + dx + dy + [whole, give(0), give(1), give(2)]:
         cpy.wait_send()
-
-
-def attention(q, kv, x, wo, cp, cid):
+    pltpu.make_async_copy(xs.at[0], h_ref, hs_.at[0]).wait()
+
+
+def front(x, idx, gates, wq, wk, wv, wo, cp, ne, cid):
     t, hd = x.shape
+    tp = ne // cp
     w = wo.shape[0]
-    heads = w // D
     vm = pl.BlockSpec(memory_space=pltpu.VMEM)
     hb = pl.BlockSpec(memory_space=pl.ANY)
     bf = jnp.bfloat16
-    dma = pltpu.SemaphoreType.DMA
-    state = pltpu.VMEM((heads, t, 128), jnp.float32)
+    dma = lambda n: pltpu.SemaphoreType.DMA((n,))
+    nk = 2 + 2 * PIECES
+    nd = 2 * CHUNKS + 1
     return pl.pallas_call(
-        functools.partial(attn_kernel, cp),
-        in_specs=[vm, vm, vm, hb], out_specs=vm,
-        out_shape=jax.ShapeDtypeStruct((t, hd), bf),
-        scratch_shapes=[pltpu.VMEM((4 * w, hd), bf), pltpu.VMEM((t, 4 * w), bf), pltpu.VMEM((4, t, w), bf), state, state, state, pltpu.VMEM((t, hd), jnp.float32),
-                        dma((CHUNKS,)), dma((CHUNKS,)), dma((CHUNKS,)), dma((CHUNKS,)), dma((2 * CHUNKS + 1,)), dma((2 * CHUNKS + 1,)), dma((4,)), dma((4,)), dma((1,))],
-        compiler_params=pltpu.CompilerParams(collective_id=cid, has_side_effects=True, vmem_limit_bytes=63 * 1024 * 1024),
-        name='attn')(q, kv, x, wo)
+        functools.partial(front_kernel, cp, ne),
+        in_specs=[vm, vm, vm, hb, hb, hb, hb], out_specs=[hb, vm, vm, vm],
+        out_shape=[jax.ShapeDtypeStruct((t, hd), bf), jax.ShapeDtypeStruct((ne, 8, 128), jnp.int32), jax.ShapeDtypeStruct((ne, t), jnp.int32), jax.ShapeDtypeStruct((t, 128), jnp.float32)],
+        scratch_shapes=[pltpu.VMEM((8, 128), jnp.int32), pltpu.VMEM((3, t, hd), bf), pltpu.VMEM(wq.shape, bf), pltpu.VMEM((hd, 2 * D), bf),
+                        pltpu.VMEM((tp * t, w), bf), pltpu.VMEM((ne * t, 2 * D), bf), pltpu.VMEM((tp * w, hd), bf), pltpu.VMEM((t, tp * w), bf), pltpu.VMEM((hd // 128, t, 128), jnp.float32),
+                        dma(ne), dma(ne), dma(PIECES), dma(PIECES), dma(PIECES), dma(PIECES), dma(1), dma(1), dma(nk), dma(nk), dma(3),
+                        dma(CHUNKS), dma(CHUNKS), dma(CHUNKS), dma(CHUNKS), dma(nd), dma(nd), dma(4), dma(4), dma(1), dma(1)],
+        compiler_params=pltpu.CompilerParams(collective_id=cid, has_side_effects=True, vmem_limit_bytes=67043328),
+        name='front')(x, idx.T, gates.T, wq, wk, wv, wo)
 
 
 def expert_ffn(rows, wg, wu, wd):
@@ -471,8 +493,7 @@
 
     def local(x, idx, gates, wq, wk, wv, wo, w1g, w1u, w2):
         t, hd = x.shape
-        q, kv, counts, slot, meta = qkv(x, idx, gates, wq, wk, wv, cp, ne, 1)
-        h = attention(q, kv, x, wo, cp, 2)
+        h, counts, slot, meta = front(x, idx, gates, wq, wk, wv, wo, cp, ne, 1)
         worst = jnp.max(counts)
 
         def tight(h):

time: 603 us -> 571 us (0.947)
  Pallas kernels: 188 us -> 171 us
  loops' own time: 11.3 us -> 0.4 us
    pallas_call x2 -> x1, Pallas kernels: 188 us -> 171 us  [front(): pl.pallas_call(functools.partial(front_kernel, cp, ne), in_specs=[vm, vm,...]
    another operation x1, loops' own time: 11.3 us -> 0.4 us  [local(): return lax.cond(worst <= t // 4, tight, roomy, h)]
where the time goes in v5:
time: 571 us; the launch traced here: 566 us
  Pallas kernels  171 us (30%)
  matrix products  133 us (23%)
  blocking collectives  128 us (22%)
  waiting for transfers between devices  122 us (21%)
    pallas_call x1, Pallas kernels, front(): pl.pallas_call(functools.partial(front_kernel, cp, ne), in_specs=[vm, vm,...  171 us
    all_to_all x1, blocking collectives, moe_any(): lax.all_to_all(send.reshape(ne, cap, hd), ('cp', 'tp'), 0, 0, tiled=True)  128 us
    all_to_all x1, waiting for transfers between devices, moe_any(): lax.all_to_all(z.reshape(ne, cap, hd), ('cp', 'tp'), 0, 0, tiled=True)  122 us
    dot_general x1, matrix products, expert_ffn(): uu = jnp.dot(rows, wu, preferred_element_type=jnp.float32)  39.4 us
    dot_general x1, matrix products, expert_ffn(): gg = jnp.dot(rows, wg, preferred_element_type=jnp.float32)  33.1 us
    dot_general x1, matrix products, expert_ffn(): jnp.dot(act, wd, preferred_element_type=jnp.float32).astype(jnp.bfloat16)  32.4 us
    dot_general x2, matrix products, moe_any(): jnp.dot(sel, back, preferred_element_type=jnp.float32)  17.8 us
  transfers between devices with their start and end apart: 1, of which 1 were waited for; matrix products, arithmetic and copies ran while one was open for 0% of the time, Pallas kernels for 0%

profile of v5, /device:TPU:0, one launch (start us, length us, event | category | flops | bytes accessed | tf_op | source)
XLA Modules:
  0.0 565.8 jit_solution(6250870544263534614)
XLA Ops:
  0.0 171.3 %front.1 = (bf16[384,3584]{1,0:T(8,128)(2,1)}, s32[8,8,128]{2,1,0:T(8,128)}, s32[8,384]{1,0:T(8,128)}, f32[384,128]{1,0:T(8,128)}) custom-call(bf16[384,3584]{1,0:T(8,128)(2,1)} %x_ref.1, s32[2,384]{1,0:T(2,128)} %bitcast.42, f32[2,384]{1,0:T(2,128)} %bitcast.43, bf16[3584,896]{1,0:T(8,128)(2,1)} %wq_ref.1, bf16[3584,128]{1,0:T(8,128)(2,1)} %wk_ref.1, ...), custom_call_target="tpu_custom_call" | custom-call | tf_op jit(solution)/shard_map/front/pallas_call | solution.py:450
  171.3 1.4 reduce_max.9
  173.3 388.7 %conditional.1 = (bf16[384,3584]{1,0:T(8,128)(2,1)}) conditional(s32[]{:T(128)} %convert_element_type.21, (bf16[384,3584]{1,0:T(8,128)(2,1)}, f32[384,2]{0,1:T(2,128)}, s32[384,2]{0,1:T(2,128)}, s32[8,384]{1,0:T(8,128)}, bf16[1,3584,2560]{2,1,0:T(8,128)(2,1)}, /*index=5*/bf16[1,3584,2560]{2,1,0:T(8,128)(2,1)}, ...), branch_computations={%region_1.4_spmd, %region_4.5_spmd} | conditional | flops 97285398528 | bytes 365052416 | solution.py:505
  173.4 0.1 eq.16
  173.4 1.1 bitcast_compare_fusion
  174.5 0.0 slice-start
  174.5 0.0 slice-start.1
  174.5 0.0 slice-start.2
  174.6 10.5 %convolution_convert_fusion = bf16[1536,3584]{1,0:T(8,128)(2,1)} fusion(pred[1536,384]{1,0:T(32,128)(4,1)S(1)} %bitcast_compare_fusion, bf16[384,3584]{1,0:T(8,128)(2,1)} %get-tuple-element.34), kind=kOutput, calls=%fused_computation.8 | convolution fusion | flops 4233363456 | bytes 14352384 | tf_op jit(solution)/shard_map/cond/branch_0_fun/dot_general | solution.py:474
  185.0 0.0 slice-start.3
  185.0 0.0 slice-start.4
  185.0 127.7 %all_to_all.8 = bf16[8,192,3584]{2,1,0:T(8,128)(2,1)} all-to-all(bf16[8,192,3584]{2,1,0:T(8,128)(2,1)} %bitcast.41), channel_id=1, replica_groups=mesh['dp'=1,'cp'=2,'tp'=4] {'cp','tp'}, dimensions={0} | all-to-all | bytes 22020096 | tf_op jit(solution)/shard_map/cond/branch_0_fun/all_to_all | solution.py:475
  312.7 0.0 slice-done
  312.7 0.0 slice-done.1
  312.7 0.0 slice-done.2
  312.7 0.0 slice-done.3
  312.8 0.0 slice-done.4
  312.8 0.0 slice-start.5
  312.8 0.0 slice-start.6
  312.8 0.0 slice-start.7
  312.8 33.1 %fusion.4 = f32[1536,2560]{1,0:T(8,128)} fusion(bf16[1536,3584]{1,0:T(8,128)(2,1)} %bitcast.39, bf16[1,3584,2560]{2,1,0:T(8,128)(2,1)S(1)} %bitcast.32), kind=kOutput, calls=%fused_computation.4 | convolution fusion | flops 28185722880 | bytes 45088768 | tf_op jit(solution)/shard_map/cond/branch_0_fun/dot_general | solution.py:463
  345.9 0.0 slice-start.8
  345.9 0.0 slice-start.9
  345.9 39.4 %multiply_convert_fusion = bf16[1536,2560]{1,0:T(8,128)(2,1)} fusion(f32[1536,2560]{1,0:T(8,128)} %fusion.4, bf16[1536,3584]{1,0:T(8,128)(2,1)} %bitcast.40, bf16[1,3584,2560]{2,1,0:T(8,128)(2,1)} %get-tuple-element.39), kind=kOutput, calls=%fused_computation.6 | convolution fusion | flops 28209315840 | bytes 52953088 | tf_op jit(solution)/shard_map/cond/branch_0_fun/dot_general | solution.py:464
  385.3 0.0 slice-done.5
  385.3 0.0 slice-done.6
  385.3 0.0 slice-done.7
  385.3 0.0 slice-done.8
  385.3 0.0 slice-done.9
  385.3 32.4 %fusion.6 = bf16[1536,3584]{1,0:T(8,128)(2,1)} fusion(bf16[1536,2560]{1,0:T(8,128)(2,1)} %multiply_convert_fusion, bf16[1,2560,3584]{2,1,0:T(8,128)(2,1)S(1)} %bitcast.36), kind=kOutput, calls=%fused_computation.7 | convolution fusion | flops 28191227904 | bytes 37224448 | tf_op jit(solution)/shard_map/cond/branch_0_fun/dot_general | solution.py:466
  417.7 0.0 copy-start.2
  417.7 0.0 copy-start.3
  417.7 0.0 copy-start.1
  417.7 4.3 all-to-all-start.1
  422.0 0.0 copy-done.2
  422.0 0.0 copy-done.3
  422.0 0.0 copy-done.1
  422.0 0.1 select_reduce_fusion.1
  422.1 121.9 %all-to-all-done.1 = bf16[8,192,3584]{2,1,0:T(8,128)(2,1)} async-done(((bf16[8,192,3584]{2,1,0:T(8,128)(2,1)}), bf16[8,192,3584]{2,1,0:T(8,128)(2,1)}, u32[]{:S(2)}, u32[]{:S(2)}) %all-to-all-start.1) | async-done | bytes 11010080 | tf_op jit(solution)/shard_map/cond/branch_0_fun/all_to_all | solution.py:477
  544.1 0.0 copy-start
  544.1 7.5 %convolution_multiply_fusion = f32[384,3584]{1,0:T(8,128)S(1)} fusion(bf16[1536,3584]{1,0:T(8,128)(2,1)} %bitcast.7, f32[384]{0:T(512)S(1)} %get-tuple-element.61, s32[384]{0:T(512)S(1)} %get-tuple-element.57), kind=kOutput, calls=%fused_computation.9 | convolution fusion | flops 4229824512 | bytes 16518144 | tf_op jit(solution)/shard_map/cond/branch_0_fun/dot_general | solution.py:483
  551.6 0.0 copy-done
  551.6 10.2 %fusion.13 = bf16[384,3584]{1,0:T(8,128)(2,1)} fusion(f32[384,3584]{1,0:T(8,128)S(1)} %convolution_multiply_fusion, bf16[1536,3584]{1,0:T(8,128)(2,1)} %bitcast.7, bf16[384,3584]{1,0:T(8,128)(2,1)S(1)} %copy-done, f32[384]{0:T(512)S(1)} %get-tuple-element.60, s32[384]{0:T(512)S(1)} %get-tuple-element.56), kind=kOutput, calls=%fused_computation.13 | convolution fusion | flops 4235329536 | bytes 22023168 | tf_op jit(solution)/shard_map/cond/branch_0_fun/dot_general | solution.py:483
  562.1 3.5 copy.18
  (6 shorter events, 0.1 us)
Async XLA Ops:
  174.5 138.2 %slice-start = ((s8[18350080]{0:T(1024)(128)(4,1)}), s8[4194304]{0:T(1024)(128)(4,1)S(1)}, s32[]{:S(2)}) async-start(s8[18350080]{0:T(1024)(128)(4,1)} %bitcast.31), calls=%async_computation.2 | async-start | bytes 8388608 | tf_op jit(solution)/shard_map/cond
  174.5 138.2 %slice-start.1 = ((s8[18350080]{0:T(1024)(128)(4,1)}), s8[4194304]{0:T(1024)(128)(4,1)S(1)}, s32[]{:S(2)}) async-start(s8[18350080]{0:T(1024)(128)(4,1)} %bitcast.31), calls=%async_computation.3 | async-start | bytes 8388608 | tf_op jit(solution)/shard_map/cond
  174.5 138.2 %slice-start.2 = ((s8[18350080]{0:T(1024)(128)(4,1)}), s8[4194304]{0:T(1024)(128)(4,1)S(1)}, s32[]{:S(2)}) async-start(s8[18350080]{0:T(1024)(128)(4,1)} %bitcast.31), calls=%async_computation.4 | async-start | bytes 8388608 | tf_op jit(solution)/shard_map/cond
  185.0 127.7 %slice-start.3 = ((s8[18350080]{0:T(1024)(128)(4,1)}), s8[4194304]{0:T(1024)(128)(4,1)S(1)}, s32[]{:S(2)}) async-start(s8[18350080]{0:T(1024)(128)(4,1)} %bitcast.31), calls=%async_computation.5 | async-start | bytes 8388608 | tf_op jit(solution)/shard_map/cond
  185.0 127.7 %slice-start.4 = ((s8[18350080]{0:T(1024)(128)(4,1)}), s8[1572864]{0:T(1024)(128)(4,1)S(1)}, s32[]{:S(2)}) async-start(s8[18350080]{0:T(1024)(128)(4,1)} %bitcast.31), calls=%async_computation.6 | async-start | bytes 3145728 | tf_op jit(solution)/shard_map/cond
  312.8 72.5 %slice-start.5 = ((s8[18350080]{0:T(1024)(128)(4,1)}), s8[4194304]{0:T(1024)(128)(4,1)S(1)}, s32[]{:S(2)}) async-start(s8[18350080]{0:T(1024)(128)(4,1)} %bitcast.35), calls=%async_computation.7 | async-start | bytes 8388608 | tf_op jit(solution)/shard_map/cond
  312.8 72.5 %slice-start.6 = ((s8[18350080]{0:T(1024)(128)(4,1)}), s8[4194304]{0:T(1024)(128)(4,1)S(1)}, s32[]{:S(2)}) async-start(s8[18350080]{0:T(1024)(128)(4,1)} %bitcast.35), calls=%async_computation.8 | async-start | bytes 8388608 | tf_op jit(solution)/shard_map/cond
  312.8 72.5 %slice-start.7 = ((s8[18350080]{0:T(1024)(128)(4,1)}), s8[1572864]{0:T(1024)(128)(4,1)S(1)}, s32[]{:S(2)}) async-start(s8[18350080]{0:T(1024)(128)(4,1)} %bitcast.35), calls=%async_computation.9 | async-start | bytes 3145728 | tf_op jit(solution)/shard_map/cond
  345.9 39.4 %slice-start.8 = ((s8[18350080]{0:T(1024)(128)(4,1)}), s8[4194304]{0:T(1024)(128)(4,1)S(1)}, s32[]{:S(2)}) async-start(s8[18350080]{0:T(1024)(128)(4,1)} %bitcast.35), calls=%async_computation.10 | async-start | bytes 8388608 | tf_op jit(solution)/shard_map/cond
  345.9 39.4 %slice-start.9 = ((s8[18350080]{0:T(1024)(128)(4,1)}), s8[4194304]{0:T(1024)(128)(4,1)S(1)}, s32[]{:S(2)}) async-start(s8[18350080]{0:T(1024)(128)(4,1)} %bitcast.35), calls=%async_computation.11 | async-start | bytes 8388608 | tf_op jit(solution)/shard_map/cond
  417.7 4.3 copy-start.2
  417.7 4.3 copy-start.3
  417.7 4.3 copy-start.1
  417.7 126.4 %all-to-all-start.1 = ((bf16[8,192,3584]{2,1,0:T(8,128)(2,1)}), bf16[8,192,3584]{2,1,0:T(8,128)(2,1)}, u32[]{:S(2)}, u32[]{:S(2)}) async-start(bf16[8,192,3584]{2,1,0:T(8,128)(2,1)} %bitcast.38), calls=%async_computation.1 | async-start | bytes 22020096 | tf_op jit(solution)/shard_map/cond/branch_0_fun/all_to_all | solution.py:477
  544.1 7.5 %copy-start = (bf16[384,3584]{1,0:T(8,128)(2,1)S(1)}, bf16[384,3584]{1,0:T(8,128)(2,1)}, u32[]{:S(2)}) copy-start(bf16[384,3584]{1,0:T(8,128)(2,1)} %get-tuple-element.34) | copy-start | bytes 8257540 | tf_op jit(solution)/shard_map/cond

commit v6 on v5

--- a/solution.py
+++ b/solution.py
@@ -40,9 +40,12 @@
     pl.semaphore_wait(pltpu.get_barrier_semaphore(), len(peers))
 
 
-def moe_kernel(ne, cap, h_ref, slot_ref, meta_ref, w1g_ref, w1u_ref, w2_ref, y_ref,
-               send, recv, act, zsend, zrecv, sel, pick, w1b, w2b, ds, dr, zs, zr, zf, w1s, w2s):
+def moe_kernel(ne, cap, hin_ref, slot_ref, meta_ref, w1g_ref, w1u_ref, w2_ref, yout_ref,
+               h_ref, y_ref, send, recv, act, zsend, zrecv, sel, pick, w1b, w2b, ds, dr, zs, zr, zf, w1s, w2s, hs, ys):
     t, hd = h_ref.shape
+    hload = pltpu.make_async_copy(hin_ref, h_ref, hs.at[0])
+    hload.start()
+    hail(range(1, ne))
     ff = w2_ref.shape[0]
     nf, nz = ff // FT, hd // NT
 
@@ -59,7 +62,6 @@
     for s in range(2):
         w2_copy(s, s).start()
 
-    hail(range(1, ne))
     tile = lambda n: pl.ds(pl.multiple_of(n * NT, NT), NT)
 
     def out_copy(r, cols=slice(None)):
@@ -69,6 +71,7 @@
         c, tt = peer(r)
         row = slot_ref[pl.ds(c * (ne // 2) + tt, 1), :]
         sel[r * cap:(r + 1) * cap, :] = (jnp.broadcast_to(row, (cap, t)) == lax.broadcasted_iota(jnp.int32, (cap, t), 0)).astype(jnp.bfloat16)
+    hload.wait()
     pl.semaphore_wait(pltpu.get_barrier_semaphore(), ne - 1)
 
     def dispatch(lo, hi, order):
@@ -157,11 +160,18 @@
         zt = jnp.dot(pick[...], zrecv[:, :, cols].reshape(ne * cap, NT), preferred_element_type=jnp.float32)
         y = h_ref[:, cols].astype(jnp.float32) + (meta_ref[:, 2:3] * zt[:t] + meta_ref[:, 3:4] * zt[t:])
         y_ref[:, cols] = y.astype(jnp.bfloat16)
+
+        @pl.when(n > 0)
+        def _():
+            leave(n - 1).start()
         return 0
+    leave = lambda n: pltpu.make_async_copy(y_ref.at[:, tile(n)], yout_ref.at[:, tile(n)], ys.at[0])
     lax.fori_loop(0, nz, combine, 0)
+    leave(nz - 1).start()
     for r in range(1, ne):
         out_copy(r).wait_send()
         whole(r).wait_send()
+    pltpu.make_async_copy(y_ref, yout_ref, ys.at[0]).wait()
 
 
 def moe_fast(h, slot, meta, w1g, w1u, w2, cap, cid):
@@ -173,14 +183,35 @@
     ff = w2.shape[0]
     return pl.pallas_call(
         functools.partial(moe_kernel, ne, cap),
-        in_specs=[vm, vm, vm, hb, hb, hb], out_specs=vm,
+        in_specs=[hb, vm, vm, hb, hb, hb], out_specs=hb,
         out_shape=jax.ShapeDtypeStruct((t, hd), bf),
-        scratch_shapes=[pltpu.VMEM((ne, cap, hd), bf), pltpu.VMEM((ne, cap, hd), bf), pltpu.VMEM((NEAR * cap, ff), bf),
+        scratch_shapes=[pltpu.VMEM((t, hd), bf), pltpu.VMEM((t, hd), bf), pltpu.VMEM((ne, cap, hd), bf), pltpu.VMEM((ne, cap, hd), bf), pltpu.VMEM((NEAR * cap, ff), bf),
                         pltpu.VMEM((ne, cap, hd), bf), pltpu.VMEM((ne, cap, hd), bf), pltpu.VMEM((ne * cap, t), bf), pltpu.VMEM((2 * t, ne * cap), bf),
                         pltpu.VMEM((2, 2, hd, FT), bf), pltpu.VMEM((2, ff, NT), bf)]
-                       + [pltpu.SemaphoreType.DMA((ne,))] * 4 + [pltpu.SemaphoreType.DMA((ne - NEAR, hd // NT))] + [pltpu.SemaphoreType.DMA((2, 2)), pltpu.SemaphoreType.DMA((2,))],
+                       + [pltpu.SemaphoreType.DMA((ne,))] * 4 + [pltpu.SemaphoreType.DMA((ne - NEAR, hd // NT))] + [pltpu.SemaphoreType.DMA((2, 2)), pltpu.SemaphoreType.DMA((2,)), pltpu.SemaphoreType.DMA((1,)), pltpu.SemaphoreType.DMA((1,))],
         compiler_params=pltpu.CompilerParams(collective_id=cid, has_side_effects=True, vmem_limit_bytes=63 * 1024 * 1024),
         name='moe')(h, slot, meta, w1g, w1u, w2)
+
+
+def settle_kernel(parts, a_ref, b_ref, buf, ins, outs):
+    n = a_ref.shape[0] // parts
+    rows = [pl.ds(i * n, n) for i in range(parts)]
+    into = [pltpu.make_async_copy(a_ref.at[r], buf.at[r], ins.at[i]) for i, r in enumerate(rows)]
+    away = [pltpu.make_async_copy(buf.at[r], b_ref.at[r], outs.at[i]) for i, r in enumerate(rows)]
+    for cpy in into:
+        cpy.start()
+    for i in range(parts):
+        into[i].wait()
+        away[i].start()
+    for cpy in away:
+        cpy.wait()
+
+
+def settle(y, parts=8):
+    hb = pl.BlockSpec(memory_space=pl.ANY)
+    dma = pltpu.SemaphoreType.DMA((parts,))
+    return pl.pallas_call(functools.partial(settle_kernel, parts), in_specs=[hb], out_specs=hb, out_shape=jax.ShapeDtypeStruct(y.shape, y.dtype),
+                          scratch_shapes=[pltpu.VMEM(y.shape, y.dtype), dma, dma], name='settle')(y)
 
 
 D = 128
@@ -223,16 +254,18 @@
     meta_ref[...] = jnp.transpose(meta)
 
 
-def front_kernel(cp, ne, x_ref, idx_ref, gate_ref, wq_ref, wk_ref, wv_ref, wo_ref, h_ref, all_ref, slot_ref, meta_ref,
-                 cnt, xs, wqb, wkvb, q_ref, kv_ref, wof, ocat, st,
+def front_kernel(cp, ne, x_ref, idx_ref, gate_ref, wq_ref, wk_ref, wv_ref, wo_ref, h_ref, worst_ref, slot_ref, meta_ref,
+                 cnt, all_ref, xv, xs, wqb, wkvb, q_ref, kv_ref, wof, ocat, st,
                  cs, cr, as_, ar_, fs, fr, bs, br, ks, kr, ws, xs_, xr_, ys_, yr_, ds_, dr_, os_, or_, ls_, hs_):
     t, hd = x_ref.shape
     c = lax.axis_index('cp')
     loads = [pltpu.make_async_copy(wk_ref, wkvb.at[:, :D], ws.at[0]), pltpu.make_async_copy(wv_ref, wkvb.at[:, D:], ws.at[1]),
              pltpu.make_async_copy(wq_ref, wqb, ws.at[2])]
-    for ld in loads:
+    hail(range(1, ne))
+    loads.append(pltpu.make_async_copy(x_ref, xv, ws.at[3]))
+    for ld in reversed(loads):
         ld.start()
-    greet(range(1, ne))
+    pl.semaphore_wait(pltpu.get_barrier_semaphore(), ne - 1)
 
     step = t // PIECES
     rows = lambda p: pl.ds(pl.multiple_of(p * step, 16), step)
@@ -285,7 +318,7 @@
         across(p).start()
     for ld in loads:
         ld.wait()
-    project(x_ref[...], 0, 0, t, 0)
+    project(xv[...], 0, 0, t, 0)
     beside.wait_recv()
     project(xs[0], 1, 0, t, 1)
 
@@ -304,6 +337,9 @@
     lax.fori_loop(0, PIECES, land, 0)
     mine.start()
     whole.start()
+    for cc in counts:
+        cc.wait_recv()
+    worst_ref[0, 0] = jnp.max(all_ref[...])
     for i in range(2):
         pair(i, 0, t).wait_recv()
     for i in range(2, 2 + 2 * PIECES):
@@ -416,7 +452,7 @@
 
     def last(n, _):
         s = held(n) + jnp.dot(ocat[:, 3 * w:], wof[3 * w:, tile(n)], preferred_element_type=jnp.float32)
-        xs[0, :, tile(n)] = (x_ref[:, tile(n)].astype(jnp.float32) + s).astype(jnp.bfloat16)
+        xs[0, :, tile(n)] = (xv[:, tile(n)].astype(jnp.float32) + s).astype(jnp.bfloat16)
 
         @pl.when(n > 0)
         def _():
@@ -424,8 +460,6 @@
         return 0
     lax.fori_loop(0, hd // NT, last, 0)
     out(hd // NT - 1).start()
-    for cc in counts:
-        cc.wait_recv()
     for p in range(PIECES):
         across(p).wait_send()
     for i in range(2):
@@ -449,11 +483,11 @@
     nd = 2 * CHUNKS + 1
     return pl.pallas_call(
         functools.partial(front_kernel, cp, ne),
-        in_specs=[vm, vm, vm, hb, hb, hb, hb], out_specs=[hb, vm, vm, vm],
-        out_shape=[jax.ShapeDtypeStruct((t, hd), bf), jax.ShapeDtypeStruct((ne, 8, 128), jnp.int32), jax.ShapeDtypeStruct((ne, t), jnp.int32), jax.ShapeDtypeStruct((t, 128), jnp.float32)],
-        scratch_shapes=[pltpu.VMEM((8, 128), jnp.int32), pltpu.VMEM((3, t, hd), bf), pltpu.VMEM(wq.shape, bf), pltpu.VMEM((hd, 2 * D), bf),
+        in_specs=[hb, vm, vm, hb, hb, hb, hb], out_specs=[hb, pl.BlockSpec(memory_space=pltpu.SMEM), vm, vm],
+        out_shape=[jax.ShapeDtypeStruct((t, hd), bf), jax.ShapeDtypeStruct((1, 1), jnp.int32), jax.ShapeDtypeStruct((ne, t), jnp.int32), jax.ShapeDtypeStruct((t, 128), jnp.float32)],
+        scratch_shapes=[pltpu.VMEM((8, 128), jnp.int32), pltpu.VMEM((ne, 8, 128), jnp.int32), pltpu.VMEM((t, hd), bf), pltpu.VMEM((3, t, hd), bf), pltpu.VMEM(wq.shape, bf), pltpu.VMEM((hd, 2 * D), bf),
                         pltpu.VMEM((tp * t, w), bf), pltpu.VMEM((ne * t, 2 * D), bf), pltpu.VMEM((tp * w, hd), bf), pltpu.VMEM((t, tp * w), bf), pltpu.VMEM((hd // 128, t, 128), jnp.float32),
-                        dma(ne), dma(ne), dma(PIECES), dma(PIECES), dma(PIECES), dma(PIECES), dma(1), dma(1), dma(nk), dma(nk), dma(3),
+                        dma(ne), dma(ne), dma(PIECES), dma(PIECES), dma(PIECES), dma(PIECES), dma(1), dma(1), dma(nk), dma(nk), dma(4),
                         dma(CHUNKS), dma(CHUNKS), dma(CHUNKS), dma(CHUNKS), dma(nd), dma(nd), dma(4), dma(4), dma(1), dma(1)],
         compiler_params=pltpu.CompilerParams(collective_id=cid, has_side_effects=True, vmem_limit_bytes=67043328),
         name='front')(x, idx.T, gates.T, wq, wk, wv, wo)
@@ -493,8 +527,7 @@
 
     def local(x, idx, gates, wq, wk, wv, wo, w1g, w1u, w2):
         t, hd = x.shape
-        h, counts, slot, meta = front(x, idx, gates, wq, wk, wv, wo, cp, ne, 1)
-        worst = jnp.max(counts)
+        h, worst, slot, meta = front(x, idx, gates, wq, wk, wv, wo, cp, ne, 1)
 
         def tight(h):
             return moe_fast(h, slot, meta, w1g[0], w1u[0], w2[0], t // 4, 3)
@@ -502,6 +535,6 @@
         def roomy(h):
             return moe_any(h, slot, idx, gates, w1g[0], w1u[0], w2[0])
 
-        return lax.cond(worst <= t // 4, tight, roomy, h)
+        return settle(lax.cond(worst[0, 0] <= t // 4, tight, roomy, h))
 
     return jax.shard_map(local, mesh=mesh, in_specs=(rows_spec, rows_spec, rows_spec, P(None, 'tp'), P(None, 'tp'), P(None, 'tp'), P('tp', None), exp_spec, exp_spec, exp_spec), out_specs=rows_spec, check_vma=False)

time: 571 us -> 567 us (level)
    pallas_call x1 -> x2, Pallas kernels: 171 us -> 173 us  [the longest x1 170 us: front(): pl.pallas_call(functools.partial(front_kernel, cp, ne), in_specs=[hb, vm,...]
where the time goes in v6:
time: 567 us; the launch traced here: 562 us
  Pallas kernels  173 us (31%)
  matrix products  133 us (23%)
  blocking collectives  128 us (23%)
  waiting for transfers between devices  122 us (22%)
    pallas_call x1, Pallas kernels, front(): pl.pallas_call(functools.partial(front_kernel, cp, ne), in_specs=[hb, vm,...  170 us
    all_to_all x1, blocking collectives, moe_any(): lax.all_to_all(send.reshape(ne, cap, hd), ('cp', 'tp'), 0, 0, tiled=True)  128 us
    all_to_all x1, waiting for transfers between devices, moe_any(): lax.all_to_all(z.reshape(ne, cap, hd), ('cp', 'tp'), 0, 0, tiled=True)  122 us
    dot_general x1, matrix products, expert_ffn(): uu = jnp.dot(rows, wu, preferred_element_type=jnp.float32)  39.4 us
    dot_general x1, matrix products, expert_ffn(): gg = jnp.dot(rows, wg, preferred_element_type=jnp.float32)  33.1 us
    dot_general x1, matrix products, expert_ffn(): jnp.dot(act, wd, preferred_element_type=jnp.float32).astype(jnp.bfloat16)  32.4 us
    dot_general x2, matrix products, moe_any(): jnp.dot(sel, back, preferred_element_type=jnp.float32)  17.8 us
  transfers between devices with their start and end apart: 1, of which 1 were waited for; matrix products, arithmetic and copies ran while one was open for 0% of the time, Pallas kernels for 0%

profile of v6, /device:TPU:0, one launch (start us, length us, event | category | flops | bytes accessed | tf_op | source)
XLA Modules:
  0.0 562.4 jit_solution(5696891571965932458)
XLA Ops:
  0.0 170.1 %front.1 = (bf16[384,3584]{1,0:T(8,128)(2,1)}, s32[1,1]{1,0:T(1,128)}, s32[8,384]{1,0:T(8,128)}, f32[384,128]{1,0:T(8,128)}) custom-call(bf16[384,3584]{1,0:T(8,128)(2,1)} %x_ref.1, s32[2,384]{1,0:T(2,128)} %bitcast.43, f32[2,384]{1,0:T(2,128)} %bitcast.44, bf16[3584,896]{1,0:T(8,128)(2,1)} %wq_ref.1, bf16[3584,128]{1,0:T(8,128)(2,1)} %wk_ref.1, ...), custom_call_target="tpu_custom_call" | custom-call | tf_op jit(solution)/shard_map/front/pallas_call | solution.py:484
  170.8 388.7 %conditional.1 = (bf16[384,3584]{1,0:T(8,128)(2,1)}) conditional(s32[]{:T(128)} %bitcast.13, (bf16[384,3584]{1,0:T(8,128)(2,1)}, f32[384,2]{0,1:T(2,128)}, s32[384,2]{0,1:T(2,128)}, s32[8,384]{1,0:T(8,128)}, bf16[1,3584,2560]{2,1,0:T(8,128)(2,1)}, /*index=5*/bf16[1,3584,2560]{2,1,0:T(8,128)(2,1)}, bf16[1,2560,3584]{2,1,0:T(8,128)(2,1)}) %tuple.11, ...), branch_computations={%region_0.3_spmd, %region_3.4_spmd} | conditional | flops 97285398528 | bytes 365052416 | solution.py:538
  170.8 0.1 eq.16
  170.9 1.1 bitcast_compare_fusion
  172.0 0.0 slice-start
  172.0 0.0 slice-start.1
  172.0 0.0 slice-start.2
  172.0 10.4 %convolution_convert_fusion = bf16[1536,3584]{1,0:T(8,128)(2,1)} fusion(pred[1536,384]{1,0:T(32,128)(4,1)S(1)} %bitcast_compare_fusion, bf16[384,3584]{1,0:T(8,128)(2,1)} %get-tuple-element.34), kind=kOutput, calls=%fused_computation.8 | convolution fusion | flops 4233363456 | bytes 14352384 | tf_op jit(solution)/shard_map/cond/branch_0_fun/dot_general | solution.py:508
  182.4 0.0 slice-start.3
  182.4 0.0 slice-start.4
  182.4 127.7 %all_to_all.8 = bf16[8,192,3584]{2,1,0:T(8,128)(2,1)} all-to-all(bf16[8,192,3584]{2,1,0:T(8,128)(2,1)} %bitcast.42), channel_id=1, replica_groups=mesh['dp'=1,'cp'=2,'tp'=4] {'cp','tp'}, dimensions={0} | all-to-all | bytes 22020096 | tf_op jit(solution)/shard_map/cond/branch_0_fun/all_to_all | solution.py:509
  310.1 0.0 slice-done
  310.1 0.0 slice-done.1
  310.2 0.0 slice-done.2
  310.2 0.0 slice-done.3
  310.2 0.0 slice-done.4
  310.2 0.0 slice-start.5
  310.2 0.0 slice-start.6
  310.2 0.0 slice-start.7
  310.2 33.1 %fusion.4 = f32[1536,2560]{1,0:T(8,128)} fusion(bf16[1536,3584]{1,0:T(8,128)(2,1)} %bitcast.40, bf16[1,3584,2560]{2,1,0:T(8,128)(2,1)S(1)} %bitcast.33), kind=kOutput, calls=%fused_computation.4 | convolution fusion | flops 28185722880 | bytes 45088768 | tf_op jit(solution)/shard_map/cond/branch_0_fun/dot_general | solution.py:497
  343.3 0.0 slice-start.8
  343.3 0.0 slice-start.9
  343.3 39.4 %multiply_convert_fusion = bf16[1536,2560]{1,0:T(8,128)(2,1)} fusion(f32[1536,2560]{1,0:T(8,128)} %fusion.4, bf16[1536,3584]{1,0:T(8,128)(2,1)} %bitcast.41, bf16[1,3584,2560]{2,1,0:T(8,128)(2,1)} %get-tuple-element.39), kind=kOutput, calls=%fused_computation.6 | convolution fusion | flops 28209315840 | bytes 52953088 | tf_op jit(solution)/shard_map/cond/branch_0_fun/dot_general | solution.py:498
  382.7 0.0 slice-done.5
  382.7 0.0 slice-done.6
  382.7 0.0 slice-done.7
  382.7 0.0 slice-done.8
  382.7 0.0 slice-done.9
  382.8 32.4 %fusion.6 = bf16[1536,3584]{1,0:T(8,128)(2,1)} fusion(bf16[1536,2560]{1,0:T(8,128)(2,1)} %multiply_convert_fusion, bf16[1,2560,3584]{2,1,0:T(8,128)(2,1)S(1)} %bitcast.37), kind=kOutput, calls=%fused_computation.7 | convolution fusion | flops 28191227904 | bytes 37224448 | tf_op jit(solution)/shard_map/cond/branch_0_fun/dot_general | solution.py:500
  415.1 0.0 copy-start.2
  415.1 0.0 copy-start.3
  415.1 0.0 copy-start.1
  415.1 4.3 all-to-all-start.1
  419.4 0.0 copy-done.2
  419.4 0.0 copy-done.3
  419.5 0.0 copy-done.1
  419.5 0.1 select_reduce_fusion.1
  419.6 121.9 %all-to-all-done.1 = bf16[8,192,3584]{2,1,0:T(8,128)(2,1)} async-done(((bf16[8,192,3584]{2,1,0:T(8,128)(2,1)}), bf16[8,192,3584]{2,1,0:T(8,128)(2,1)}, u32[]{:S(2)}, u32[]{:S(2)}) %all-to-all-start.1) | async-done | bytes 11010080 | tf_op jit(solution)/shard_map/cond/branch_0_fun/all_to_all | solution.py:511
  541.5 0.0 copy-start
  541.5 7.5 %convolution_multiply_fusion = f32[384,3584]{1,0:T(8,128)S(1)} fusion(bf16[1536,3584]{1,0:T(8,128)(2,1)} %bitcast.7, f32[384]{0:T(512)S(1)} %get-tuple-element.60, s32[384]{0:T(512)S(1)} %get-tuple-element.56), kind=kOutput, calls=%fused_computation.9 | convolution fusion | flops 4229824512 | bytes 16518144 | tf_op jit(solution)/shard_map/cond/branch_0_fun/dot_general | solution.py:517
  549.0 0.0 copy-done
  549.1 10.3 %fusion.13 = bf16[384,3584]{1,0:T(8,128)(2,1)} fusion(f32[384,3584]{1,0:T(8,128)S(1)} %convolution_multiply_fusion, bf16[1536,3584]{1,0:T(8,128)(2,1)} %bitcast.7, bf16[384,3584]{1,0:T(8,128)(2,1)S(1)} %copy-done, f32[384]{0:T(512)S(1)} %get-tuple-element.59, s32[384]{0:T(512)S(1)} %get-tuple-element.55), kind=kOutput, calls=%fused_computation.13 | convolution fusion | flops 4235329536 | bytes 22023168 | tf_op jit(solution)/shard_map/cond/branch_0_fun/dot_general | solution.py:517
  559.5 2.6 settle.1
  (6 shorter events, 0.1 us)
Async XLA Ops:
  172.0 138.2 %slice-start = ((s8[18350080]{0:T(1024)(128)(4,1)}), s8[4194304]{0:T(1024)(128)(4,1)S(1)}, s32[]{:S(2)}) async-start(s8[18350080]{0:T(1024)(128)(4,1)} %bitcast.32), calls=%async_computation.2 | async-start | bytes 8388608 | tf_op jit(solution)/shard_map/cond
  172.0 138.2 %slice-start.1 = ((s8[18350080]{0:T(1024)(128)(4,1)}), s8[4194304]{0:T(1024)(128)(4,1)S(1)}, s32[]{:S(2)}) async-start(s8[18350080]{0:T(1024)(128)(4,1)} %bitcast.32), calls=%async_computation.3 | async-start | bytes 8388608 | tf_op jit(solution)/shard_map/cond
  172.0 138.2 %slice-start.2 = ((s8[18350080]{0:T(1024)(128)(4,1)}), s8[4194304]{0:T(1024)(128)(4,1)S(1)}, s32[]{:S(2)}) async-start(s8[18350080]{0:T(1024)(128)(4,1)} %bitcast.32), calls=%async_computation.4 | async-start | bytes 8388608 | tf_op jit(solution)/shard_map/cond
  182.4 127.7 %slice-start.3 = ((s8[18350080]{0:T(1024)(128)(4,1)}), s8[4194304]{0:T(1024)(128)(4,1)S(1)}, s32[]{:S(2)}) async-start(s8[18350080]{0:T(1024)(128)(4,1)} %bitcast.32), calls=%async_computation.5 | async-start | bytes 8388608 | tf_op jit(solution)/shard_map/cond
  182.4 127.7 %slice-start.4 = ((s8[18350080]{0:T(1024)(128)(4,1)}), s8[1572864]{0:T(1024)(128)(4,1)S(1)}, s32[]{:S(2)}) async-start(s8[18350080]{0:T(1024)(128)(4,1)} %bitcast.32), calls=%async_computation.6 | async-start | bytes 3145728 | tf_op jit(solution)/shard_map/cond
  310.2 72.5 %slice-start.5 = ((s8[18350080]{0:T(1024)(128)(4,1)}), s8[4194304]{0:T(1024)(128)(4,1)S(1)}, s32[]{:S(2)}) async-start(s8[18350080]{0:T(1024)(128)(4,1)} %bitcast.36), calls=%async_computation.7 | async-start | bytes 8388608 | tf_op jit(solution)/shard_map/cond
  310.2 72.5 %slice-start.6 = ((s8[18350080]{0:T(1024)(128)(4,1)}), s8[4194304]{0:T(1024)(128)(4,1)S(1)}, s32[]{:S(2)}) async-start(s8[18350080]{0:T(1024)(128)(4,1)} %bitcast.36), calls=%async_computation.8 | async-start | bytes 8388608 | tf_op jit(solution)/shard_map/cond
  310.2 72.5 %slice-start.7 = ((s8[18350080]{0:T(1024)(128)(4,1)}), s8[1572864]{0:T(1024)(128)(4,1)S(1)}, s32[]{:S(2)}) async-start(s8[18350080]{0:T(1024)(128)(4,1)} %bitcast.36), calls=%async_computation.9 | async-start | bytes 3145728 | tf_op jit(solution)/shard_map/cond
  343.3 39.4 %slice-start.8 = ((s8[18350080]{0:T(1024)(128)(4,1)}), s8[4194304]{0:T(1024)(128)(4,1)S(1)}, s32[]{:S(2)}) async-start(s8[18350080]{0:T(1024)(128)(4,1)} %bitcast.36), calls=%async_computation.10 | async-start | bytes 8388608 | tf_op jit(solution)/shard_map/cond
  343.3 39.5 %slice-start.9 = ((s8[18350080]{0:T(1024)(128)(4,1)}), s8[4194304]{0:T(1024)(128)(4,1)S(1)}, s32[]{:S(2)}) async-start(s8[18350080]{0:T(1024)(128)(4,1)} %bitcast.36), calls=%async_computation.11 | async-start | bytes 8388608 | tf_op jit(solution)/shard_map/cond
  415.1 4.3 copy-start.2
  415.1 4.3 copy-start.3
  415.1 4.4 copy-start.1
  415.1 126.4 %all-to-all-start.1 = ((bf16[8,192,3584]{2,1,0:T(8,128)(2,1)}), bf16[8,192,3584]{2,1,0:T(8,128)(2,1)}, u32[]{:S(2)}, u32[]{:S(2)}) async-start(bf16[8,192,3584]{2,1,0:T(8,128)(2,1)} %bitcast.39), calls=%async_computation.1 | async-start | bytes 22020096 | tf_op jit(solution)/shard_map/cond/branch_0_fun/all_to_all | solution.py:511
  541.5 7.5 %copy-start = (bf16[384,3584]{1,0:T(8,128)(2,1)S(1)}, bf16[384,3584]{1,0:T(8,128)(2,1)}, u32[]{:S(2)}) copy-start(bf16[384,3584]{1,0:T(8,128)(2,1)} %get-tuple-element.34) | copy-start | bytes 8257540 | tf_op jit(solution)/shard_map/cond
